TPU v7x, 32 devices: a whole 2x2x4 slice. The times are simulated.
32 devices in a mesh: seq: 16 (over z, y, core), grp: 2 (over x).
Axes of the slice: x: 2, y: 2, z: 4, core: 2. Of those that a mesh axis runs over, the one named last changes fastest.
Arguments:
- queries: bfloat16 [4096, 3584], P(('grp', 'seq')), parts along dimension 0, may hold values from -5 to 5
- keys: bfloat16 [4096, 512], P(('grp', 'seq')), parts along dimension 0, may hold values from -5 to 5
- values: bfloat16 [4096, 512], P(('grp', 'seq')), parts along dimension 0, may hold values from -6 to 6
- doc_lengths: int32 [16], P('grp'), parts along dimension 0, may hold values from 1 to 1280, 2048 in all
Outputs:
- attended: bfloat16 [4096, 3584], P(('grp', 'seq')), parts along dimension 0
There are 2 independent parts, one for each index of `grp`. A program takes and returns all parts, laid end to end along the dimension named above; each array names one. Nothing has to cross between parts.
Inputs may be any that keep to these rules, and one draw needn't show every extreme that they name: `doc_lengths`: the 8 documents lie one after another and their lengths sum to 2048; the longest has exactly 1280 tokens.
All inputs are finite; a program needn't handle non-finite values.
Results may differ from a plain program's by a relative error of at most 0.0085.
Values may be sent and summed in bfloat16 or wider, within the bound.
No kernel may reach another device: no remote copies, remote signals or barrier semaphores. Data moves between devices by JAX's collectives and lax.ppermute only.
A program may use at most 192 MiB of HBM per device.

v0:
```python
import jax
import jax.numpy as jnp
from jax import lax
from jax.sharding import PartitionSpec as P

HEADS = 28
KV_HEADS = 4
HEAD_DIM = 128


rope_base = 1000000.0
negative = -1e30


def doc_place(position, doc_lengths):
    doc_ends = jnp.cumsum(doc_lengths)
    beyond = position[:, None] >= doc_ends[None, :]
    doc_index = jnp.sum(beyond.astype(jnp.int32), axis=1)
    doc_start = jnp.sum(jnp.where(beyond, doc_lengths[None, :], 0), axis=1)
    return (doc_index, doc_start)


def rotate(values_in, within_doc, head_count):
    row_count = values_in.shape[0]
    half_dim = HEAD_DIM // 2
    inverse_freq = jnp.power(
        jnp.float32(rope_base), -2.0 * jnp.arange(half_dim, dtype=jnp.float32) / HEAD_DIM
    )
    angles = within_doc.astype(jnp.float32)[:, None] * inverse_freq[None, :]
    cosine = jnp.cos(angles)[:, None, :]
    sines = jnp.sin(angles)[:, None, :]
    fields = values_in.astype(jnp.float32).reshape(row_count, head_count, HEAD_DIM)
    lower_half = fields[..., :half_dim]
    upper_half = fields[..., half_dim:]
    rotated = jnp.concatenate(
        [lower_half * cosine - upper_half * sines, upper_half * cosine + lower_half * sines],
        axis=-1,
    )
    return rotated.reshape(row_count, head_count * HEAD_DIM).astype(jnp.bfloat16)


def per_device(queries, keys, values, doc_lengths):
    row_count = queries.shape[0]
    dev_index = lax.axis_index("seq")
    group_size = HEADS // KV_HEADS
    score_scale = HEAD_DIM ** (-0.5)
    local_rows = jnp.arange(row_count, dtype=jnp.int32)
    own_pos = dev_index * row_count + local_rows
    own_start = doc_place(own_pos, doc_lengths)[1]
    within_doc = own_pos - own_start
    q_rot = rotate(queries, within_doc, HEADS)
    k_rot = rotate(keys, within_doc, KV_HEADS)
    query_doc = doc_place(own_pos, doc_lengths)[0]
    q_heads = q_rot.reshape(row_count, KV_HEADS, group_size, HEAD_DIM)
    k_piece = lax.all_gather(k_rot, "seq", axis=0, tiled=True)
    v_piece = lax.all_gather(values, "seq", axis=0, tiled=True)
    length = k_piece.shape[0]
    key_pos = jnp.arange(length, dtype=jnp.int32)
    key_doc = doc_place(key_pos, doc_lengths)[0]
    allowed = (key_doc[None, :] == query_doc[:, None]) & (key_pos[None, :] <= own_pos[:, None])
    allowed_wide = allowed[:, None, None, :]
    running_max = jnp.full((row_count, KV_HEADS, group_size), negative, jnp.float32)
    k_heads = k_piece.reshape(length, KV_HEADS, HEAD_DIM)
    v_heads = v_piece.reshape(length, KV_HEADS, HEAD_DIM)
    scores = (
        jnp.einsum("qkgd,skd->qkgs", q_heads, k_heads, preferred_element_type=jnp.float32)
        * score_scale
    )
    scores = jnp.where(allowed_wide, scores, negative)
    new_max = jnp.maximum(running_max, jnp.max(scores, axis=-1))
    weight = jnp.where(allowed_wide, jnp.exp(scores - new_max[..., None]), 0.0)
    weight_sum = jnp.sum(weight, axis=-1)
    weighted = jnp.einsum(
        "qkgs,skd->qkgd", weight.astype(jnp.bfloat16), v_heads, preferred_element_type=jnp.float32
    )
    running_max, weight_sum, weighted = (new_max, weight_sum, weighted)
    attended = (
        (weighted / weight_sum[..., None]).reshape(row_count, HEADS * HEAD_DIM).astype(jnp.bfloat16)
    )
    return attended


def solution(mesh):
    return jax.shard_map(
        per_device,
        mesh=mesh,
        in_specs=(
            P(("grp", "seq"), None),
            P(("grp", "seq"), None),
            P(("grp", "seq"), None),
            P("grp"),
        ),
        out_specs=P(("grp", "seq"), None),
        check_vma=False,
    )
```

profile of v0, /device:TPU:0, one launch (start us, length us, event | category | flops | bytes accessed | tf_op | source)
XLA Modules:
  0.0 121.0 jit_solution(10799247144488770682)
XLA Ops:
  6.5 0.0 all-gather.3.cloned.1.call-start
  6.6 0.8 reduce-window.8
  7.4 0.7 fusion.10
  8.2 1.0 copy.31
  9.2 0.2 multiply_cosine_fusion
  9.4 0.7 pad_maximum_fusion.1
  10.1 0.0 all-gather.3.cloned.1.call-update
  10.1 0.0 all-gather.5.cloned.1.call-start
  10.1 0.7 all-gather.5.cloned.1.call-update
  10.9 0.1 convert_reduce_fusion
  10.9 1.6 %copy.20 = bf16[128,3584]{0,1:T(8,128)(2,1)S(1)} copy(bf16[128,3584]{1,0:T(8,128)(2,1)} %param.4) | data formatting | bytes 1835008 | tf_op args[0]
  12.5 0.2 convert.18
  12.7 0.3 fusion.9
  13.1 0.3 subtract_convert_fusion
  13.3 0.1 pad_maximum_fusion
  13.4 40.6 %all-gather.3.cloned.1.call-done = bf16[2048,512]{0,1:T(8,128)(2,1)} async-done(((bf16[128,512]{0,1:T(8,128)(2,1)}), bf16[2048,512]{0,1:T(8,128)(2,1)}) %all-gather.3.cloned.1.call-update) | async-done | bytes 2097168 | tf_op jit(solution)/shard_map/all_gather | solution.py:55
  54.0 13.3 %fusion = (f32[128,4,7]{0,2,1:T(8,128)S(1)}, f32[4,2048,128,7]{2,1,3,0:T(8,128)}) fusion(pred[128,2048]{0,1:T(8,128)(4,1)S(1)} %fusion.9, bf16[2048,4,128,1]{0,2,3,1:T(8,128)(2,1)} %bitcast.42, bf16[128,4,7,128]{0,3,2,1:T(8,128)(2,1)S(1)} %bitcast.40), kind=kOutput, calls=%fused_computation.2 | convolution fusion | flops 1901064704 | bytes 32651264 | tf_op jit(solution)/shard_map/qkgd,skd->qkgs/dot_general | solution.py:66
  67.4 13.2 %fusion.1 = f32[128,4,7]{0,2,1:T(8,128)S(1)} fusion(f32[4,2048,128,7]{2,1,3,0:T(8,128)} %get-tuple-element.14, f32[128,4,7]{0,2,1:T(8,128)S(1)} %broadcast_maximum_fusion, pred[128,2048]{0,1:T(8,128)(4,1)S(1)} %fusion.9), kind=kLoop, calls=%fused_computation.3 | loop fusion | flops 36696576 | bytes 29650944 | tf_op jit(solution)/shard_map/reduce_sum | solution.py:72
  80.6 16.2 %all-gather.5.cloned.1.call-done = bf16[2048,512]{1,0:T(8,128)(2,1)} async-done(((bf16[128,512]{1,0:T(8,128)(2,1)}), bf16[2048,512]{1,0:T(8,128)(2,1)}) %all-gather.5.cloned.1.call-update) | async-done | bytes 2097168 | tf_op jit(solution)/shard_map/all_gather | solution.py:56
  96.8 2.9 %copy.23 = bf16[2048,512]{0,1:T(8,128)(2,1)S(1)} copy(bf16[2048,512]{1,0:T(8,128)(2,1)} %all-gather.5.cloned.1.call-done) | data formatting | bytes 4194304 | tf_op jit(solution)/shard_map/all_gather | solution.py:56
  99.7 13.2 %fusion.6 = bf16[128,4,7,128]{0,3,2,1:T(8,128)(2,1)S(1)} fusion(bf16[2048,4,128,1]{0,2,3,1:T(8,128)(2,1)S(1)} %bitcast.41, f32[4,2048,128,7]{2,1,3,0:T(8,128)} %get-tuple-element.14, f32[128,4,7]{0,2,1:T(8,128)S(1)} %broadcast_maximum_fusion, pred[128,2048]{0,1:T(8,128)(4,1)S(1)} %fusion.9, f32[128,4,7]{0,2,1:T(8,128)S(1)} %fusion.1), kind=kOutput, calls=%fused_computation.8 | convolution fusion | flops 1916665856 | bytes 32665600 | tf_op jit(solution)/shard_map/qkgs,skd->qkgd/dot_general | solution.py:73
  112.9 1.3 %copy.25 = bf16[128,3584]{1,0:T(8,128)(2,1)} copy(bf16[128,3584]{0,1:T(8,128)(2,1)S(1)} %bitcast.44) | data formatting | bytes 1835008 | tf_op jit(solution)/shard_map/convert_element_type | solution.py:78
  (5 shorter events, 0.1 us)
Async XLA Ops:
  6.5 47.5 %all-gather.3.cloned.1.call-start = ((), (), s32[]{:S(2)}) async-start(), calls=%async_computation | async-start | bytes 2228224 | tf_op jit(solution)/shard_map/all_gather | solution.py:55
  10.1 86.7 %all-gather.5.cloned.1.call-start = ((), (), s32[]{:S(2)}) async-start(), calls=%async_computation.1 | async-start | bytes 2228224 | tf_op jit(solution)/shard_map/all_gather | solution.py:56
Sparse Core Ops, SparseCore 0:
  10.2 43.7 all-gather.2
  56.2 40.5 all-gather.4
where the time goes:
time: 121 us
  waiting for transfers between devices  57.5 us (48%)
  matrix products  26.5 us (22%)
  other arithmetic  16.7 us (14%)
  between operations  13.5 us (11%)
  local copies, waits for them, and re-layouts  6.76 us (6%)
    all_gather x1, waiting for transfers between devices, per_device(): k_piece = lax.all_gather(k_rot, 'seq', axis=0, tiled=True)  40.6 us
    all_gather x1, waiting for transfers between devices, per_device(): v_piece = lax.all_gather(values, 'seq', axis=0, tiled=True)  16.2 us
    dot_general x1, matrix products, per_device(): jnp.einsum('qkgd,skd->qkgs', q_heads, k_heads, preferred_element_type=jnp...  13.3 us
    reduce_sum x1, other arithmetic, per_device(): weight_sum = jnp.sum(weight, axis=-1)  13.2 us
    dot_general x1, matrix products, per_device(): jnp.einsum('qkgs,skd->qkgd', weight.astype(jnp.bfloat16), v_heads, prefer...  13.2 us
    all_gather x1, local copies, waits for them, and re-layouts, per_device(): v_piece = lax.all_gather(values, 'seq', axis=0, tiled=True)  2.93 us
  transfers between devices with their start and end apart: 2, of which 2 were waited for; matrix products, arithmetic and copies ran while one was open for 24% of the time, Pallas kernels for 0%

commit v1 on v0

v1 whole, which is shorter than its diff:
```python
import functools

import jax
import jax.numpy as jnp
import numpy as np
from jax import lax
from jax.experimental import pallas as pl
from jax.experimental.pallas import tpu as pltpu
from jax.sharding import PartitionSpec as P

HEADS = 28
KV_HEADS = 4
HEAD_DIM = 128
GROUP = HEADS // KV_HEADS
ROPE_BASE = 1000000.0
NEGATIVE = -1e30
SCORE_SCALE = HEAD_DIM ** (-0.5) * 1.4426950408889634
NOWHERE = 1 << 28
VMEM_LIMIT = 24 * 1024 * 1024


def cycles(wanted, count):
    pairs = dict(wanted)
    starts = [s for s in pairs if s not in set(pairs.values())]
    for start in starts:
        at = start
        while at in pairs:
            at = pairs[at]
        pairs[at] = start
    for i in range(count):
        pairs.setdefault(i, i)
    assert sorted(pairs.values()) == list(range(count))
    return sorted(pairs.items())


class Piece:
    def __init__(self, data, source):
        self.data, self.source = data, source

    def move(self, pairs):
        source = list(self.source)
        for s, t in pairs:
            source[t] = self.source[s]
        return Piece(lax.ppermute(self.data, "seq", pairs), source)


def rotated(x, cosine, sine):
    return x * cosine + pltpu.roll(x, HEAD_DIM // 2, 1) * sine


def prepare_kernel(k_ref, v_ref, cos_ref, sin_ref, kv_ref):
    width = KV_HEADS * HEAD_DIM
    cosine, sine = cos_ref[...], sin_ref[...]
    for g in range(KV_HEADS):
        cols = slice(g * HEAD_DIM, (g + 1) * HEAD_DIM)
        kv_ref[:, cols] = rotated(k_ref[:, cols].astype(jnp.float32), cosine, sine).astype(jnp.bfloat16)
    kv_ref[:, width:] = v_ref[...]


def prepare(keys, values, cosine, sine):
    rows = keys.shape[0]
    return pl.pallas_call(
        prepare_kernel,
        out_shape=jax.ShapeDtypeStruct((rows, 2 * KV_HEADS * HEAD_DIM), jnp.bfloat16),
        cost_estimate=pl.CostEstimate(flops=10**6, bytes_accessed=6 * 10**5, transcendentals=0),
        compiler_params=pltpu.CompilerParams(vmem_limit_bytes=VMEM_LIMIT),
        name="prepare",
    )(keys, values, cosine, sine)


def attend_kernel(count, first, last, *refs):
    refs = list(refs)
    take = lambda n: [refs.pop(0) for _ in range(n)]
    lengths_ref, bases_ref = take(2)
    if first:
        cos_ref, sin_ref = take(2)
    (q_ref,) = take(1)
    k_refs, v_refs = take(count), take(count)
    if not first:
        max_in, sum_in, acc_in = take(3)
    if last:
        (out_ref,) = take(1)
    else:
        if first:
            (q_out,) = take(1)
        max_out, sum_out, acc_out = take(3)
    (bias_ref,) = take(1)

    me = lax.axis_index("seq")
    rows = k_refs[0].shape[0]

    @pl.when(pl.program_id(0) == 0)
    def _():
        own = me * rows + lax.broadcasted_iota(jnp.int32, (rows, rows), 0)
        start = jnp.zeros((rows, rows), jnp.int32)
        end = 0
        for d in range(lengths_ref.shape[0]):
            end = end + lengths_ref[d]
            start = start + jnp.where(own >= end, lengths_ref[d], 0)
        for b in range(count):
            place = bases_ref[b, me] + lax.broadcasted_iota(jnp.int32, (rows, rows), 1)
            allowed = (place >= start) & (place <= own)
            bias_ref[:, b * rows:(b + 1) * rows] = jnp.where(allowed, 0.0, NEGATIVE)

    if first:
        parts = []
        for h in range(GROUP):
            head = q_ref[:, h * HEAD_DIM:(h + 1) * HEAD_DIM].astype(jnp.float32)
            parts.append((rotated(head, cos_ref[...], sin_ref[...]) * SCORE_SCALE).astype(jnp.bfloat16))
        q = jnp.concatenate(parts, axis=0)
        q_out[0] = q
    else:
        q = q_ref[0]
    k = jnp.concatenate([r[...] for r in k_refs], axis=0)
    v = jnp.concatenate([r[...] for r in v_refs], axis=0)
    scores = lax.dot_general(q, k, (((1,), (1,)), ((), ())), preferred_element_type=jnp.float32)
    scores = scores.reshape(GROUP, rows, count * rows) + bias_ref[...][None]
    scores = scores.reshape(GROUP * rows, count * rows)
    top = jnp.max(scores, axis=1, keepdims=True)
    if not first:
        top = jnp.maximum(max_in[0][:, :1], top)
    weight = jnp.exp2(scores - top)
    part = weight[:, :HEAD_DIM]
    for c in range(HEAD_DIM, count * rows, HEAD_DIM):
        part = part + weight[:, c:c + HEAD_DIM]
    acc = jnp.dot(weight.astype(jnp.bfloat16), v, preferred_element_type=jnp.float32)
    if not first:
        shrink = jnp.exp2(max_in[0] - top)
        acc = acc + acc_in[0] * shrink
        part = part + sum_in[0] * shrink
    if last:
        acc = acc / jnp.sum(part, axis=1, keepdims=True)
        for h in range(GROUP):
            out_ref[:, h * HEAD_DIM:(h + 1) * HEAD_DIM] = acc[h * rows:(h + 1) * rows].astype(jnp.bfloat16)
    else:
        max_out[0] = jnp.broadcast_to(top, acc.shape)
        sum_out[0] = part
        acc_out[0] = acc


def attend(lengths, q, pieces, tables, state=None, turn=None, last=False):
    first = state is None
    count = len(pieces)
    rows = pieces[0].data.shape[0]
    stacked = (KV_HEADS, GROUP * rows, HEAD_DIM)
    smem = pl.BlockSpec(memory_space=pltpu.SMEM)
    whole = pl.BlockSpec((rows, HEAD_DIM), lambda g: (0, 0))
    wide = pl.BlockSpec((rows, GROUP * HEAD_DIM), lambda g: (0, g))
    deep = pl.BlockSpec((1, GROUP * rows, HEAD_DIM), lambda g: (g, 0, 0))
    key_spec = pl.BlockSpec((rows, HEAD_DIM), lambda g: (0, g))
    value_spec = pl.BlockSpec((rows, HEAD_DIM), lambda g: (0, KV_HEADS + g))
    data = [p.data for p in pieces]
    args = [lengths, tables]
    specs = [smem, smem]
    if first:
        args += list(turn)
        specs += [whole] * 2
    args += [q] + data + data
    specs += [wide if first else deep] + [key_spec] * count + [value_spec] * count
    state_shape = [jax.ShapeDtypeStruct(stacked, jnp.float32)] * 3
    aliases = {}
    if not first:
        if not last:
            aliases = {len(args) + n: n for n in range(3)}
        args += list(state)
        specs += [deep] * 3
    if last:
        out_shape = jax.ShapeDtypeStruct((rows, HEADS * HEAD_DIM), jnp.bfloat16)
        out_specs = wide
    elif first:
        out_shape = [jax.ShapeDtypeStruct(stacked, jnp.bfloat16)] + state_shape
        out_specs = [deep] * 4
    else:
        out_shape = state_shape
        out_specs = [deep] * 3
    flops = 4 * rows * HEADS * count * rows * HEAD_DIM
    return pl.pallas_call(
        functools.partial(attend_kernel, count, first, last),
        out_shape=out_shape,
        grid=(KV_HEADS,),
        in_specs=specs,
        out_specs=out_specs,
        scratch_shapes=[pltpu.VMEM((rows, count * rows), jnp.float32)],
        input_output_aliases=aliases,
        cost_estimate=pl.CostEstimate(
            flops=flops, bytes_accessed=10**7, transcendentals=rows * HEADS * count * rows
        ),
        compiler_params=pltpu.CompilerParams(vmem_limit_bytes=VMEM_LIMIT),
        name="attend%d%s" % (count, "f" if first else "l" if last else "m"),
    )(*args)


def per_device(count, queries, keys, values, doc_lengths):
    rows = queries.shape[0]
    tokens = rows * count
    most_doc = tokens * 5 // 8
    reach = -(-(most_doc - 1) // rows)
    chip_reach = -(-(most_doc - 1) // (2 * rows))

    half = HEAD_DIM // 2
    place = lax.axis_index("seq") * rows + jnp.arange(rows, dtype=jnp.int32)
    freq = jnp.power(jnp.float32(ROPE_BASE), -2.0 * jnp.arange(half, dtype=jnp.float32) / HEAD_DIM)
    angle = place.astype(jnp.float32)[:, None] * freq[None, :]
    cosine, sine = jnp.cos(angle), jnp.sin(angle)
    cosine = jnp.concatenate([cosine, cosine], axis=1)
    sine = jnp.concatenate([-sine, sine], axis=1)

    def closed(shift, keep):
        return cycles({i: i + shift for i in range(count) if i + shift < count and keep(i)}, count)

    sibling = [(i, i ^ 1) for i in range(count)]
    across = [(i, i ^ 2) for i in range(count)]
    own = Piece(prepare(keys, values, cosine, sine), list(range(count)))
    stages = [[own.move(sibling)]]
    a, before = own, None
    for s in range(1, chip_reach // 2 + 1):
        b = a.move(across)
        a = a.move(closed(4, lambda i: i >= 4 * (s - 1)))
        stages.append([a, b, a.move(sibling), b.move(sibling)])
        before = b
    if chip_reach % 2:
        near = 4 * (chip_reach // 2)
        c = before.move(closed(4, lambda i: not i & 2 and i >= 4 * (chip_reach // 2 - 1)))
        a = a.move(closed(2, lambda i: i >= near))
        stages.append([a, c, a.move(sibling), c.move(sibling)])
    else:
        b = a.move(across)
        stages.append([b, b.move(sibling)])

    seen = [{i} for i in range(count)]
    tables = []
    for n, pieces in enumerate(stages):
        pieces = ([own] if n == 0 else []) + pieces
        table = np.full((len(pieces), count), NOWHERE, np.int32)
        for b, piece in enumerate(pieces):
            for i in range(count):
                j = piece.source[i]
                if piece is own or (i - reach <= j < i and j not in seen[i]):
                    seen[i].add(j)
                    table[b, i] = j * rows
        stages[n] = pieces
        tables.append(jnp.asarray(table))
    for i in range(count):
        assert seen[i] == set(range(max(0, i - reach), i + 1))

    q, *state = attend(doc_lengths, queries, stages[0], tables[0], turn=(cosine, sine))
    for n in range(1, len(stages) - 1):
        state = attend(doc_lengths, q, stages[n], tables[n], state=state)
    return attend(doc_lengths, q, stages[-1], tables[-1], state=state, last=True)


def solution(mesh):
    return jax.shard_map(
        functools.partial(per_device, mesh.shape["seq"]),
        mesh=mesh,
        in_specs=(
            P(("grp", "seq"), None),
            P(("grp", "seq"), None),
            P(("grp", "seq"), None),
            P("grp"),
        ),
        out_specs=P(("grp", "seq"), None),
        check_vma=False,
    )
```

time: 121 us -> 71.9 us (0.59)
  the two profiles are of different devices: /device:TPU:0 before, /device:TPU:19 now
where the time goes in v1:
time: 71.9 us; the launch traced here: 71.6 us
  Pallas kernels  31.3 us (44%)
  starting transfers between devices  22.3 us (31%)
  waiting for transfers between devices  13 us (18%)
  local copies, waits for them, and re-layouts  4.33 us (6%)
    pallas_call x4, Pallas kernels, attend(): pl.pallas_call(functools.partial(attend_kernel, count, first, last), out_...  31.2 us
    ppermute x13, starting transfers between devices, move(): return Piece(lax.ppermute(self.data, 'seq', pairs), source)  22.3 us
    ppermute x13, waiting for transfers between devices, move(): return Piece(lax.ppermute(self.data, 'seq', pairs), source)  13 us
    unnamed x16, local copies, waits for them, and re-layouts  4.33 us
  transfers between devices with their start and end apart: 13, of which 3 were waited for; matrix products, arithmetic and copies ran while one was open for 0% of the time, Pallas kernels for 30%

profile of v1, /device:TPU:19, one launch (start us, length us, event | category | flops | bytes accessed | tf_op | source)
XLA Modules:
  0.0 71.6 jit_solution(16223492848161480788)
XLA Ops:
  0.0 0.3 fusion
  0.3 0.1 pad_maximum_fusion
  0.5 0.0 copy-start.1
  0.5 0.9 %copy-done.1 = bf16[128,512]{1,0:T(8,128)(2,1)S(1)} copy-done((bf16[128,512]{1,0:T(8,128)(2,1)S(1)}, bf16[128,512]{1,0:T(8,128)(2,1)}, u32[]{:S(2)}) %copy-start.1) | copy-done | bytes 131096
  1.4 0.9 %copy-done.2 = bf16[128,512]{1,0:T(8,128)(2,1)S(1)} copy-done((bf16[128,512]{1,0:T(8,128)(2,1)S(1)}, bf16[128,512]{1,0:T(8,128)(2,1)}, u32[]{:S(2)}) %copy-start.2) | copy-done | bytes 131096
  2.3 0.1 prepare.1.refs_5_.refs_7_
  2.4 1.3 %collective-permute-start.1 = (bf16[128,1024]{1,0:T(8,128)(2,1)S(1)}, bf16[128,1024]{1,0:T(8,128)(2,1)S(1)}, u32[]{:S(2)}, u32[]{:S(2)}) collective-permute-start(bf16[128,1024]{1,0:T(8,128)(2,1)S(1)} %prepare.1.refs_5_.refs_7_), channel_id=1, source_target_pairs={{0,8},{2,10},{4,12},{6,14},{8,16},{10,18},{12,20},{14,22},{16,24},... | collective-permute-start | bytes 786440 | tf_op jit(solution)/shard_map/ppermute | solution.py:44
  3.7 5.9 %collective-permute-done.1.refs_3_.refs_7_ = bf16[128,1024]{1,0:T(8,128)(2,1)S(1)} collective-permute-done((bf16[128,1024]{1,0:T(8,128)(2,1)S(1)}, bf16[128,1024]{1,0:T(8,128)(2,1)S(1)}, u32[]{:S(2)}, u32[]{:S(2)}) %collective-permute-start.1) | collective-permute-done | bytes 262176 | tf_op jit(solution)/shard_map/ppermute | solution.py:44
  9.6 3.2 %collective-permute-start.2 = (bf16[128,1024]{1,0:T(8,128)(2,1)S(1)}, bf16[128,1024]{1,0:T(8,128)(2,1)S(1)}, u32[]{:S(2)}, u32[]{:S(2)}) collective-permute-start(bf16[128,1024]{1,0:T(8,128)(2,1)S(1)} %collective-permute-done.1.refs_3_.refs_7_), channel_id=1, source_target_pairs={{0,0},{2,2},{4,4},{6,6},{8,16},{10,18},{12,20},{14,22},{16,24},{18... | collective-permute-start | bytes 786440 | tf_op jit(solution)/shard_map/ppermute | solution.py:44
  12.8 1.3 %collective-permute-start.4 = (bf16[128,1024]{1,0:T(8,128)(2,1)S(1)}, bf16[128,1024]{1,0:T(8,128)(2,1)S(1)}, u32[]{:S(2)}, u32[]{:S(2)}) collective-permute-start(bf16[128,1024]{1,0:T(8,128)(2,1)S(1)} %collective-permute-done.1.refs_3_.refs_7_), channel_id=1, source_target_pairs={{0,4},{2,6},{4,0},{6,2},{8,12},{10,14},{12,8},{14,10},{16,20},{18,... | collective-permute-start | bytes 786440 | tf_op jit(solution)/shard_map/ppermute | solution.py:44
  14.1 0.2 collective-permute-start.10
  14.4 2.4 %collective-permute-start = (bf16[128,1024]{1,0:T(8,128)(2,1)S(1)}, bf16[128,1024]{1,0:T(8,128)(2,1)S(1)}, u32[]{:S(2)}, u32[]{:S(2)}) collective-permute-start(bf16[128,1024]{1,0:T(8,128)(2,1)S(1)} %prepare.1.refs_5_.refs_7_), channel_id=1, source_target_pairs={{0,2},{2,0},{4,6},{6,4},{8,10},{10,8},{12,14},{14,12},{16,18},{18,... | collective-permute-start | bytes 786440 | tf_op jit(solution)/shard_map/ppermute | solution.py:44
  16.7 1.1 %collective-permute-done.2.refs_3_.refs_7_ = bf16[128,1024]{1,0:T(8,128)(2,1)S(1)} collective-permute-done((bf16[128,1024]{1,0:T(8,128)(2,1)S(1)}, bf16[128,1024]{1,0:T(8,128)(2,1)S(1)}, u32[]{:S(2)}, u32[]{:S(2)}) %collective-permute-start.2) | collective-permute-done | bytes 262176 | tf_op jit(solution)/shard_map/ppermute | solution.py:44
  17.8 3.1 %collective-permute-start.3 = (bf16[128,1024]{1,0:T(8,128)(2,1)S(1)}, bf16[128,1024]{1,0:T(8,128)(2,1)S(1)}, u32[]{:S(2)}, u32[]{:S(2)}) collective-permute-start(bf16[128,1024]{1,0:T(8,128)(2,1)S(1)} %collective-permute-done.2.refs_3_.refs_7_), channel_id=1, source_target_pairs={{0,0},{2,2},{4,4},{6,6},{8,8},{10,10},{12,12},{14,14},{16,20},{18,... | collective-permute-start | bytes 786440 | tf_op jit(solution)/shard_map/ppermute | solution.py:44
  21.0 0.0 collective-permute-done.4.refs_4_.refs_8_
  21.0 3.2 %collective-permute-start.5 = (bf16[128,1024]{1,0:T(8,128)(2,1)S(1)}, bf16[128,1024]{1,0:T(8,128)(2,1)S(1)}, u32[]{:S(2)}, u32[]{:S(2)}) collective-permute-start(bf16[128,1024]{1,0:T(8,128)(2,1)S(1)} %collective-permute-done.4.refs_4_.refs_8_), channel_id=1, source_target_pairs={{0,0},{2,2},{4,4},{6,6},{8,16},{10,18},{12,12},{14,14},{16,24},{18... | collective-permute-start | bytes 786440 | tf_op jit(solution)/shard_map/ppermute | solution.py:44
  24.2 6.0 %collective-permute-done.10.refs_4_.refs_8_ = bf16[128,1024]{1,0:T(8,128)(2,1)S(1)} collective-permute-done((bf16[128,1024]{1,0:T(8,128)(2,1)S(1)}, bf16[128,1024]{1,0:T(8,128)(2,1)S(1)}, u32[]{:S(2)}, u32[]{:S(2)}) %collective-permute-start.10) | collective-permute-done | bytes 262176 | tf_op jit(solution)/shard_map/ppermute | solution.py:44
  30.2 2.7 %collective-permute-start.12 = (bf16[128,1024]{1,0:T(8,128)(2,1)S(1)}, bf16[128,1024]{1,0:T(8,128)(2,1)S(1)}, u32[]{:S(2)}, u32[]{:S(2)}) collective-permute-start(bf16[128,1024]{1,0:T(8,128)(2,1)S(1)} %collective-permute-done.10.refs_4_.refs_8_), channel_id=1, source_target_pairs={{0,2},{2,0},{4,6},{6,4},{8,10},{10,8},{12,14},{14,12},{16,18},{18,... | collective-permute-start | bytes 786440 | tf_op jit(solution)/shard_map/ppermute | solution.py:44
  32.8 0.0 collective-permute-done.refs_6_.refs_8_
  32.9 0.0 collective-permute-start.8
  32.9 0.5 collective-permute-start.9
  33.4 0.1 collective-permute-start.6
  33.4 4.3 %collective-permute-start.7 = (bf16[128,1024]{1,0:T(8,128)(2,1)S(1)}, bf16[128,1024]{1,0:T(8,128)(2,1)S(1)}, u32[]{:S(2)}, u32[]{:S(2)}) collective-permute-start(bf16[128,1024]{1,0:T(8,128)(2,1)S(1)} %collective-permute-done.5.refs_4_.refs_8_), channel_id=1, source_target_pairs={{0,2},{2,0},{4,6},{6,4},{8,10},{10,8},{12,14},{14,12},{16,18},{18,... | collective-permute-start | bytes 786440 | tf_op jit(solution)/shard_map/ppermute | solution.py:44
  37.8 1.2 %copy-done = bf16[128,3584]{1,0:T(8,128)(2,1)S(1)} copy-done((bf16[128,3584]{1,0:T(8,128)(2,1)S(1)}, bf16[128,3584]{1,0:T(8,128)(2,1)}, u32[]{:S(2)}) %copy-start) | copy-done | bytes 917528
  38.9 0.7 copy-done.3
  39.6 0.7 copy-done.7
  40.3 3.9 %attend2f.1 = (bf16[4,896,128]{2,1,0:T(8,128)(2,1)S(1)}, f32[4,896,128]{2,1,0:T(8,128)S(1)}, f32[4,896,128]{2,1,0:T(8,128)S(1)}, f32[4,896,128]{2,1,0:T(8,128)S(1)}) custom-call(s32[8]{0:T(128)S(1)} %copy-done.3, s32[2,16]{1,0:T(2,128)S(1)} %copy-done.7, f32[128,128]{1,0:T(8,128)S(1)} %get-tuple-element.28.cos_ref.refs_2_, ...), custom_call_target="tpu_custom_call" | custom-call | flops 469762048 | bytes 10000000 | tf_op jit(solution)/shard_map/attend2f/pallas_call | solution.py:177
  44.2 0.0 copy-start.4
  44.2 8.9 %attend4m.2 = (f32[4,896,128]{2,1,0:T(8,128)S(1)}, f32[4,896,128]{2,1,0:T(8,128)S(1)}, f32[4,896,128]{2,1,0:T(8,128)S(1)}) custom-call(s32[8]{0:T(128)S(1)} %copy-done.3, s32[4,16]{1,0:T(4,128)S(1)} %copy-done.5, bf16[4,896,128]{2,1,0:T(8,128)(2,1)S(1)} %get-tuple-element.15.refs_2_, ...), custom_call_target="tpu_custom_call", output_to_operand_aliasing={{0}: (11, {}), {1}: (12, {}), {2}: (13, {})} | custom-call | flops 939524096 | bytes 10000000 | tf_op jit(solution)/shard_map/attend4m/pallas_call | solution.py:177
  53.1 0.0 copy-start.6
  53.1 8.9 %attend4m.3 = (f32[4,896,128]{2,1,0:T(8,128)S(1)}, f32[4,896,128]{2,1,0:T(8,128)S(1)}, f32[4,896,128]{2,1,0:T(8,128)S(1)}) custom-call(s32[8]{0:T(128)S(1)} %copy-done.3, s32[4,16]{1,0:T(4,128)S(1)} %copy-done.4, bf16[4,896,128]{2,1,0:T(8,128)(2,1)S(1)} %get-tuple-element.15.refs_2_, ...), custom_call_target="tpu_custom_call", output_to_operand_aliasing={{0}: (11, {}), {1}: (12, {}), {2}: (13, {})} | custom-call | flops 939524096 | bytes 10000000 | tf_op jit(solution)/shard_map/attend4m/pallas_call | solution.py:177
  62.0 9.6 %attend4l.1 = bf16[128,3584]{1,0:T(8,128)(2,1)} custom-call(s32[8]{0:T(128)S(1)} %copy-done.3, s32[4,16]{1,0:T(4,128)S(1)} %copy-done.6, bf16[4,896,128]{2,1,0:T(8,128)(2,1)S(1)} %get-tuple-element.15.refs_2_, bf16[128,1024]{1,0:T(8,128)(2,1)S(1)} %collective-permute-done.3.refs_3_.refs_7_, bf16[128,1024]{1,0:T(8,128)(2,1)S(1)} %collective-permute-done.5.refs_4_.refs_8_, ...), custom_call_target="tpu_custom_call" | custom-call | flops 939524096 | bytes 10000000 | tf_op jit(solution)/shard_map/attend4l/pallas_call | solution.py:177
  (19 shorter events, 0.1 us)
Async XLA Ops:
  0.0 44.2 %copy-start.5 = (s32[4,16]{1,0:T(4,128)S(1)}, s32[4,16]{1,0:T(4,128)}, u32[]{:S(2)}) copy-start(s32[4,16]{1,0:T(4,128)} %constant.24.clone.refs_1_) | copy-start | bytes 772
  0.5 0.9 %copy-start.1 = (bf16[128,512]{1,0:T(8,128)(2,1)S(1)}, bf16[128,512]{1,0:T(8,128)(2,1)}, u32[]{:S(2)}) copy-start(bf16[128,512]{1,0:T(8,128)(2,1)} %k_ref.1) | copy-start | bytes 393220
  1.4 0.9 %copy-start.2 = (bf16[128,512]{1,0:T(8,128)(2,1)S(1)}, bf16[128,512]{1,0:T(8,128)(2,1)}, u32[]{:S(2)}) copy-start(bf16[128,512]{1,0:T(8,128)(2,1)} %v_ref.1) | copy-start | bytes 393220
  2.4 7.2 %collective-permute-start.1 = (bf16[128,1024]{1,0:T(8,128)(2,1)S(1)}, bf16[128,1024]{1,0:T(8,128)(2,1)S(1)}, u32[]{:S(2)}, u32[]{:S(2)}) collective-permute-start(bf16[128,1024]{1,0:T(8,128)(2,1)S(1)} %prepare.1.refs_5_.refs_7_), channel_id=1, source_target_pairs={{0,8},{2,10},{4,12},{6,14},{8,16},{10,18},{12,20},{14,22},{16,24},... | collective-permute-start | bytes 786440 | tf_op jit(solution)/shard_map/ppermute | solution.py:44
  9.6 8.2 %collective-permute-start.2 = (bf16[128,1024]{1,0:T(8,128)(2,1)S(1)}, bf16[128,1024]{1,0:T(8,128)(2,1)S(1)}, u32[]{:S(2)}, u32[]{:S(2)}) collective-permute-start(bf16[128,1024]{1,0:T(8,128)(2,1)S(1)} %collective-permute-done.1.refs_3_.refs_7_), channel_id=1, source_target_pairs={{0,0},{2,2},{4,4},{6,6},{8,16},{10,18},{12,20},{14,22},{16,24},{18... | collective-permute-start | bytes 786440 | tf_op jit(solution)/shard_map/ppermute | solution.py:44
  12.8 8.2 %collective-permute-start.4 = (bf16[128,1024]{1,0:T(8,128)(2,1)S(1)}, bf16[128,1024]{1,0:T(8,128)(2,1)S(1)}, u32[]{:S(2)}, u32[]{:S(2)}) collective-permute-start(bf16[128,1024]{1,0:T(8,128)(2,1)S(1)} %collective-permute-done.1.refs_3_.refs_7_), channel_id=1, source_target_pairs={{0,4},{2,6},{4,0},{6,2},{8,12},{10,14},{12,8},{14,10},{16,20},{18,... | collective-permute-start | bytes 786440 | tf_op jit(solution)/shard_map/ppermute | solution.py:44
  14.1 16.1 %collective-permute-start.10 = (bf16[128,1024]{1,0:T(8,128)(2,1)S(1)}, bf16[128,1024]{1,0:T(8,128)(2,1)S(1)}, u32[]{:S(2)}, u32[]{:S(2)}) collective-permute-start(bf16[128,1024]{1,0:T(8,128)(2,1)S(1)} %prepare.1.refs_5_.refs_7_), channel_id=1, source_target_pairs={{0,4},{2,6},{4,0},{6,2},{8,12},{10,14},{12,8},{14,10},{16,20},{18,... | collective-permute-start | bytes 786440 | tf_op jit(solution)/shard_map/ppermute | solution.py:44
  14.4 18.5 %collective-permute-start = (bf16[128,1024]{1,0:T(8,128)(2,1)S(1)}, bf16[128,1024]{1,0:T(8,128)(2,1)S(1)}, u32[]{:S(2)}, u32[]{:S(2)}) collective-permute-start(bf16[128,1024]{1,0:T(8,128)(2,1)S(1)} %prepare.1.refs_5_.refs_7_), channel_id=1, source_target_pairs={{0,2},{2,0},{4,6},{6,4},{8,10},{10,8},{12,14},{14,12},{16,18},{18,... | collective-permute-start | bytes 786440 | tf_op jit(solution)/shard_map/ppermute | solution.py:44
  16.7 16.1 %collective-permute-start.11 = (bf16[128,1024]{1,0:T(8,128)(2,1)S(1)}, bf16[128,1024]{1,0:T(8,128)(2,1)S(1)}, u32[]{:S(2)}, u32[]{:S(2)}) collective-permute-start(bf16[128,1024]{1,0:T(8,128)(2,1)S(1)} %collective-permute-done.1.refs_3_.refs_7_), channel_id=1, source_target_pairs={{0,2},{2,0},{4,6},{6,4},{8,10},{10,8},{12,14},{14,12},{16,18},{18,... | collective-permute-start | bytes 786440 | tf_op jit(solution)/shard_map/ppermute | solution.py:44
  17.8 15.5 %collective-permute-start.3 = (bf16[128,1024]{1,0:T(8,128)(2,1)S(1)}, bf16[128,1024]{1,0:T(8,128)(2,1)S(1)}, u32[]{:S(2)}, u32[]{:S(2)}) collective-permute-start(bf16[128,1024]{1,0:T(8,128)(2,1)S(1)} %collective-permute-done.2.refs_3_.refs_7_), channel_id=1, source_target_pairs={{0,0},{2,2},{4,4},{6,6},{8,8},{10,10},{12,12},{14,14},{16,20},{18,... | collective-permute-start | bytes 786440 | tf_op jit(solution)/shard_map/ppermute | solution.py:44
  21.0 12.4 %collective-permute-start.5 = (bf16[128,1024]{1,0:T(8,128)(2,1)S(1)}, bf16[128,1024]{1,0:T(8,128)(2,1)S(1)}, u32[]{:S(2)}, u32[]{:S(2)}) collective-permute-start(bf16[128,1024]{1,0:T(8,128)(2,1)S(1)} %collective-permute-done.4.refs_4_.refs_8_), channel_id=1, source_target_pairs={{0,0},{2,2},{4,4},{6,6},{8,16},{10,18},{12,12},{14,14},{16,24},{18... | collective-permute-start | bytes 786440 | tf_op jit(solution)/shard_map/ppermute | solution.py:44
  30.2 14.0 %collective-permute-start.12 = (bf16[128,1024]{1,0:T(8,128)(2,1)S(1)}, bf16[128,1024]{1,0:T(8,128)(2,1)S(1)}, u32[]{:S(2)}, u32[]{:S(2)}) collective-permute-start(bf16[128,1024]{1,0:T(8,128)(2,1)S(1)} %collective-permute-done.10.refs_4_.refs_8_), channel_id=1, source_target_pairs={{0,2},{2,0},{4,6},{6,4},{8,10},{10,8},{12,14},{14,12},{16,18},{18,... | collective-permute-start | bytes 786440 | tf_op jit(solution)/shard_map/ppermute | solution.py:44
  32.9 20.2 %collective-permute-start.8 = (bf16[128,1024]{1,0:T(8,128)(2,1)S(1)}, bf16[128,1024]{1,0:T(8,128)(2,1)S(1)}, u32[]{:S(2)}, u32[]{:S(2)}) collective-permute-start(bf16[128,1024]{1,0:T(8,128)(2,1)S(1)} %collective-permute-done.2.refs_3_.refs_7_), channel_id=1, source_target_pairs={{0,2},{2,0},{4,6},{6,4},{8,10},{10,8},{12,14},{14,12},{16,18},{18,... | collective-permute-start | bytes 786440 | tf_op jit(solution)/shard_map/ppermute | solution.py:44
  32.9 20.2 %collective-permute-start.9 = (bf16[128,1024]{1,0:T(8,128)(2,1)S(1)}, bf16[128,1024]{1,0:T(8,128)(2,1)S(1)}, u32[]{:S(2)}, u32[]{:S(2)}) collective-permute-start(bf16[128,1024]{1,0:T(8,128)(2,1)S(1)} %collective-permute-done.4.refs_4_.refs_8_), channel_id=1, source_target_pairs={{0,2},{2,0},{4,6},{6,4},{8,10},{10,8},{12,14},{14,12},{16,18},{18,... | collective-permute-start | bytes 786440 | tf_op jit(solution)/shard_map/ppermute | solution.py:44
  33.4 28.6 %collective-permute-start.6 = (bf16[128,1024]{1,0:T(8,128)(2,1)S(1)}, bf16[128,1024]{1,0:T(8,128)(2,1)S(1)}, u32[]{:S(2)}, u32[]{:S(2)}) collective-permute-start(bf16[128,1024]{1,0:T(8,128)(2,1)S(1)} %collective-permute-done.3.refs_3_.refs_7_), channel_id=1, source_target_pairs={{0,2},{2,0},{4,6},{6,4},{8,10},{10,8},{12,14},{14,12},{16,18},{18,... | collective-permute-start | bytes 786440 | tf_op jit(solution)/shard_map/ppermute | solution.py:44
  33.4 28.5 %collective-permute-start.7 = (bf16[128,1024]{1,0:T(8,128)(2,1)S(1)}, bf16[128,1024]{1,0:T(8,128)(2,1)S(1)}, u32[]{:S(2)}, u32[]{:S(2)}) collective-permute-start(bf16[128,1024]{1,0:T(8,128)(2,1)S(1)} %collective-permute-done.5.refs_4_.refs_8_), channel_id=1, source_target_pairs={{0,2},{2,0},{4,6},{6,4},{8,10},{10,8},{12,14},{14,12},{16,18},{18,... | collective-permute-start | bytes 786440 | tf_op jit(solution)/shard_map/ppermute | solution.py:44
  37.8 1.2 %copy-start = (bf16[128,3584]{1,0:T(8,128)(2,1)S(1)}, bf16[128,3584]{1,0:T(8,128)(2,1)}, u32[]{:S(2)}) copy-start(bf16[128,3584]{1,0:T(8,128)(2,1)} %refs_4_.1) | copy-start | bytes 2752516
  38.9 0.7 copy-start.3
  39.6 0.7 copy-start.7
  44.2 8.9 %copy-start.4 = (s32[4,16]{1,0:T(4,128)S(1)}, s32[4,16]{1,0:T(4,128)}, u32[]{:S(2)}) copy-start(s32[4,16]{1,0:T(4,128)} %constant.25.clone.refs_1_) | copy-start | bytes 772
  53.1 8.9 %copy-start.6 = (s32[4,16]{1,0:T(4,128)S(1)}, s32[4,16]{1,0:T(4,128)}, u32[]{:S(2)}) copy-start(s32[4,16]{1,0:T(4,128)} %constant.26.clone.refs_1_) | copy-start | bytes 772

commit v2 on v1

v2 whole, which is shorter than its diff:
```python
import functools

import jax
import jax.numpy as jnp
import numpy as np
from jax import lax
from jax.experimental import pallas as pl
from jax.experimental.pallas import tpu as pltpu
from jax.sharding import PartitionSpec as P


HEADS = 28
KV_HEADS = 4
HEAD_DIM = 128
GROUP = HEADS // KV_HEADS
ROPE_BASE = 1000000.0
SCORE_SCALE = HEAD_DIM ** (-0.5) * 1.4426950408889634
MASKED = -65536.0
NOWHERE = 1 << 28
VMEM_LIMIT = 24 * 1024 * 1024
SLAB = 32


def cycles(wanted, count):
    pairs = dict(wanted)
    starts = [s for s in pairs if s not in set(pairs.values())]
    for start in starts:
        at = start
        while at in pairs:
            at = pairs[at]
        pairs[at] = start
    for i in range(count):
        pairs.setdefault(i, i)
    assert sorted(pairs.values()) == list(range(count))
    return sorted(pairs.items())


class Piece:
    def __init__(self, data, source):
        self.data, self.source = data, source

    def move(self, pairs):
        source = list(self.source)
        for s, t in pairs:
            source[t] = self.source[s]
        return Piece(lax.ppermute(self.data, "seq", pairs), source)


def rotated(x, cosine, sine):
    return x * cosine + pltpu.roll(x, HEAD_DIM // 2, 1) * sine


def prepare_kernel(k_ref, v_ref, cos_ref, sin_ref, kv_ref):
    width = KV_HEADS * HEAD_DIM
    cosine, sine = cos_ref[...], sin_ref[...]
    for g in range(KV_HEADS):
        cols = slice(g * HEAD_DIM, (g + 1) * HEAD_DIM)
        kv_ref[:, cols] = rotated(k_ref[:, cols].astype(jnp.float32), cosine, sine).astype(jnp.bfloat16)
    kv_ref[:, width:] = v_ref[...]


def prepare(keys, values, cosine, sine):
    rows = keys.shape[0]
    return pl.pallas_call(
        prepare_kernel,
        out_shape=jax.ShapeDtypeStruct((rows, 2 * KV_HEADS * HEAD_DIM), jnp.bfloat16),
        cost_estimate=pl.CostEstimate(flops=10**6, bytes_accessed=6 * 10**5, transcendentals=0),
        compiler_params=pltpu.CompilerParams(vmem_limit_bytes=VMEM_LIMIT),
        name="prepare",
    )(keys, values, cosine, sine)


def attend_kernel(count, first, last, *refs):
    refs = list(refs)
    take = lambda n: [refs.pop(0) for _ in range(n)]
    lengths_ref, bases_ref, q_ref = take(3)
    kv_refs = take(count)
    if first:
        cos_ref, sin_ref = take(2)
    else:
        max_in, sum_in, acc_in = take(3)
    if last:
        (out_ref,) = take(1)
    elif first:
        q_out, max_out, sum_out, acc_out = take(4)
    else:
        max_out, sum_out, acc_out = take(3)
    score_ref, weight_ref, bias_ref = take(3)
    if last:
        sum_out, acc_out = take(2)

    me = lax.axis_index("seq")
    rows = kv_refs[0].shape[0]
    width = KV_HEADS * HEAD_DIM
    tall = GROUP * rows

    own = me * rows + lax.broadcasted_iota(jnp.int32, (rows, rows), 1)
    start = jnp.zeros((rows, rows), jnp.int32)
    end = 0
    for d in range(lengths_ref.shape[0]):
        end = end + lengths_ref[d]
        start = start + jnp.where(own >= end, lengths_ref[d], 0)
    for b in range(count):
        place = bases_ref[b, me] + lax.broadcasted_iota(jnp.int32, (rows, rows), 0)
        allowed = (place >= start) & (place <= own)
        bias_ref[b * rows:(b + 1) * rows, :] = jnp.where(allowed, 0.0, MASKED).astype(jnp.bfloat16)
    same = lax.broadcasted_iota(jnp.int32, (rows, rows), 0) == lax.broadcasted_iota(jnp.int32, (rows, rows), 1)
    unit = jnp.where(same, 1.0, 0.0).astype(jnp.bfloat16)
    units = jnp.concatenate([unit] * GROUP, axis=0)

    if first:
        cosine, sine = cos_ref[...], sin_ref[...]
        for h in range(HEADS):
            head = q_ref[:, h * HEAD_DIM:(h + 1) * HEAD_DIM].astype(jnp.float32)
            g, at = h // GROUP, h % GROUP * rows
            q_out[g, at:at + rows] = rotated(head, cosine, sine).astype(jnp.bfloat16)
        q_ref = q_out

    def score(g):
        q = jnp.concatenate([q_ref[g], units], axis=1)
        k = jnp.concatenate([r[:, g * HEAD_DIM:(g + 1) * HEAD_DIM] for r in kv_refs], axis=0)
        k = jnp.concatenate([k, bias_ref[...]], axis=1)
        return lax.dot_general(q, k, (((1,), (1,)), ((), ())), preferred_element_type=jnp.float32)

    score_ref[0] = score(0)
    for g in range(KV_HEADS):
        slot = g % 2
        if g + 1 < KV_HEADS:
            score_ref[1 - slot] = score(g + 1)
        v = jnp.concatenate(
            [r[:, width + g * HEAD_DIM:width + (g + 1) * HEAD_DIM] for r in kv_refs], axis=0
        )
        for at in range(0, tall, SLAB):
            here = slice(at, at + SLAB)
            raw = score_ref[slot, here]
            top = jnp.max(raw, axis=1, keepdims=True) * SCORE_SCALE
            if first:
                top = jnp.broadcast_to(top, (SLAB, HEAD_DIM))
                total = None
            else:
                old = max_in[g, here]
                top = jnp.maximum(old, top)
                shrink = jnp.exp2(old - top)
                total = sum_in[g, here] * shrink
                acc_out[g, here] = acc_in[g, here] * shrink
            for b in range(count):
                cols = slice(b * rows, (b + 1) * rows)
                weight = jnp.exp2(raw[:, cols] * SCORE_SCALE - top)
                total = weight if total is None else total + weight
                weight_ref[slot, here, cols] = weight.astype(jnp.bfloat16)
            sum_out[g, here] = total
            if not last:
                max_out[g, here] = top
        mixed = jnp.dot(weight_ref[slot], v, preferred_element_type=jnp.float32)
        if first:
            acc_out[g] = mixed
        elif not last:
            acc_out[g] += mixed
        else:
            for h in range(GROUP):
                here = slice(h * rows, (h + 1) * rows)
                cols = slice((g * GROUP + h) * HEAD_DIM, (g * GROUP + h + 1) * HEAD_DIM)
                total = jnp.sum(sum_out[g, here], axis=1, keepdims=True)
                out_ref[:, cols] = ((acc_out[g, here] + mixed[here]) / total).astype(jnp.bfloat16)


def attend(lengths, q, pieces, table, state=None, turn=None, last=False):
    first = state is None
    count = len(pieces)
    rows = pieces[0].data.shape[0]
    assert rows == HEAD_DIM
    stacked = (KV_HEADS, GROUP * rows, HEAD_DIM)
    smem = pl.BlockSpec(memory_space=pltpu.SMEM)
    vmem = pl.BlockSpec(memory_space=pltpu.VMEM)
    args = [lengths, table, q] + [p.data for p in pieces]
    aliases = {}
    if first:
        args += list(turn)
    else:
        if not last:
            aliases = {len(args) + n: n for n in range(3)}
        args += list(state)
    held = jax.ShapeDtypeStruct(stacked, jnp.float32)
    if last:
        out_shape = [jax.ShapeDtypeStruct((rows, HEADS * HEAD_DIM), jnp.bfloat16)]
    elif first:
        out_shape = [jax.ShapeDtypeStruct(stacked, jnp.bfloat16)] + [held] * 3
    else:
        out_shape = [held] * 3
    scratch = [
        pltpu.VMEM((2, GROUP * rows, count * rows), jnp.float32),
        pltpu.VMEM((2, GROUP * rows, count * rows), jnp.bfloat16),
        pltpu.VMEM((count * rows, rows), jnp.bfloat16),
    ]
    if last:
        scratch += [pltpu.VMEM(stacked, jnp.float32)] * 2
    out = pl.pallas_call(
        functools.partial(attend_kernel, count, first, last),
        out_shape=out_shape,
        in_specs=[smem, smem] + [vmem] * (len(args) - 2),
        out_specs=[vmem] * len(out_shape),
        scratch_shapes=scratch,
        input_output_aliases=aliases,
        cost_estimate=pl.CostEstimate(
            flops=4 * rows * HEADS * count * rows * HEAD_DIM,
            bytes_accessed=4 * 10**6,
            transcendentals=rows * HEADS * count * rows,
        ),
        compiler_params=pltpu.CompilerParams(vmem_limit_bytes=VMEM_LIMIT),
    )(*args)
    return out[0] if last else out


def turns(rows, doc_lengths):
    half = HEAD_DIM // 2
    place = lax.axis_index("seq") * rows + jnp.arange(rows, dtype=jnp.int32)
    start = jnp.zeros_like(place)
    end = jnp.int32(0)
    for d in range(doc_lengths.shape[0]):
        end = end + doc_lengths[d]
        start = start + jnp.where(place >= end, doc_lengths[d], 0)
    freq = jnp.power(jnp.float32(ROPE_BASE), -2.0 * jnp.arange(half, dtype=jnp.float32) / HEAD_DIM)
    angle = (place - start).astype(jnp.float32)[:, None] * freq[None, :]
    cosine, sine = jnp.cos(angle), jnp.sin(angle)
    return jnp.concatenate([cosine, cosine], axis=1), jnp.concatenate([-sine, sine], axis=1)


def per_device(count, queries, keys, values, doc_lengths):
    rows = queries.shape[0]
    most_doc = rows * count * 5 // 8
    reach = -(-(most_doc - 1) // rows)
    chip_reach = -(-(most_doc - 1) // (2 * rows))

    def closed(shift, keep):
        return cycles({i: i + shift for i in range(count) if i + shift < count and keep(i)}, count)

    sibling = [(i, i ^ 1) for i in range(count)]
    across = [(i, i ^ 2) for i in range(count)]
    turn = turns(rows, doc_lengths)
    own = Piece(prepare(keys, values, *turn), list(range(count)))
    late = own.move(sibling)
    stages = [[own]]
    a, before = own, None
    half_reach = chip_reach // 2
    for s in range(1, half_reach + 1):
        b = a.move(across)
        a = a.move(closed(4, lambda i: i >= 4 * (s - 1)))
        stage = [a, b, a.move(sibling), b.move(sibling)]
        stages.append(([late] if s == 1 else []) + stage)
        before = b
    if chip_reach % 2:
        near = 4 * half_reach
        c = before.move(closed(4, lambda i: not i & 2 and i >= near - 4))
        a = a.move(closed(2, lambda i: i >= near))
        stages += [[a, c], [a.move(sibling), c.move(sibling)]]
    else:
        b = a.move(across)
        stages += [[b], [b.move(sibling)]]

    seen = [set() for _ in range(count)]
    tables = []
    for pieces in stages:
        table = np.full((len(pieces), count), NOWHERE, np.int32)
        for b, piece in enumerate(pieces):
            for i in range(count):
                j = piece.source[i]
                if i - reach <= j <= i and j not in seen[i]:
                    seen[i].add(j)
                    table[b, i] = j * rows
        tables.append(jnp.asarray(table))
    for i in range(count):
        assert seen[i] == set(range(max(0, i - reach), i + 1))

    state = None
    for n, pieces in enumerate(stages):
        if n == 0:
            q, *state = attend(doc_lengths, queries, pieces, tables[n], turn=turn)
        elif n < len(stages) - 1:
            state = attend(doc_lengths, q, pieces, tables[n], state=state)
        else:
            return attend(doc_lengths, q, pieces, tables[n], state=state, last=True)


def solution(mesh):
    count = mesh.shape["seq"]

    def body(*args):
        return per_device(count, *args)

    return jax.shard_map(
        body,
        mesh=mesh,
        in_specs=(
            P(("grp", "seq"), None),
            P(("grp", "seq"), None),
            P(("grp", "seq"), None),
            P("grp"),
        ),
        out_specs=P(("grp", "seq"), None),
        check_vma=False,
    )
```

time: 71.9 us -> 71.5 us (level)
  Pallas kernels: 31.3 us -> 19 us
  other arithmetic: 0.42 us -> 5.5 us
  between operations: 0.19 us -> 5.26 us
  local copies, waits for them, and re-layouts: 4.33 us -> 5.95 us
    pallas_call x4 -> x5, Pallas kernels: 31.2 us -> 18.9 us  [attend(): pl.pallas_call(functools.partial(attend_kernel, count, first, last), out_...]
    convert_element_type x1, other arithmetic: 0.01 us -> 5.08 us  [turns(): angle = (place - start).astype(jnp.float32)[:, None] * freq[None, :]]
    slice x0 -> x1, local copies, waits for them, and re-layouts: none -> 1.64 us  [turns(): end = end + doc_lengths[d]]
    unnamed x16 -> x18, local copies, waits for them, and re-layouts: 4.33 us -> 4.31 us
  transfers between devices with their start and end apart: 13 -> 13, of which waited for: 3 -> 3; matrix products, arithmetic and copies ran while one was open for 0% -> 0% of each run, Pallas kernels for 30% -> 21%
where the time goes in v2:
time: 71.5 us; the launch traced here: 71.1 us
  starting transfers between devices  22.3 us (31%)
  Pallas kernels  19 us (27%)
  waiting for transfers between devices  13 us (18%)
  local copies, waits for them, and re-layouts  5.95 us (8%)
  other arithmetic  5.5 us (8%)
  between operations  5.26 us (7%)
    ppermute x13, starting transfers between devices, move(): return Piece(lax.ppermute(self.data, 'seq', pairs), source)  22.3 us
    pallas_call x5, Pallas kernels, attend(): pl.pallas_call(functools.partial(attend_kernel, count, first, last), out_...  18.9 us
    ppermute x13, waiting for transfers between devices, move(): return Piece(lax.ppermute(self.data, 'seq', pairs), source)  13 us
    convert_element_type x1, other arithmetic, turns(): angle = (place - start).astype(jnp.float32)[:, None] * freq[None, :]  5.08 us
    unnamed x18, local copies, waits for them, and re-layouts  4.31 us
    slice x1, local copies, waits for them, and re-layouts, turns(): end = end + doc_lengths[d]  1.64 us
  transfers between devices with their start and end apart: 13, of which 3 were waited for; matrix products, arithmetic and copies ran while one was open for 0% of the time, Pallas kernels for 21%

profile of v2, /device:TPU:19, one launch (start us, length us, event | category | flops | bytes accessed | tf_op | source)
XLA Modules:
  0.0 71.1 jit_solution(4949553915662992910)
XLA Ops:
  0.0 1.6 %fusion.10 = (s32[1]{0:T(128)}, s32[1]{0:T(128)}, s32[1]{0:T(128)}, s32[1]{0:T(128)}, s32[1]{0:T(128)}, /*index=5*/s32[1]{0:T(128)}, s32[1]{0:T(128)}, s32[1]{0:T(128)}) fusion(s32[8]{0:T(128)} %refs_0_.9), kind=kLoop, calls=%fused_computation.23 | loop fusion | bytes 64 | tf_op jit(solution)/shard_map/slice | solution.py:220
  6.7 5.1 %fusion.9 = f32[128]{0:T(128)S(1)} fusion(s32[]{:T(128)} %bitcast.7, s32[]{:T(128)S(6)} %add.94, s32[]{:T(128)} %bitcast.6, s32[]{:T(128)S(6)} %add.92, s32[]{:T(128)} %bitcast.5, s32[]{:T(128)S(6)} %add.90, s32[]{:T(128)} %bitcast.4, s32[]{:T(128)S(6)} %add.88, s32[]{:T(128)} %bitcast.3, s32[]{:T(128)S(6)} %add.86, s32[]{:T(128)} %bitcast.2, s32[]{:T(128)S(6)} %add.84, ...), kind=kLoop, calls=%fused_computation.21 | loop fusion | flops 3328 | bytes 576 | tf_op jit(solution)/shard_map/convert_element_type | solution.py:223
  11.8 0.3 fusion
  12.1 0.1 pad_maximum_fusion
  12.2 0.0 copy-start.1
  12.3 0.9 %copy-done.1 = bf16[128,512]{1,0:T(8,128)(2,1)S(1)} copy-done((bf16[128,512]{1,0:T(8,128)(2,1)S(1)}, bf16[128,512]{1,0:T(8,128)(2,1)}, u32[]{:S(2)}) %copy-start.1) | copy-done | bytes 131096
  13.2 0.9 %copy-done.2 = bf16[128,512]{1,0:T(8,128)(2,1)S(1)} copy-done((bf16[128,512]{1,0:T(8,128)(2,1)S(1)}, bf16[128,512]{1,0:T(8,128)(2,1)}, u32[]{:S(2)}) %copy-start.2) | copy-done | bytes 131096
  14.1 0.1 prepare.1.refs_3_
  14.2 1.3 %collective-permute-start = (bf16[128,1024]{1,0:T(8,128)(2,1)S(1)}, bf16[128,1024]{1,0:T(8,128)(2,1)S(1)}, u32[]{:S(2)}, u32[]{:S(2)}) collective-permute-start(bf16[128,1024]{1,0:T(8,128)(2,1)S(1)} %prepare.1.refs_3_), channel_id=1, source_target_pairs={{0,8},{2,10},{4,12},{6,14},{8,16},{10,18},{12,20},{14,22},{16,24},... | collective-permute-start | bytes 786440 | tf_op jit(solution)/shard_map/ppermute | solution.py:46
  15.5 5.9 %collective-permute-done.refs_4_ = bf16[128,1024]{1,0:T(8,128)(2,1)S(1)} collective-permute-done((bf16[128,1024]{1,0:T(8,128)(2,1)S(1)}, bf16[128,1024]{1,0:T(8,128)(2,1)S(1)}, u32[]{:S(2)}, u32[]{:S(2)}) %collective-permute-start) | collective-permute-done | bytes 262176 | tf_op jit(solution)/shard_map/ppermute | solution.py:46
  21.4 3.2 %collective-permute-start.1 = (bf16[128,1024]{1,0:T(8,128)(2,1)S(1)}, bf16[128,1024]{1,0:T(8,128)(2,1)S(1)}, u32[]{:S(2)}, u32[]{:S(2)}) collective-permute-start(bf16[128,1024]{1,0:T(8,128)(2,1)S(1)} %collective-permute-done.refs_4_), channel_id=1, source_target_pairs={{0,0},{2,2},{4,4},{6,6},{8,16},{10,18},{12,20},{14,22},{16,24},{18... | collective-permute-start | bytes 786440 | tf_op jit(solution)/shard_map/ppermute | solution.py:46
  24.6 1.3 %collective-permute-start.4 = (bf16[128,1024]{1,0:T(8,128)(2,1)S(1)}, bf16[128,1024]{1,0:T(8,128)(2,1)S(1)}, u32[]{:S(2)}, u32[]{:S(2)}) collective-permute-start(bf16[128,1024]{1,0:T(8,128)(2,1)S(1)} %collective-permute-done.refs_4_), channel_id=1, source_target_pairs={{0,4},{2,6},{4,0},{6,2},{8,12},{10,14},{12,8},{14,10},{16,20},{18,... | collective-permute-start | bytes 786440 | tf_op jit(solution)/shard_map/ppermute | solution.py:46
  25.9 0.2 collective-permute-start.10
  26.1 2.4 %collective-permute-start.9 = (bf16[128,1024]{1,0:T(8,128)(2,1)S(1)}, bf16[128,1024]{1,0:T(8,128)(2,1)S(1)}, u32[]{:S(2)}, u32[]{:S(2)}) collective-permute-start(bf16[128,1024]{1,0:T(8,128)(2,1)S(1)} %prepare.1.refs_3_), channel_id=1, source_target_pairs={{0,2},{2,0},{4,6},{6,4},{8,10},{10,8},{12,14},{14,12},{16,18},{18,... | collective-permute-start | bytes 786440 | tf_op jit(solution)/shard_map/ppermute | solution.py:46
  28.5 1.1 %collective-permute-done.1.refs_3_ = bf16[128,1024]{1,0:T(8,128)(2,1)S(1)} collective-permute-done((bf16[128,1024]{1,0:T(8,128)(2,1)S(1)}, bf16[128,1024]{1,0:T(8,128)(2,1)S(1)}, u32[]{:S(2)}, u32[]{:S(2)}) %collective-permute-start.1) | collective-permute-done | bytes 262176 | tf_op jit(solution)/shard_map/ppermute | solution.py:46
  29.6 3.1 %collective-permute-start.2 = (bf16[128,1024]{1,0:T(8,128)(2,1)S(1)}, bf16[128,1024]{1,0:T(8,128)(2,1)S(1)}, u32[]{:S(2)}, u32[]{:S(2)}) collective-permute-start(bf16[128,1024]{1,0:T(8,128)(2,1)S(1)} %collective-permute-done.1.refs_3_), channel_id=1, source_target_pairs={{0,0},{2,2},{4,4},{6,6},{8,8},{10,10},{12,12},{14,14},{16,20},{18,... | collective-permute-start | bytes 786440 | tf_op jit(solution)/shard_map/ppermute | solution.py:46
  32.8 3.2 %collective-permute-start.5 = (bf16[128,1024]{1,0:T(8,128)(2,1)S(1)}, bf16[128,1024]{1,0:T(8,128)(2,1)S(1)}, u32[]{:S(2)}, u32[]{:S(2)}) collective-permute-start(bf16[128,1024]{1,0:T(8,128)(2,1)S(1)} %collective-permute-done.4.refs_4_), channel_id=1, source_target_pairs={{0,0},{2,2},{4,4},{6,6},{8,16},{10,18},{12,12},{14,14},{16,24},{18... | collective-permute-start | bytes 786440 | tf_op jit(solution)/shard_map/ppermute | solution.py:46
  36.0 6.0 %collective-permute-done.10.refs_5_ = bf16[128,1024]{1,0:T(8,128)(2,1)S(1)} collective-permute-done((bf16[128,1024]{1,0:T(8,128)(2,1)S(1)}, bf16[128,1024]{1,0:T(8,128)(2,1)S(1)}, u32[]{:S(2)}, u32[]{:S(2)}) %collective-permute-start.10) | collective-permute-done | bytes 262176 | tf_op jit(solution)/shard_map/ppermute | solution.py:46
  42.0 2.7 %collective-permute-start.12 = (bf16[128,1024]{1,0:T(8,128)(2,1)S(1)}, bf16[128,1024]{1,0:T(8,128)(2,1)S(1)}, u32[]{:S(2)}, u32[]{:S(2)}) collective-permute-start(bf16[128,1024]{1,0:T(8,128)(2,1)S(1)} %collective-permute-done.10.refs_5_), channel_id=1, source_target_pairs={{0,2},{2,0},{4,6},{6,4},{8,10},{10,8},{12,14},{14,12},{16,18},{18,... | collective-permute-start | bytes 786440 | tf_op jit(solution)/shard_map/ppermute | solution.py:46
  44.6 0.5 collective-permute-start.8
  45.2 0.1 collective-permute-start.3
  45.2 4.3 %collective-permute-start.6 = (bf16[128,1024]{1,0:T(8,128)(2,1)S(1)}, bf16[128,1024]{1,0:T(8,128)(2,1)S(1)}, u32[]{:S(2)}, u32[]{:S(2)}) collective-permute-start(bf16[128,1024]{1,0:T(8,128)(2,1)S(1)} %collective-permute-done.5.refs_4_), channel_id=1, source_target_pairs={{0,2},{2,0},{4,6},{6,4},{8,10},{10,8},{12,14},{14,12},{16,18},{18,... | collective-permute-start | bytes 786440 | tf_op jit(solution)/shard_map/ppermute | solution.py:46
  49.5 1.2 %copy-done = bf16[128,3584]{1,0:T(8,128)(2,1)S(1)} copy-done((bf16[128,3584]{1,0:T(8,128)(2,1)S(1)}, bf16[128,3584]{1,0:T(8,128)(2,1)}, u32[]{:S(2)}) %copy-start) | copy-done | bytes 917528
  50.7 0.7 copy-done.3
  51.4 0.7 copy-done.8
  52.0 2.5 %shard_map.91 = (bf16[4,896,128]{2,1,0:T(8,128)(2,1)S(1)}, f32[4,896,128]{2,1,0:T(8,128)S(1)}, f32[4,896,128]{2,1,0:T(8,128)S(1)}, f32[4,896,128]{2,1,0:T(8,128)S(1)}) custom-call(s32[8]{0:T(128)S(1)} %copy-done.3, s32[1,16]{1,0:T(1,128)S(1)} %copy-done.8, bf16[128,3584]{1,0:T(8,128)(2,1)S(1)} %copy-done, bf16[128,1024]{1,0:T(8,128)(2,1)S(1)} %prepare.1.refs_3_, ...), custom_call_target="tpu_custom_call" | custom-call | flops 234881024 | bytes 4000000 | tf_op jit(solution)/shard_map/pallas_call | solution.py:197
  54.6 5.4 %shard_map.92 = (f32[4,896,128]{2,1,0:T(8,128)S(1)}, f32[4,896,128]{2,1,0:T(8,128)S(1)}, f32[4,896,128]{2,1,0:T(8,128)S(1)}) custom-call(s32[8]{0:T(128)S(1)} %copy-done.3, s32[5,16]{1,0:T(8,128)S(1)} %copy-done.4, bf16[4,896,128]{2,1,0:T(8,128)(2,1)S(1)} %get-tuple-element.18.refs_2_, ...), custom_call_target="tpu_custom_call", output_to_operand_aliasing={{0}: (8, {}), {1}: (9, {}), {2}: (10, {})} | custom-call | flops 1174405120 | bytes 4000000 | tf_op jit(solution)/shard_map/pallas_call | solution.py:197
  60.0 0.0 copy-start.7
  60.0 4.2 %shard_map.93 = (f32[4,896,128]{2,1,0:T(8,128)S(1)}, f32[4,896,128]{2,1,0:T(8,128)S(1)}, f32[4,896,128]{2,1,0:T(8,128)S(1)}) custom-call(s32[8]{0:T(128)S(1)} %copy-done.3, s32[4,16]{1,0:T(4,128)S(1)} %copy-done.5, bf16[4,896,128]{2,1,0:T(8,128)(2,1)S(1)} %get-tuple-element.18.refs_2_, ...), custom_call_target="tpu_custom_call", output_to_operand_aliasing={{0}: (7, {}), {1}: (8, {}), {2}: (9, {})} | custom-call | flops 939524096 | bytes 4000000 | tf_op jit(solution)/shard_map/pallas_call | solution.py:197
  64.3 0.0 copy-start.6
  64.3 3.0 %shard_map.94 = (f32[4,896,128]{2,1,0:T(8,128)S(1)}, f32[4,896,128]{2,1,0:T(8,128)S(1)}, f32[4,896,128]{2,1,0:T(8,128)S(1)}) custom-call(s32[8]{0:T(128)S(1)} %copy-done.3, s32[2,16]{1,0:T(2,128)S(1)} %copy-done.7, bf16[4,896,128]{2,1,0:T(8,128)(2,1)S(1)} %get-tuple-element.18.refs_2_, ...), custom_call_target="tpu_custom_call", output_to_operand_aliasing={{0}: (5, {}), {1}: (6, {}), {2}: (7, {})} | custom-call | flops 469762048 | bytes 4000000 | tf_op jit(solution)/shard_map/pallas_call | solution.py:197
  67.3 3.8 %shard_map.95 = bf16[128,3584]{1,0:T(8,128)(2,1)} custom-call(s32[8]{0:T(128)S(1)} %copy-done.3, s32[2,16]{1,0:T(2,128)S(1)} %copy-done.6, bf16[4,896,128]{2,1,0:T(8,128)(2,1)S(1)} %get-tuple-element.18.refs_2_, bf16[128,1024]{1,0:T(8,128)(2,1)S(1)} %collective-permute-done.3.refs_3_, bf16[128,1024]{1,0:T(8,128)(2,1)S(1)} %collective-permute-done.6.refs_4_, ...), custom_call_target="tpu_custom_call" | custom-call | flops 469762048 | bytes 4000000 | tf_op jit(solution)/shard_map/pallas_call | solution.py:197
  (23 shorter events, 0.1 us)
Async XLA Ops:
  0.0 54.6 %copy-start.4 = (s32[5,16]{1,0:T(8,128)S(1)}, s32[5,16]{1,0:T(8,128)}, u32[]{:S(2)}) copy-start(s32[5,16]{1,0:T(8,128)} %constant.28.clone.refs_1_) | copy-start | bytes 964
  12.2 0.9 %copy-start.1 = (bf16[128,512]{1,0:T(8,128)(2,1)S(1)}, bf16[128,512]{1,0:T(8,128)(2,1)}, u32[]{:S(2)}) copy-start(bf16[128,512]{1,0:T(8,128)(2,1)} %k_ref.1) | copy-start | bytes 393220
  13.2 0.9 %copy-start.2 = (bf16[128,512]{1,0:T(8,128)(2,1)S(1)}, bf16[128,512]{1,0:T(8,128)(2,1)}, u32[]{:S(2)}) copy-start(bf16[128,512]{1,0:T(8,128)(2,1)} %v_ref.1) | copy-start | bytes 393220
  14.2 7.2 %collective-permute-start = (bf16[128,1024]{1,0:T(8,128)(2,1)S(1)}, bf16[128,1024]{1,0:T(8,128)(2,1)S(1)}, u32[]{:S(2)}, u32[]{:S(2)}) collective-permute-start(bf16[128,1024]{1,0:T(8,128)(2,1)S(1)} %prepare.1.refs_3_), channel_id=1, source_target_pairs={{0,8},{2,10},{4,12},{6,14},{8,16},{10,18},{12,20},{14,22},{16,24},... | collective-permute-start | bytes 786440 | tf_op jit(solution)/shard_map/ppermute | solution.py:46
  21.4 8.2 %collective-permute-start.1 = (bf16[128,1024]{1,0:T(8,128)(2,1)S(1)}, bf16[128,1024]{1,0:T(8,128)(2,1)S(1)}, u32[]{:S(2)}, u32[]{:S(2)}) collective-permute-start(bf16[128,1024]{1,0:T(8,128)(2,1)S(1)} %collective-permute-done.refs_4_), channel_id=1, source_target_pairs={{0,0},{2,2},{4,4},{6,6},{8,16},{10,18},{12,20},{14,22},{16,24},{18... | collective-permute-start | bytes 786440 | tf_op jit(solution)/shard_map/ppermute | solution.py:46
  24.6 8.2 %collective-permute-start.4 = (bf16[128,1024]{1,0:T(8,128)(2,1)S(1)}, bf16[128,1024]{1,0:T(8,128)(2,1)S(1)}, u32[]{:S(2)}, u32[]{:S(2)}) collective-permute-start(bf16[128,1024]{1,0:T(8,128)(2,1)S(1)} %collective-permute-done.refs_4_), channel_id=1, source_target_pairs={{0,4},{2,6},{4,0},{6,2},{8,12},{10,14},{12,8},{14,10},{16,20},{18,... | collective-permute-start | bytes 786440 | tf_op jit(solution)/shard_map/ppermute | solution.py:46
  25.9 16.1 %collective-permute-start.10 = (bf16[128,1024]{1,0:T(8,128)(2,1)S(1)}, bf16[128,1024]{1,0:T(8,128)(2,1)S(1)}, u32[]{:S(2)}, u32[]{:S(2)}) collective-permute-start(bf16[128,1024]{1,0:T(8,128)(2,1)S(1)} %prepare.1.refs_3_), channel_id=1, source_target_pairs={{0,4},{2,6},{4,0},{6,2},{8,12},{10,14},{12,8},{14,10},{16,20},{18,... | collective-permute-start | bytes 786440 | tf_op jit(solution)/shard_map/ppermute | solution.py:46
  26.1 18.5 %collective-permute-start.9 = (bf16[128,1024]{1,0:T(8,128)(2,1)S(1)}, bf16[128,1024]{1,0:T(8,128)(2,1)S(1)}, u32[]{:S(2)}, u32[]{:S(2)}) collective-permute-start(bf16[128,1024]{1,0:T(8,128)(2,1)S(1)} %prepare.1.refs_3_), channel_id=1, source_target_pairs={{0,2},{2,0},{4,6},{6,4},{8,10},{10,8},{12,14},{14,12},{16,18},{18,... | collective-permute-start | bytes 786440 | tf_op jit(solution)/shard_map/ppermute | solution.py:46
  28.5 16.1 %collective-permute-start.11 = (bf16[128,1024]{1,0:T(8,128)(2,1)S(1)}, bf16[128,1024]{1,0:T(8,128)(2,1)S(1)}, u32[]{:S(2)}, u32[]{:S(2)}) collective-permute-start(bf16[128,1024]{1,0:T(8,128)(2,1)S(1)} %collective-permute-done.refs_4_), channel_id=1, source_target_pairs={{0,2},{2,0},{4,6},{6,4},{8,10},{10,8},{12,14},{14,12},{16,18},{18,... | collective-permute-start | bytes 786440 | tf_op jit(solution)/shard_map/ppermute | solution.py:46
  29.6 15.5 %collective-permute-start.2 = (bf16[128,1024]{1,0:T(8,128)(2,1)S(1)}, bf16[128,1024]{1,0:T(8,128)(2,1)S(1)}, u32[]{:S(2)}, u32[]{:S(2)}) collective-permute-start(bf16[128,1024]{1,0:T(8,128)(2,1)S(1)} %collective-permute-done.1.refs_3_), channel_id=1, source_target_pairs={{0,0},{2,2},{4,4},{6,6},{8,8},{10,10},{12,12},{14,14},{16,20},{18,... | collective-permute-start | bytes 786440 | tf_op jit(solution)/shard_map/ppermute | solution.py:46
  32.8 12.4 %collective-permute-start.5 = (bf16[128,1024]{1,0:T(8,128)(2,1)S(1)}, bf16[128,1024]{1,0:T(8,128)(2,1)S(1)}, u32[]{:S(2)}, u32[]{:S(2)}) collective-permute-start(bf16[128,1024]{1,0:T(8,128)(2,1)S(1)} %collective-permute-done.4.refs_4_), channel_id=1, source_target_pairs={{0,0},{2,2},{4,4},{6,6},{8,16},{10,18},{12,12},{14,14},{16,24},{18... | collective-permute-start | bytes 786440 | tf_op jit(solution)/shard_map/ppermute | solution.py:46
  42.0 12.6 %collective-permute-start.12 = (bf16[128,1024]{1,0:T(8,128)(2,1)S(1)}, bf16[128,1024]{1,0:T(8,128)(2,1)S(1)}, u32[]{:S(2)}, u32[]{:S(2)}) collective-permute-start(bf16[128,1024]{1,0:T(8,128)(2,1)S(1)} %collective-permute-done.10.refs_5_), channel_id=1, source_target_pairs={{0,2},{2,0},{4,6},{6,4},{8,10},{10,8},{12,14},{14,12},{16,18},{18,... | collective-permute-start | bytes 786440 | tf_op jit(solution)/shard_map/ppermute | solution.py:46
  44.6 15.3 %collective-permute-start.7 = (bf16[128,1024]{1,0:T(8,128)(2,1)S(1)}, bf16[128,1024]{1,0:T(8,128)(2,1)S(1)}, u32[]{:S(2)}, u32[]{:S(2)}) collective-permute-start(bf16[128,1024]{1,0:T(8,128)(2,1)S(1)} %collective-permute-done.1.refs_3_), channel_id=1, source_target_pairs={{0,2},{2,0},{4,6},{6,4},{8,10},{10,8},{12,14},{14,12},{16,18},{18,... | collective-permute-start | bytes 786440 | tf_op jit(solution)/shard_map/ppermute | solution.py:46
  44.6 15.3 %collective-permute-start.8 = (bf16[128,1024]{1,0:T(8,128)(2,1)S(1)}, bf16[128,1024]{1,0:T(8,128)(2,1)S(1)}, u32[]{:S(2)}, u32[]{:S(2)}) collective-permute-start(bf16[128,1024]{1,0:T(8,128)(2,1)S(1)} %collective-permute-done.4.refs_4_), channel_id=1, source_target_pairs={{0,2},{2,0},{4,6},{6,4},{8,10},{10,8},{12,14},{14,12},{16,18},{18,... | collective-permute-start | bytes 786440 | tf_op jit(solution)/shard_map/ppermute | solution.py:46
  45.2 22.2 %collective-permute-start.3 = (bf16[128,1024]{1,0:T(8,128)(2,1)S(1)}, bf16[128,1024]{1,0:T(8,128)(2,1)S(1)}, u32[]{:S(2)}, u32[]{:S(2)}) collective-permute-start(bf16[128,1024]{1,0:T(8,128)(2,1)S(1)} %collective-permute-done.2.refs_3_), channel_id=1, source_target_pairs={{0,2},{2,0},{4,6},{6,4},{8,10},{10,8},{12,14},{14,12},{16,18},{18,... | collective-permute-start | bytes 786440 | tf_op jit(solution)/shard_map/ppermute | solution.py:46
  45.2 22.1 %collective-permute-start.6 = (bf16[128,1024]{1,0:T(8,128)(2,1)S(1)}, bf16[128,1024]{1,0:T(8,128)(2,1)S(1)}, u32[]{:S(2)}, u32[]{:S(2)}) collective-permute-start(bf16[128,1024]{1,0:T(8,128)(2,1)S(1)} %collective-permute-done.5.refs_4_), channel_id=1, source_target_pairs={{0,2},{2,0},{4,6},{6,4},{8,10},{10,8},{12,14},{14,12},{16,18},{18,... | collective-permute-start | bytes 786440 | tf_op jit(solution)/shard_map/ppermute | solution.py:46
  49.5 1.2 %copy-start = (bf16[128,3584]{1,0:T(8,128)(2,1)S(1)}, bf16[128,3584]{1,0:T(8,128)(2,1)}, u32[]{:S(2)}) copy-start(bf16[128,3584]{1,0:T(8,128)(2,1)} %refs_2_.1) | copy-start | bytes 2752516
  50.7 0.7 copy-start.3
  51.4 0.7 copy-start.8
  54.6 5.4 %copy-start.5 = (s32[4,16]{1,0:T(4,128)S(1)}, s32[4,16]{1,0:T(4,128)}, u32[]{:S(2)}) copy-start(s32[4,16]{1,0:T(4,128)} %constant.29.clone.refs_1_) | copy-start | bytes 772
  60.0 4.3 %copy-start.7 = (s32[2,16]{1,0:T(2,128)S(1)}, s32[2,16]{1,0:T(2,128)}, u32[]{:S(2)}) copy-start(s32[2,16]{1,0:T(2,128)} %constant.30.clone.refs_1_) | copy-start | bytes 388
  64.3 3.1 %copy-start.6 = (s32[2,16]{1,0:T(2,128)S(1)}, s32[2,16]{1,0:T(2,128)}, u32[]{:S(2)}) copy-start(s32[2,16]{1,0:T(2,128)} %constant.31.clone.refs_1_) | copy-start | bytes 388

commit v3 on v2

v3 whole, which is shorter than its diff:
```python
import functools

import jax
import jax.numpy as jnp
from jax import lax
from jax.experimental import pallas as pl
from jax.experimental.pallas import tpu as pltpu
from jax.sharding import PartitionSpec as P


HEADS = 28
KV_HEADS = 4
HEAD_DIM = 128
GROUP = HEADS // KV_HEADS
ROPE_BASE = 1000000.0
SCORE_SCALE = HEAD_DIM ** (-0.5) * 1.4426950408889634
MASKED = -65536.0
NOWHERE = 1 << 28
VMEM_LIMIT = 24 * 1024 * 1024
SLAB = 32


def cycles(wanted, count):
    pairs = dict(wanted)
    starts = [s for s in pairs if s not in set(pairs.values())]
    for start in starts:
        at = start
        while at in pairs:
            at = pairs[at]
        pairs[at] = start
    for i in range(count):
        pairs.setdefault(i, i)
    assert sorted(pairs.values()) == list(range(count))
    return sorted(pairs.items())


class Piece:
    def __init__(self, data, source):
        self.data, self.source = data, source

    def move(self, pairs):
        source = list(self.source)
        for s, t in pairs:
            source[t] = self.source[s]
        return Piece(lax.ppermute(self.data, "seq", pairs), source)


def rotated(x, cosine, sine):
    return x * cosine + pltpu.roll(x, HEAD_DIM // 2, 1) * sine


def in_hbm(x):
    return pltpu.with_memory_space_constraint(x, pltpu.HBM)


def lanes_iota(shape, dim):
    return lax.broadcasted_iota(jnp.int32, shape, dim)


def doc_starts(place, lengths_ref):
    start = jnp.zeros_like(place)
    end = 0
    for d in range(lengths_ref.shape[0]):
        end = end + lengths_ref[d]
        start = start + jnp.where(place >= end, lengths_ref[d], 0)
    return start


def prepare_kernel(freq_ref, lengths_hbm, k_hbm, v_hbm, kv_ref, cos_ref, sin_ref, lengths_ref, k_ref, sems):
    rows = k_ref.shape[0]
    width = KV_HEADS * HEAD_DIM
    copies = [
        pltpu.make_async_copy(lengths_hbm, lengths_ref, sems.at[0]),
        pltpu.make_async_copy(k_hbm, k_ref, sems.at[1]),
        pltpu.make_async_copy(v_hbm, kv_ref.at[:, pl.ds(width, width)], sems.at[2]),
    ]
    for copy in copies:
        copy.start()
    copies[0].wait()
    shape = (rows, HEAD_DIM)
    place = lax.axis_index("seq") * rows + lanes_iota(shape, 0)
    within = (place - doc_starts(place, lengths_ref)).astype(jnp.float32)
    angle = within * freq_ref[...]
    cosine = jnp.cos(angle)
    sine = jnp.sin(angle)
    sine = jnp.where(lanes_iota(shape, 1) < HEAD_DIM // 2, -sine, sine)
    cos_ref[...] = cosine
    sin_ref[...] = sine
    copies[1].wait()
    for g in range(KV_HEADS):
        cols = slice(g * HEAD_DIM, (g + 1) * HEAD_DIM)
        kv_ref[:, cols] = rotated(k_ref[:, cols].astype(jnp.float32), cosine, sine).astype(jnp.bfloat16)
    copies[2].wait()


def prepare(lengths, keys, values):
    rows = keys.shape[0]
    half = HEAD_DIM // 2
    lane = jnp.arange(HEAD_DIM, dtype=jnp.int32)[None, :]
    step = jnp.where(lane < half, lane, lane - half).astype(jnp.float32)
    freq = jnp.power(jnp.float32(ROPE_BASE), -2.0 * step / HEAD_DIM)
    vmem = pl.BlockSpec(memory_space=pltpu.VMEM)
    hbm = pl.BlockSpec(memory_space=pltpu.HBM)
    turn = jax.ShapeDtypeStruct((rows, HEAD_DIM), jnp.float32)
    return pl.pallas_call(
        prepare_kernel,
        out_shape=[jax.ShapeDtypeStruct((rows, 2 * KV_HEADS * HEAD_DIM), jnp.bfloat16), turn, turn],
        in_specs=[vmem, hbm, hbm, hbm],
        out_specs=[vmem] * 3,
        scratch_shapes=[
            pltpu.SMEM(lengths.shape, jnp.int32),
            pltpu.VMEM(keys.shape, keys.dtype),
            pltpu.SemaphoreType.DMA((3,)),
        ],
        cost_estimate=pl.CostEstimate(flops=10**6, bytes_accessed=6 * 10**5, transcendentals=0),
        compiler_params=pltpu.CompilerParams(vmem_limit_bytes=VMEM_LIMIT),
        name="prepare",
    )(freq, in_hbm(lengths), in_hbm(keys), in_hbm(values))


def attend_kernel(count, first, last, places, *refs):
    refs = list(refs)
    take = lambda n: [refs.pop(0) for _ in range(n)]
    if first:
        lengths_hbm, q_hbm, cos_ref, sin_ref = take(4)
        kv_refs = take(count)
        q_ref, max_out, sum_out, acc_out = take(4)
        all_bias = take(len(places))
        bias_ref = all_bias[0]
    else:
        q_ref, bias_ref = take(2)
        kv_refs = take(count)
        max_in, sum_in, acc_in = take(3)
        if last:
            (out_ref,) = take(1)
        else:
            max_out, sum_out, acc_out = take(3)
    score_ref, weight_ref = take(2)
    if last:
        sum_out, acc_out = take(2)
    if first:
        lengths_ref, q_raw, sems = take(3)

    rows = kv_refs[0].shape[0]
    width = KV_HEADS * HEAD_DIM
    tall = GROUP * rows
    square = (rows, rows)

    if first:
        copies = [
            pltpu.make_async_copy(lengths_hbm, lengths_ref, sems.at[0]),
            pltpu.make_async_copy(q_hbm, q_raw, sems.at[1]),
        ]
        for copy in copies:
            copy.start()
        copies[0].wait()
        me = lax.axis_index("seq")
        own = me * rows + lanes_iota((8, rows), 1)
        start = jnp.broadcast_to(doc_starts(own, lengths_ref)[:1], square)
        own = me * rows + lanes_iota(square, 1)
        for n, stage in enumerate(places):
            for b, bases in enumerate(stage):
                base = jnp.int32(NOWHERE)
                for i, value in enumerate(bases):
                    if value != NOWHERE:
                        base = jnp.where(me == i, value, base)
                place = base + lanes_iota(square, 0)
                allowed = (place >= start) & (place <= own)
                bias = jnp.where(allowed, 0.0, MASKED).astype(jnp.bfloat16)
                all_bias[n][b * rows:(b + 1) * rows, :] = bias
        copies[1].wait()
        cosine, sine = cos_ref[...], sin_ref[...]
        for h in range(HEADS):
            head = q_raw[:, h * HEAD_DIM:(h + 1) * HEAD_DIM].astype(jnp.float32)
            g, at = h // GROUP, h % GROUP * rows
            q_ref[g, at:at + rows] = rotated(head, cosine, sine).astype(jnp.bfloat16)

    unit = jnp.where(lanes_iota(square, 0) == lanes_iota(square, 1), 1.0, 0.0).astype(jnp.bfloat16)
    units = jnp.concatenate([unit] * GROUP, axis=0)

    def score(g):
        q = jnp.concatenate([q_ref[g], units], axis=1)
        k = jnp.concatenate([r[:, g * HEAD_DIM:(g + 1) * HEAD_DIM] for r in kv_refs], axis=0)
        k = jnp.concatenate([k, bias_ref[...]], axis=1)
        return lax.dot_general(q, k, (((1,), (1,)), ((), ())), preferred_element_type=jnp.float32)

    score_ref[0] = score(0)
    for g in range(KV_HEADS):
        slot = g % 2
        if g + 1 < KV_HEADS:
            score_ref[1 - slot] = score(g + 1)
        v = jnp.concatenate(
            [r[:, width + g * HEAD_DIM:width + (g + 1) * HEAD_DIM] for r in kv_refs], axis=0
        )
        for at in range(0, tall, SLAB):
            here = slice(at, at + SLAB)
            raw = score_ref[slot, here]
            top = jnp.max(raw, axis=1, keepdims=True) * SCORE_SCALE
            if first:
                top = jnp.broadcast_to(top, (SLAB, HEAD_DIM))
                total = None
            else:
                old = max_in[g, here]
                top = jnp.maximum(old, top)
                shrink = jnp.exp2(old - top)
                total = sum_in[g, here] * shrink
                acc_out[g, here] = acc_in[g, here] * shrink
            for b in range(count):
                cols = slice(b * rows, (b + 1) * rows)
                weight = jnp.exp2(raw[:, cols] * SCORE_SCALE - top)
                total = weight if total is None else total + weight
                weight_ref[slot, here, cols] = weight.astype(jnp.bfloat16)
            sum_out[g, here] = total
            if not last:
                max_out[g, here] = top
        mixed = jnp.dot(weight_ref[slot], v, preferred_element_type=jnp.float32)
        if first:
            acc_out[g] = mixed
        elif not last:
            acc_out[g] += mixed
        else:
            for h in range(GROUP):
                here = slice(h * rows, (h + 1) * rows)
                cols = slice((g * GROUP + h) * HEAD_DIM, (g * GROUP + h + 1) * HEAD_DIM)
                total = jnp.sum(sum_out[g, here], axis=1, keepdims=True)
                out_ref[:, cols] = ((acc_out[g, here] + mixed[here]) / total).astype(jnp.bfloat16)


def attend(pieces, bias=None, q=None, state=None, start=None, last=False):
    first = start is not None
    count = len(pieces)
    rows = pieces[0].data.shape[0]
    assert rows == HEAD_DIM
    stacked = (KV_HEADS, GROUP * rows, HEAD_DIM)
    vmem = pl.BlockSpec(memory_space=pltpu.VMEM)
    hbm = pl.BlockSpec(memory_space=pltpu.HBM)
    data = [p.data for p in pieces]
    held = [jax.ShapeDtypeStruct(stacked, jnp.float32)] * 3
    scratch = [
        pltpu.VMEM((2, GROUP * rows, count * rows), jnp.float32),
        pltpu.VMEM((2, GROUP * rows, count * rows), jnp.bfloat16),
    ]
    aliases = {}
    places = None
    if first:
        lengths, queries, cosine, sine, places = start
        args = [in_hbm(lengths), in_hbm(queries), cosine, sine] + data
        in_specs = [hbm, hbm] + [vmem] * (2 + count)
        out_shape = [jax.ShapeDtypeStruct(stacked, jnp.bfloat16)] + held
        out_shape += [jax.ShapeDtypeStruct((len(stage) * rows, rows), jnp.bfloat16) for stage in places]
        scratch += [
            pltpu.SMEM(lengths.shape, jnp.int32),
            pltpu.VMEM(queries.shape, queries.dtype),
            pltpu.SemaphoreType.DMA((2,)),
        ]
    else:
        args = [q, bias] + data + list(state)
        in_specs = [vmem] * len(args)
        if last:
            out_shape = [jax.ShapeDtypeStruct((rows, HEADS * HEAD_DIM), jnp.bfloat16)]
            scratch += [pltpu.VMEM(stacked, jnp.float32)] * 2
        else:
            out_shape = held
            aliases = {2 + count + n: n for n in range(3)}
    return pl.pallas_call(
        functools.partial(attend_kernel, count, first, last, places),
        out_shape=out_shape,
        in_specs=in_specs,
        out_specs=[vmem] * len(out_shape),
        scratch_shapes=scratch,
        input_output_aliases=aliases,
        cost_estimate=pl.CostEstimate(
            flops=4 * rows * HEADS * count * rows * HEAD_DIM,
            bytes_accessed=4 * 10**6,
            transcendentals=rows * HEADS * count * rows,
        ),
        compiler_params=pltpu.CompilerParams(vmem_limit_bytes=VMEM_LIMIT),
    )(*args)


def block_reach(count):
    return -(-5 * count // 8)


def chip_reach_of(count):
    return -(-block_reach(count) // 2)


def per_device(count, queries, keys, values, doc_lengths):
    rows = queries.shape[0]
    reach, chip_reach = block_reach(count), chip_reach_of(count)

    def closed(shift, keep):
        return cycles({i: i + shift for i in range(count) if i + shift < count and keep(i)}, count)

    sibling = [(i, i ^ 1) for i in range(count)]
    across = [(i, i ^ 2) for i in range(count)]
    own, cosine, sine = prepare(doc_lengths, keys, values)
    own = Piece(own, list(range(count)))
    stages = [[own, own.move(sibling)]]
    a, before = own, None
    half_reach = chip_reach // 2
    for s in range(1, half_reach + 1):
        b = a.move(across)
        a = a.move(closed(4, lambda i: i >= 4 * (s - 1)))
        stages.append([a, b, a.move(sibling), b.move(sibling)])
        before = b
    if chip_reach % 2:
        near = 4 * half_reach
        c = before.move(closed(4, lambda i: not i & 2 and i >= near - 4))
        a = a.move(closed(2, lambda i: i >= near))
        stages += [[a, c], [a.move(sibling), c.move(sibling)]]
    else:
        b = a.move(across)
        stages += [[b], [b.move(sibling)]]

    seen = [set() for _ in range(count)]
    places = []
    for pieces in stages:
        table = [[NOWHERE] * count for _ in pieces]
        for b, piece in enumerate(pieces):
            for i in range(count):
                j = piece.source[i]
                if i - reach <= j <= i and j not in seen[i]:
                    seen[i].add(j)
                    table[b][i] = j * rows
        places.append(table)
    for i in range(count):
        assert seen[i] == set(range(max(0, i - reach), i + 1))

    for n, pieces in enumerate(stages):
        if n == 0:
            out = attend(pieces, start=(doc_lengths, queries, cosine, sine, places))
            q, state, bias = out[0], out[1:4], out[4:]
        else:
            state = attend(pieces, bias[n], q, state, last=n == len(stages) - 1)
    return state[0]


def solution(mesh):
    count = mesh.shape["seq"]

    def body(*args):
        return per_device(count, *args)

    return jax.shard_map(
        body,
        mesh=mesh,
        in_specs=(
            P(("grp", "seq"), None),
            P(("grp", "seq"), None),
            P(("grp", "seq"), None),
            P("grp"),
        ),
        out_specs=P(("grp", "seq"), None),
        check_vma=False,
    )
```

time: 71.5 us -> 53.3 us (0.75)
  local copies, waits for them, and re-layouts: 5.95 us -> 0 us
  other arithmetic: 5.5 us -> 0.01 us
  between operations: 5.26 us -> 0.11 us
  Pallas kernels: 19 us -> 17.6 us
    convert_element_type x1 -> x0, other arithmetic: 5.08 us -> none  [turns(): angle = (place - start).astype(jnp.float32)[:, None] * freq[None, :]]
    unnamed x18 -> x0, local copies, waits for them, and re-layouts: 4.31 us -> none
    slice x1 -> x0, local copies, waits for them, and re-layouts: 1.64 us -> none  [turns(): end = end + doc_lengths[d]]
    pallas_call x6, Pallas kernels: 19 us -> 17.6 us  [the longest x5 16.5 us: attend(): pl.pallas_call(functools.partial(attend_kernel, count, first, last, place...]
  transfers between devices with their start and end apart: 13 -> 13, of which waited for: 3 -> 3; matrix products, arithmetic and copies ran while one was open for 0% -> 0% of each run, Pallas kernels for 21% -> 26%
where the time goes in v3:
time: 53.3 us; the launch traced here: 53.1 us
  starting transfers between devices  22.3 us (42%)
  Pallas kernels  17.6 us (33%)
  waiting for transfers between devices  13 us (24%)
    ppermute x13, starting transfers between devices, move(): return Piece(lax.ppermute(self.data, 'seq', pairs), source)  22.3 us
    pallas_call x5, Pallas kernels, attend(): pl.pallas_call(functools.partial(attend_kernel, count, first, last, place...  16.5 us
    ppermute x13, waiting for transfers between devices, move(): return Piece(lax.ppermute(self.data, 'seq', pairs), source)  13 us
    pallas_call x1, Pallas kernels, prepare(): pl.pallas_call(prepare_kernel, out_shape=[jax.ShapeDtypeStruct((rows, 2 *...  1.13 us
  transfers between devices with their start and end apart: 13, of which 3 were waited for; matrix products, arithmetic and copies ran while one was open for 0% of the time, Pallas kernels for 26%

profile of v3, /device:TPU:19, one launch (start us, length us, event | category | flops | bytes accessed | tf_op | source)
XLA Modules:
  0.0 53.1 jit_solution(2320590935893556822)
XLA Ops:
  0.0 1.1 %prepare.1 = (bf16[128,1024]{1,0:T(8,128)(2,1)S(1)}, f32[128,128]{1,0:T(8,128)S(1)}, f32[128,128]{1,0:T(8,128)S(1)}) custom-call(f32[1,128]{1,0:T(1,128)S(1)} %fusion.2.freq_ref, s32[8]{0:T(128)} %refs_0_.1, bf16[128,512]{1,0:T(8,128)(2,1)} %k_hbm.1, bf16[128,512]{1,0:T(8,128)(2,1)} %v_hbm.1), custom_call_target="tpu_custom_call" | custom-call | flops 1000000 | bytes 600000 | tf_op jit(solution)/shard_map/prepare/pallas_call | solution.py:105
  1.1 1.3 %collective-permute-start.1 = (bf16[128,1024]{1,0:T(8,128)(2,1)S(1)}, bf16[128,1024]{1,0:T(8,128)(2,1)S(1)}, u32[]{:S(2)}, u32[]{:S(2)}) collective-permute-start(bf16[128,1024]{1,0:T(8,128)(2,1)S(1)} %get-tuple-element.27.refs_4_), channel_id=1, source_target_pairs={{0,8},{2,10},{4,12},{6,14},{8,16},{10,18},{12,20},{14,22},{16,24},... | collective-permute-start | bytes 786440 | tf_op jit(solution)/shard_map/ppermute | solution.py:45
  2.5 5.9 %collective-permute-done.1.refs_2_ = bf16[128,1024]{1,0:T(8,128)(2,1)S(1)} collective-permute-done((bf16[128,1024]{1,0:T(8,128)(2,1)S(1)}, bf16[128,1024]{1,0:T(8,128)(2,1)S(1)}, u32[]{:S(2)}, u32[]{:S(2)}) %collective-permute-start.1) | collective-permute-done | bytes 262176 | tf_op jit(solution)/shard_map/ppermute | solution.py:45
  8.4 3.2 %collective-permute-start.2 = (bf16[128,1024]{1,0:T(8,128)(2,1)S(1)}, bf16[128,1024]{1,0:T(8,128)(2,1)S(1)}, u32[]{:S(2)}, u32[]{:S(2)}) collective-permute-start(bf16[128,1024]{1,0:T(8,128)(2,1)S(1)} %collective-permute-done.1.refs_2_), channel_id=1, source_target_pairs={{0,0},{2,2},{4,4},{6,6},{8,16},{10,18},{12,20},{14,22},{16,24},{18... | collective-permute-start | bytes 786440 | tf_op jit(solution)/shard_map/ppermute | solution.py:45
  11.6 1.3 %collective-permute-start.5 = (bf16[128,1024]{1,0:T(8,128)(2,1)S(1)}, bf16[128,1024]{1,0:T(8,128)(2,1)S(1)}, u32[]{:S(2)}, u32[]{:S(2)}) collective-permute-start(bf16[128,1024]{1,0:T(8,128)(2,1)S(1)} %collective-permute-done.1.refs_2_), channel_id=1, source_target_pairs={{0,4},{2,6},{4,0},{6,2},{8,12},{10,14},{12,8},{14,10},{16,20},{18,... | collective-permute-start | bytes 786440 | tf_op jit(solution)/shard_map/ppermute | solution.py:45
  12.9 0.2 collective-permute-start.10
  13.1 2.4 %collective-permute-start = (bf16[128,1024]{1,0:T(8,128)(2,1)S(1)}, bf16[128,1024]{1,0:T(8,128)(2,1)S(1)}, u32[]{:S(2)}, u32[]{:S(2)}) collective-permute-start(bf16[128,1024]{1,0:T(8,128)(2,1)S(1)} %get-tuple-element.27.refs_4_), channel_id=1, source_target_pairs={{0,2},{2,0},{4,6},{6,4},{8,10},{10,8},{12,14},{14,12},{16,18},{18,... | collective-permute-start | bytes 786440 | tf_op jit(solution)/shard_map/ppermute | solution.py:45
  15.5 0.0 collective-permute-start.11
  15.5 1.1 %collective-permute-done.2.refs_2_ = bf16[128,1024]{1,0:T(8,128)(2,1)S(1)} collective-permute-done((bf16[128,1024]{1,0:T(8,128)(2,1)S(1)}, bf16[128,1024]{1,0:T(8,128)(2,1)S(1)}, u32[]{:S(2)}, u32[]{:S(2)}) %collective-permute-start.2) | collective-permute-done | bytes 262176 | tf_op jit(solution)/shard_map/ppermute | solution.py:45
  16.6 3.1 %collective-permute-start.3 = (bf16[128,1024]{1,0:T(8,128)(2,1)S(1)}, bf16[128,1024]{1,0:T(8,128)(2,1)S(1)}, u32[]{:S(2)}, u32[]{:S(2)}) collective-permute-start(bf16[128,1024]{1,0:T(8,128)(2,1)S(1)} %collective-permute-done.2.refs_2_), channel_id=1, source_target_pairs={{0,0},{2,2},{4,4},{6,6},{8,8},{10,10},{12,12},{14,14},{16,20},{18,... | collective-permute-start | bytes 786440 | tf_op jit(solution)/shard_map/ppermute | solution.py:45
  19.8 0.0 collective-permute-done.5.refs_3_
  19.8 3.2 %collective-permute-start.6 = (bf16[128,1024]{1,0:T(8,128)(2,1)S(1)}, bf16[128,1024]{1,0:T(8,128)(2,1)S(1)}, u32[]{:S(2)}, u32[]{:S(2)}) collective-permute-start(bf16[128,1024]{1,0:T(8,128)(2,1)S(1)} %collective-permute-done.5.refs_3_), channel_id=1, source_target_pairs={{0,0},{2,2},{4,4},{6,6},{8,16},{10,18},{12,12},{14,14},{16,24},{18... | collective-permute-start | bytes 786440 | tf_op jit(solution)/shard_map/ppermute | solution.py:45
  23.0 6.0 %collective-permute-done.10.refs_3_ = bf16[128,1024]{1,0:T(8,128)(2,1)S(1)} collective-permute-done((bf16[128,1024]{1,0:T(8,128)(2,1)S(1)}, bf16[128,1024]{1,0:T(8,128)(2,1)S(1)}, u32[]{:S(2)}, u32[]{:S(2)}) %collective-permute-start.10) | collective-permute-done | bytes 262176 | tf_op jit(solution)/shard_map/ppermute | solution.py:45
  28.9 2.7 %collective-permute-start.12 = (bf16[128,1024]{1,0:T(8,128)(2,1)S(1)}, bf16[128,1024]{1,0:T(8,128)(2,1)S(1)}, u32[]{:S(2)}, u32[]{:S(2)}) collective-permute-start(bf16[128,1024]{1,0:T(8,128)(2,1)S(1)} %collective-permute-done.10.refs_3_), channel_id=1, source_target_pairs={{0,2},{2,0},{4,6},{6,4},{8,10},{10,8},{12,14},{14,12},{16,18},{18,... | collective-permute-start | bytes 786440 | tf_op jit(solution)/shard_map/ppermute | solution.py:45
  31.6 0.0 collective-permute-done.refs_5_
  31.6 0.0 collective-permute-start.8
  31.6 0.0 collective-permute-done.11.refs_4_
  31.6 0.5 collective-permute-start.9
  32.1 0.0 collective-permute-done.3.refs_2_
  32.1 0.1 collective-permute-start.4
  32.2 0.0 collective-permute-done.6.refs_3_
  32.2 4.3 %collective-permute-start.7 = (bf16[128,1024]{1,0:T(8,128)(2,1)S(1)}, bf16[128,1024]{1,0:T(8,128)(2,1)S(1)}, u32[]{:S(2)}, u32[]{:S(2)}) collective-permute-start(bf16[128,1024]{1,0:T(8,128)(2,1)S(1)} %collective-permute-done.6.refs_3_), channel_id=1, source_target_pairs={{0,2},{2,0},{4,6},{6,4},{8,10},{10,8},{12,14},{14,12},{16,18},{18,... | collective-permute-start | bytes 786440 | tf_op jit(solution)/shard_map/ppermute | solution.py:45
  36.5 4.2 %shard_map.46 = (bf16[4,896,128]{2,1,0:T(8,128)(2,1)S(1)}, f32[4,896,128]{2,1,0:T(8,128)S(1)}, f32[4,896,128]{2,1,0:T(8,128)S(1)}, f32[4,896,128]{2,1,0:T(8,128)...) custom-call(s32[8]{0:T(128)} %refs_0_.1, ...), custom_call_target="tpu_custom_call" | custom-call | flops 469762048 | bytes 4000000 | tf_op jit(solution)/shard_map/pallas_call | solution.py:265
  40.7 0.0 collective-permute-done.12.refs_5_
  40.8 3.5 %shard_map.47 = (f32[4,896,128]{2,1,0:T(8,128)S(1)}, f32[4,896,128]{2,1,0:T(8,128)S(1)}, f32[4,896,128]{2,1,0:T(8,128)S(1)}) custom-call(bf16[4,896,128]{2,1,0:T(8,128)(2,1)S(1)} %get-tuple-element.28.refs_0_, bf16[512,128]{1,0:T(8,128)(2,1)S(1)} %get-tuple-element.32.refs_1_, ...), custom_call_target="tpu_custom_call", output_to_operand_aliasing={{0}: (6, {}), {1}: (7, {}), {2}: (8, {})} | custom-call | flops 939524096 | bytes 4000000 | tf_op jit(solution)/shard_map/pallas_call | solution.py:265
  44.3 0.0 collective-permute-done.8.refs_4_
  44.3 0.0 collective-permute-done.9.refs_5_
  44.3 3.5 %shard_map.48 = (f32[4,896,128]{2,1,0:T(8,128)S(1)}, f32[4,896,128]{2,1,0:T(8,128)S(1)}, f32[4,896,128]{2,1,0:T(8,128)S(1)}) custom-call(bf16[4,896,128]{2,1,0:T(8,128)(2,1)S(1)} %get-tuple-element.28.refs_0_, bf16[512,128]{1,0:T(8,128)(2,1)S(1)} %get-tuple-element.31.refs_1_, ...), custom_call_target="tpu_custom_call", output_to_operand_aliasing={{0}: (6, {}), {1}: (7, {}), {2}: (8, {})} | custom-call | flops 939524096 | bytes 4000000 | tf_op jit(solution)/shard_map/pallas_call | solution.py:265
  47.8 2.3 %shard_map.49 = (f32[4,896,128]{2,1,0:T(8,128)S(1)}, f32[4,896,128]{2,1,0:T(8,128)S(1)}, f32[4,896,128]{2,1,0:T(8,128)S(1)}) custom-call(bf16[4,896,128]{2,1,0:T(8,128)(2,1)S(1)} %get-tuple-element.28.refs_0_, bf16[256,128]{1,0:T(8,128)(2,1)S(1)} %get-tuple-element.30.refs_1_, ...), custom_call_target="tpu_custom_call", output_to_operand_aliasing={{0}: (4, {}), {1}: (5, {}), {2}: (6, {})} | custom-call | flops 469762048 | bytes 4000000 | tf_op jit(solution)/shard_map/pallas_call | solution.py:265
  50.2 0.0 collective-permute-done.4.refs_2_
  50.2 0.0 collective-permute-done.7.refs_3_
  50.2 2.9 %shard_map.50 = bf16[128,3584]{1,0:T(8,128)(2,1)} custom-call(bf16[4,896,128]{2,1,0:T(8,128)(2,1)S(1)} %get-tuple-element.28.refs_0_, bf16[256,128]{1,0:T(8,128)(2,1)S(1)} %get-tuple-element.29.refs_1_, bf16[128,1024]{1,0:T(8,128)(2,1)S(1)} %collective-permute-done.4.refs_2_, bf16[128,1024]{1,0:T(8,128)(2,1)S(1)} %collective-permute-done.7.refs_3_, ...), custom_call_target="tpu_custom_call" | custom-call | flops 469762048 | bytes 4000000 | tf_op jit(solution)/shard_map/pallas_call | solution.py:265
  (1 shorter events, 0.0 us)
Async XLA Ops:
  1.1 7.2 %collective-permute-start.1 = (bf16[128,1024]{1,0:T(8,128)(2,1)S(1)}, bf16[128,1024]{1,0:T(8,128)(2,1)S(1)}, u32[]{:S(2)}, u32[]{:S(2)}) collective-permute-start(bf16[128,1024]{1,0:T(8,128)(2,1)S(1)} %get-tuple-element.27.refs_4_), channel_id=1, source_target_pairs={{0,8},{2,10},{4,12},{6,14},{8,16},{10,18},{12,20},{14,22},{16,24},... | collective-permute-start | bytes 786440 | tf_op jit(solution)/shard_map/ppermute | solution.py:45
  8.4 8.2 %collective-permute-start.2 = (bf16[128,1024]{1,0:T(8,128)(2,1)S(1)}, bf16[128,1024]{1,0:T(8,128)(2,1)S(1)}, u32[]{:S(2)}, u32[]{:S(2)}) collective-permute-start(bf16[128,1024]{1,0:T(8,128)(2,1)S(1)} %collective-permute-done.1.refs_2_), channel_id=1, source_target_pairs={{0,0},{2,2},{4,4},{6,6},{8,16},{10,18},{12,20},{14,22},{16,24},{18... | collective-permute-start | bytes 786440 | tf_op jit(solution)/shard_map/ppermute | solution.py:45
  11.6 8.2 %collective-permute-start.5 = (bf16[128,1024]{1,0:T(8,128)(2,1)S(1)}, bf16[128,1024]{1,0:T(8,128)(2,1)S(1)}, u32[]{:S(2)}, u32[]{:S(2)}) collective-permute-start(bf16[128,1024]{1,0:T(8,128)(2,1)S(1)} %collective-permute-done.1.refs_2_), channel_id=1, source_target_pairs={{0,4},{2,6},{4,0},{6,2},{8,12},{10,14},{12,8},{14,10},{16,20},{18,... | collective-permute-start | bytes 786440 | tf_op jit(solution)/shard_map/ppermute | solution.py:45
  12.9 16.1 %collective-permute-start.10 = (bf16[128,1024]{1,0:T(8,128)(2,1)S(1)}, bf16[128,1024]{1,0:T(8,128)(2,1)S(1)}, u32[]{:S(2)}, u32[]{:S(2)}) collective-permute-start(bf16[128,1024]{1,0:T(8,128)(2,1)S(1)} %get-tuple-element.27.refs_4_), channel_id=1, source_target_pairs={{0,4},{2,6},{4,0},{6,2},{8,12},{10,14},{12,8},{14,10},{16,20},{18,... | collective-permute-start | bytes 786440 | tf_op jit(solution)/shard_map/ppermute | solution.py:45
  13.1 18.5 %collective-permute-start = (bf16[128,1024]{1,0:T(8,128)(2,1)S(1)}, bf16[128,1024]{1,0:T(8,128)(2,1)S(1)}, u32[]{:S(2)}, u32[]{:S(2)}) collective-permute-start(bf16[128,1024]{1,0:T(8,128)(2,1)S(1)} %get-tuple-element.27.refs_4_), channel_id=1, source_target_pairs={{0,2},{2,0},{4,6},{6,4},{8,10},{10,8},{12,14},{14,12},{16,18},{18,... | collective-permute-start | bytes 786440 | tf_op jit(solution)/shard_map/ppermute | solution.py:45
  15.5 16.1 %collective-permute-start.11 = (bf16[128,1024]{1,0:T(8,128)(2,1)S(1)}, bf16[128,1024]{1,0:T(8,128)(2,1)S(1)}, u32[]{:S(2)}, u32[]{:S(2)}) collective-permute-start(bf16[128,1024]{1,0:T(8,128)(2,1)S(1)} %collective-permute-done.1.refs_2_), channel_id=1, source_target_pairs={{0,2},{2,0},{4,6},{6,4},{8,10},{10,8},{12,14},{14,12},{16,18},{18,... | collective-permute-start | bytes 786440 | tf_op jit(solution)/shard_map/ppermute | solution.py:45
  16.6 15.5 %collective-permute-start.3 = (bf16[128,1024]{1,0:T(8,128)(2,1)S(1)}, bf16[128,1024]{1,0:T(8,128)(2,1)S(1)}, u32[]{:S(2)}, u32[]{:S(2)}) collective-permute-start(bf16[128,1024]{1,0:T(8,128)(2,1)S(1)} %collective-permute-done.2.refs_2_), channel_id=1, source_target_pairs={{0,0},{2,2},{4,4},{6,6},{8,8},{10,10},{12,12},{14,14},{16,20},{18,... | collective-permute-start | bytes 786440 | tf_op jit(solution)/shard_map/ppermute | solution.py:45
  19.8 12.4 %collective-permute-start.6 = (bf16[128,1024]{1,0:T(8,128)(2,1)S(1)}, bf16[128,1024]{1,0:T(8,128)(2,1)S(1)}, u32[]{:S(2)}, u32[]{:S(2)}) collective-permute-start(bf16[128,1024]{1,0:T(8,128)(2,1)S(1)} %collective-permute-done.5.refs_3_), channel_id=1, source_target_pairs={{0,0},{2,2},{4,4},{6,6},{8,16},{10,18},{12,12},{14,14},{16,24},{18... | collective-permute-start | bytes 786440 | tf_op jit(solution)/shard_map/ppermute | solution.py:45
  28.9 11.8 %collective-permute-start.12 = (bf16[128,1024]{1,0:T(8,128)(2,1)S(1)}, bf16[128,1024]{1,0:T(8,128)(2,1)S(1)}, u32[]{:S(2)}, u32[]{:S(2)}) collective-permute-start(bf16[128,1024]{1,0:T(8,128)(2,1)S(1)} %collective-permute-done.10.refs_3_), channel_id=1, source_target_pairs={{0,2},{2,0},{4,6},{6,4},{8,10},{10,8},{12,14},{14,12},{16,18},{18,... | collective-permute-start | bytes 786440 | tf_op jit(solution)/shard_map/ppermute | solution.py:45
  31.6 12.7 %collective-permute-start.8 = (bf16[128,1024]{1,0:T(8,128)(2,1)S(1)}, bf16[128,1024]{1,0:T(8,128)(2,1)S(1)}, u32[]{:S(2)}, u32[]{:S(2)}) collective-permute-start(bf16[128,1024]{1,0:T(8,128)(2,1)S(1)} %collective-permute-done.2.refs_2_), channel_id=1, source_target_pairs={{0,2},{2,0},{4,6},{6,4},{8,10},{10,8},{12,14},{14,12},{16,18},{18,... | collective-permute-start | bytes 786440 | tf_op jit(solution)/shard_map/ppermute | solution.py:45
  31.6 12.7 %collective-permute-start.9 = (bf16[128,1024]{1,0:T(8,128)(2,1)S(1)}, bf16[128,1024]{1,0:T(8,128)(2,1)S(1)}, u32[]{:S(2)}, u32[]{:S(2)}) collective-permute-start(bf16[128,1024]{1,0:T(8,128)(2,1)S(1)} %collective-permute-done.5.refs_3_), channel_id=1, source_target_pairs={{0,2},{2,0},{4,6},{6,4},{8,10},{10,8},{12,14},{14,12},{16,18},{18,... | collective-permute-start | bytes 786440 | tf_op jit(solution)/shard_map/ppermute | solution.py:45
  32.1 18.0 %collective-permute-start.4 = (bf16[128,1024]{1,0:T(8,128)(2,1)S(1)}, bf16[128,1024]{1,0:T(8,128)(2,1)S(1)}, u32[]{:S(2)}, u32[]{:S(2)}) collective-permute-start(bf16[128,1024]{1,0:T(8,128)(2,1)S(1)} %collective-permute-done.3.refs_2_), channel_id=1, source_target_pairs={{0,2},{2,0},{4,6},{6,4},{8,10},{10,8},{12,14},{14,12},{16,18},{18,... | collective-permute-start | bytes 786440 | tf_op jit(solution)/shard_map/ppermute | solution.py:45
  32.2 18.0 %collective-permute-start.7 = (bf16[128,1024]{1,0:T(8,128)(2,1)S(1)}, bf16[128,1024]{1,0:T(8,128)(2,1)S(1)}, u32[]{:S(2)}, u32[]{:S(2)}) collective-permute-start(bf16[128,1024]{1,0:T(8,128)(2,1)S(1)} %collective-permute-done.6.refs_3_), channel_id=1, source_target_pairs={{0,2},{2,0},{4,6},{6,4},{8,10},{10,8},{12,14},{14,12},{16,18},{18,... | collective-permute-start | bytes 786440 | tf_op jit(solution)/shard_map/ppermute | solution.py:45

commit v4 on v3

v4 whole, which is shorter than its diff:
```python
import functools

import jax
import jax.numpy as jnp
from jax import lax
from jax.experimental import pallas as pl
from jax.experimental.pallas import tpu as pltpu
from jax.sharding import PartitionSpec as P


HEADS = 28
KV_HEADS = 4
HEAD_DIM = 128
GROUP = HEADS // KV_HEADS
ROPE_BASE = 1000000.0
SCORE_SCALE = HEAD_DIM ** (-0.5) * 1.4426950408889634
MASKED = -16384.0
NOWHERE = 1 << 28
VMEM_LIMIT = 24 * 1024 * 1024
SLAB = 32


def cycles(wanted, count):
    pairs = dict(wanted)
    starts = [s for s in pairs if s not in set(pairs.values())]
    for start in starts:
        at = start
        while at in pairs:
            at = pairs[at]
        pairs[at] = start
    for i in range(count):
        pairs.setdefault(i, i)
    assert sorted(pairs.values()) == list(range(count))
    return sorted(pairs.items())


class Piece:
    def __init__(self, data, source):
        self.data, self.source = data, source

    def move(self, pairs):
        source = list(self.source)
        for s, t in pairs:
            source[t] = self.source[s]
        return Piece(lax.ppermute(self.data, "seq", pairs), source)


def rotated(x, cosine, sine):
    return x * cosine + pltpu.roll(x, HEAD_DIM // 2, 1) * sine


def in_hbm(x):
    return pltpu.with_memory_space_constraint(x, pltpu.HBM)


def lanes_iota(shape, dim):
    return lax.broadcasted_iota(jnp.int32, shape, dim)


def doc_starts(place, lengths_ref):
    start = jnp.zeros_like(place)
    end = 0
    for d in range(lengths_ref.shape[0]):
        end = end + lengths_ref[d]
        start = start + jnp.where(place >= end, lengths_ref[d], 0)
    return start


def prepare_kernel(freq_ref, lengths_hbm, k_hbm, v_hbm, kv_ref, cos_ref, sin_ref, lengths_ref, k_ref, sems):
    rows = k_ref.shape[0]
    width = KV_HEADS * HEAD_DIM
    copies = [
        pltpu.make_async_copy(lengths_hbm, lengths_ref, sems.at[0]),
        pltpu.make_async_copy(k_hbm, k_ref, sems.at[1]),
        pltpu.make_async_copy(v_hbm, kv_ref.at[:, pl.ds(width, width)], sems.at[2]),
    ]
    for copy in copies:
        copy.start()
    copies[0].wait()
    shape = (rows, HEAD_DIM)
    place = lax.axis_index("seq") * rows + lanes_iota(shape, 0)
    within = (place - doc_starts(place, lengths_ref)).astype(jnp.float32)
    angle = within * freq_ref[...]
    cosine = jnp.cos(angle)
    sine = jnp.sin(angle)
    sine = jnp.where(lanes_iota(shape, 1) < HEAD_DIM // 2, -sine, sine)
    cos_ref[...] = cosine
    sin_ref[...] = sine
    copies[1].wait()
    for g in range(KV_HEADS):
        cols = slice(g * HEAD_DIM, (g + 1) * HEAD_DIM)
        kv_ref[:, cols] = rotated(k_ref[:, cols].astype(jnp.float32), cosine, sine).astype(jnp.bfloat16)
    copies[2].wait()


def prepare(lengths, keys, values):
    rows = keys.shape[0]
    half = HEAD_DIM // 2
    lane = jnp.arange(HEAD_DIM, dtype=jnp.int32)[None, :]
    step = jnp.where(lane < half, lane, lane - half).astype(jnp.float32)
    freq = jnp.power(jnp.float32(ROPE_BASE), -2.0 * step / HEAD_DIM)
    vmem = pl.BlockSpec(memory_space=pltpu.VMEM)
    hbm = pl.BlockSpec(memory_space=pltpu.HBM)
    turn = jax.ShapeDtypeStruct((rows, HEAD_DIM), jnp.float32)
    return pl.pallas_call(
        prepare_kernel,
        out_shape=[jax.ShapeDtypeStruct((rows, 2 * KV_HEADS * HEAD_DIM), jnp.bfloat16), turn, turn],
        in_specs=[vmem, hbm, hbm, hbm],
        out_specs=[vmem] * 3,
        scratch_shapes=[
            pltpu.SMEM(lengths.shape, jnp.int32),
            pltpu.VMEM(keys.shape, keys.dtype),
            pltpu.SemaphoreType.DMA((3,)),
        ],
        cost_estimate=pl.CostEstimate(flops=10**6, bytes_accessed=6 * 10**5, transcendentals=0),
        compiler_params=pltpu.CompilerParams(vmem_limit_bytes=VMEM_LIMIT),
        name="prepare",
    )(freq, in_hbm(lengths), in_hbm(keys), in_hbm(values))


def turn_kernel(places, docs, lengths_hbm, q_hbm, cos_ref, sin_ref, *refs):
    q_ref, *rest = refs
    mask_refs, (lengths_ref, q_raw, sems) = rest[:-3], rest[-3:]
    rows = q_raw.shape[0]
    copies = [
        pltpu.make_async_copy(lengths_hbm, lengths_ref, sems.at[0]),
        pltpu.make_async_copy(q_hbm, q_raw, sems.at[1]),
    ]
    for copy in copies:
        copy.start()
    copies[0].wait()
    me = lax.axis_index("seq")
    square = (rows, HEAD_DIM)
    row, lane = lanes_iota(square, 0), lanes_iota(square, 1)
    first = jnp.full((8, HEAD_DIM), NOWHERE, jnp.int32)
    after = first
    end = 0
    for d in range(docs):
        here = lanes_iota((8, HEAD_DIM), 1) == d
        first = jnp.where(here, end, first)
        end = end + lengths_ref[d]
        after = jnp.where(here, end, after)
    first = jnp.broadcast_to(first[:1], square)
    after = jnp.broadcast_to(after[:1], square)
    for n, stage in enumerate(places):
        for b, bases in enumerate(stage):
            place = block_base(bases, me) + row
            member = (place >= first) & (place < after)
            mask_refs[n][b * rows:(b + 1) * rows, :] = jnp.where(member, 0.0, MASKED).astype(jnp.bfloat16)
    place = me * rows + row
    own_doc = jnp.where((place >= first) & (place < after), 1.0, 0.0)
    copies[1].wait()
    cosine, sine = cos_ref[...], sin_ref[...]
    for h in range(HEADS):
        head = q_raw[:, h * HEAD_DIM:(h + 1) * HEAD_DIM].astype(jnp.float32)
        g, at = h // GROUP, h % GROUP * rows
        turned = rotated(head, cosine, sine).astype(jnp.bfloat16).astype(jnp.float32) * SCORE_SCALE
        coarse = turned.astype(jnp.bfloat16)
        fine = turned - coarse.astype(jnp.float32)
        q_ref[g, at:at + rows, :HEAD_DIM] = coarse
        q_ref[g, at:at + rows, HEAD_DIM:] = jnp.where(lane < docs, own_doc, fine).astype(jnp.bfloat16)


def block_base(bases, me):
    base = jnp.int32(NOWHERE)
    for i, value in enumerate(bases):
        if value != NOWHERE:
            base = jnp.where(me == i, value, base)
    return base


def turn_queries(lengths, queries, cosine, sine, places):
    rows = queries.shape[0]
    assert rows == HEAD_DIM
    vmem = pl.BlockSpec(memory_space=pltpu.VMEM)
    hbm = pl.BlockSpec(memory_space=pltpu.HBM)
    out_shape = [jax.ShapeDtypeStruct((KV_HEADS, GROUP * rows, 2 * HEAD_DIM), jnp.bfloat16)]
    out_shape += [jax.ShapeDtypeStruct((len(stage) * rows, HEAD_DIM), jnp.bfloat16) for stage in places]
    return pl.pallas_call(
        functools.partial(turn_kernel, places, lengths.shape[0]),
        out_shape=out_shape,
        in_specs=[hbm, hbm, vmem, vmem],
        out_specs=[vmem] * len(out_shape),
        scratch_shapes=[
            pltpu.SMEM(lengths.shape, jnp.int32),
            pltpu.VMEM(queries.shape, queries.dtype),
            pltpu.SemaphoreType.DMA((2,)),
        ],
        cost_estimate=pl.CostEstimate(flops=10**8, bytes_accessed=4 * 10**6, transcendentals=0),
        compiler_params=pltpu.CompilerParams(vmem_limit_bytes=VMEM_LIMIT),
        name="turn_queries",
    )(in_hbm(lengths), in_hbm(queries), cosine, sine)


def attend_kernel(count, docs, first, last, users, *refs):
    refs = list(refs)
    take = lambda n: [refs.pop(0) for _ in range(n)]
    q_ref, mask_ref = take(2)
    kv_refs = take(count)
    if not first:
        max_in, sum_in, acc_in = take(3)
    if last:
        (out_ref,) = take(1)
    else:
        max_out, sum_out, acc_out = take(3)
    score_ref, shrink_ref = take(2)

    rows = kv_refs[0].shape[0]
    width = KV_HEADS * HEAD_DIM
    tall = GROUP * rows
    key_lane = lanes_iota((count * rows, HEAD_DIM), 1)
    ones = jnp.ones((count * rows, HEAD_DIM), jnp.bfloat16)

    def body():
        def score(g):
            k = jnp.concatenate([r[:, g * HEAD_DIM:(g + 1) * HEAD_DIM] for r in kv_refs], axis=0)
            k = jnp.concatenate([k, jnp.where(key_lane < docs, mask_ref[...], k)], axis=1)
            return lax.dot_general(q_ref[g], k, (((1,), (1,)), ((), ())), preferred_element_type=jnp.float32)

        score_ref[0] = score(0)
        for g in range(KV_HEADS):
            slot = g % 2
            if g + 1 < KV_HEADS:
                score_ref[1 - slot] = score(g + 1)
            v = jnp.concatenate(
                [r[:, width + g * HEAD_DIM:width + (g + 1) * HEAD_DIM] for r in kv_refs], axis=0
            )
            weights = []
            for at in range(0, tall, SLAB):
                here = slice(at, at + SLAB)
                scores = score_ref[slot, here]
                if first:
                    shape = (SLAB, count * rows)
                    after = lanes_iota(shape, 1) - lanes_iota(shape, 0) > at % rows
                    after &= lanes_iota(shape, 1) < rows
                    scores = jnp.where(after, MASKED, scores)
                    top = jnp.max(scores, axis=1, keepdims=True)
                    top = jnp.broadcast_to(top, (SLAB, HEAD_DIM))
                else:
                    old = max_in[g, here]
                    top = jnp.maximum(old, jnp.max(scores, axis=1, keepdims=True))
                    shrink_ref[slot, here] = jnp.exp2(old - top)
                if not last:
                    max_out[g, here] = top
                parts = [
                    jnp.exp2(scores[:, b * rows:(b + 1) * rows] - top).astype(jnp.bfloat16)
                    for b in range(count)
                ]
                weights.append(jnp.concatenate(parts, axis=1))
            mixed = jnp.dot(
                jnp.concatenate(weights, axis=0),
                jnp.concatenate([v, ones], axis=1),
                preferred_element_type=jnp.float32,
            )
            for at in range(0, tall, SLAB):
                here = slice(at, at + SLAB)
                acc, total = mixed[here, :HEAD_DIM], mixed[here, HEAD_DIM:]
                if not first:
                    shrink = shrink_ref[slot, here]
                    acc = acc_in[g, here] * shrink + acc
                    total = sum_in[g, here] * shrink + total
                if last:
                    head, row = g * GROUP + at // rows, at % rows
                    cols = slice(head * HEAD_DIM, (head + 1) * HEAD_DIM)
                    out_ref[row:row + SLAB, cols] = (acc / total).astype(jnp.bfloat16)
                else:
                    acc_out[g, here] = acc
                    sum_out[g, here] = total

    if first or last:
        body()
    else:
        me = lax.axis_index("seq")
        wanted = jnp.bool_(False)
        for i in users:
            wanted |= me == i
        pl.when(wanted)(body)


def attend(pieces, docs, places, q, mask, state=None, last=False):
    first = state is None
    count = len(pieces)
    rows = pieces[0].data.shape[0]
    stacked = (KV_HEADS, GROUP * rows, HEAD_DIM)
    vmem = pl.BlockSpec(memory_space=pltpu.VMEM)
    args = [q, mask] + [p.data for p in pieces] + ([] if first else list(state))
    if last:
        out_shape = [jax.ShapeDtypeStruct((rows, HEADS * HEAD_DIM), jnp.bfloat16)]
    else:
        out_shape = [jax.ShapeDtypeStruct(stacked, jnp.float32)] * 3
    users = [i for i in range(len(places[0])) if any(bases[i] != NOWHERE for bases in places)]
    return pl.pallas_call(
        functools.partial(attend_kernel, count, docs, first, last, users),
        out_shape=out_shape,
        in_specs=[vmem] * len(args),
        out_specs=[vmem] * len(out_shape),
        scratch_shapes=[
            pltpu.VMEM((2, GROUP * rows, count * rows), jnp.float32),
            pltpu.VMEM((2, GROUP * rows, HEAD_DIM), jnp.float32),
        ],
        input_output_aliases={} if first or last else {2 + count + n: n for n in range(3)},
        cost_estimate=pl.CostEstimate(
            flops=4 * rows * HEADS * count * rows * HEAD_DIM,
            bytes_accessed=4 * 10**6,
            transcendentals=rows * HEADS * count * rows,
        ),
        compiler_params=pltpu.CompilerParams(vmem_limit_bytes=VMEM_LIMIT),
    )(*args)


def block_reach(count):
    return -(-5 * count // 8)


def chip_reach_of(count):
    return -(-block_reach(count) // 2)


def per_device(count, queries, keys, values, doc_lengths):
    rows = queries.shape[0]
    reach, chip_reach = block_reach(count), chip_reach_of(count)

    def closed(shift, keep):
        return cycles({i: i + shift for i in range(count) if i + shift < count and keep(i)}, count)

    sibling = [(i, i ^ 1) for i in range(count)]
    across = [(i, i ^ 2) for i in range(count)]
    own, cosine, sine = prepare(doc_lengths, keys, values)
    own = Piece(own, list(range(count)))
    stages = [[own, own.move(sibling)]]
    a, before, late = own, None, []
    half_reach = chip_reach // 2
    for s in range(1, half_reach + 1):
        b = a.move(across)
        a = a.move(closed(4, lambda i: i >= 4 * (s - 1)))
        stages.append(late + [a, b])
        late = [a.move(sibling), b.move(sibling)]
        before = b
    if chip_reach % 2:
        near = 4 * half_reach
        c = before.move(closed(4, lambda i: not i & 2 and i >= near - 4))
        a = a.move(closed(2, lambda i: i >= near))
        stages += [late + [a, c], [a.move(sibling), c.move(sibling)]]
    else:
        b = a.move(across)
        stages += [late + [b], [b.move(sibling)]]

    seen = [set() for _ in range(count)]
    places = []
    for pieces in stages:
        table = [[NOWHERE] * count for _ in pieces]
        for b, piece in enumerate(pieces):
            for i in range(count):
                j = piece.source[i]
                if i - reach <= j <= i and j not in seen[i]:
                    seen[i].add(j)
                    table[b][i] = j * rows
        places.append(table)
    for i in range(count):
        assert seen[i] == set(range(max(0, i - reach), i + 1))

    q, *masks = turn_queries(doc_lengths, queries, cosine, sine, places)
    state, docs = None, doc_lengths.shape[0]
    for n, pieces in enumerate(stages):
        state = attend(pieces, docs, places[n], q, masks[n], state, last=n == len(stages) - 1)
    return state[0]


def solution(mesh):
    count = mesh.shape["seq"]

    def body(*args):
        return per_device(count, *args)

    return jax.shard_map(
        body,
        mesh=mesh,
        in_specs=(
            P(("grp", "seq"), None),
            P(("grp", "seq"), None),
            P(("grp", "seq"), None),
            P("grp"),
        ),
        out_specs=P(("grp", "seq"), None),
        check_vma=False,
    )
```

time: 53.3 us -> 50 us (0.938)
  the two profiles are of different devices: /device:TPU:19 before, /device:TPU:17 now
where the time goes in v4:
time: 50 us; the launch traced here: 49.8 us
  starting transfers between devices  20.3 us (41%)
  Pallas kernels  16.4 us (33%)
  waiting for transfers between devices  13 us (26%)
    ppermute x13, starting transfers between devices, move(): return Piece(lax.ppermute(self.data, 'seq', pairs), source)  20.3 us
    pallas_call x5, Pallas kernels, attend(): pl.pallas_call(functools.partial(attend_kernel, count, docs, first, last,...  13.2 us
    ppermute x13, waiting for transfers between devices, move(): return Piece(lax.ppermute(self.data, 'seq', pairs), source)  13 us
    pallas_call x1, Pallas kernels, turn_queries(): pl.pallas_call(functools.partial(turn_kernel, places, lengths.shape[0]),...  2.06 us
    pallas_call x1, Pallas kernels, prepare(): pl.pallas_call(prepare_kernel, out_shape=[jax.ShapeDtypeStruct((rows, 2 *...  1.13 us
  transfers between devices with their start and end apart: 13, of which 3 were waited for; matrix products, arithmetic and copies ran while one was open for 0% of the time, Pallas kernels for 25%

profile of v4, /device:TPU:17, one launch (start us, length us, event | category | flops | bytes accessed | tf_op | source)
XLA Modules:
  0.0 49.8 jit_solution(14459283214871163126)
XLA Ops:
  0.0 1.1 %prepare.1 = (bf16[128,1024]{1,0:T(8,128)(2,1)S(1)}, f32[128,128]{1,0:T(8,128)S(1)}, f32[128,128]{1,0:T(8,128)S(1)}) custom-call(f32[1,128]{1,0:T(1,128)S(1)} %fusion.2.freq_ref, s32[8]{0:T(128)} %lengths_hbm.3, bf16[128,512]{1,0:T(8,128)(2,1)} %k_hbm.1, bf16[128,512]{1,0:T(8,128)(2,1)} %v_hbm.1), custom_call_target="tpu_custom_call" | custom-call | flops 1000000 | bytes 600000 | tf_op jit(solution)/shard_map/prepare/pallas_call | solution.py:105
  1.1 1.3 %collective-permute-start = (bf16[128,1024]{1,0:T(8,128)(2,1)S(1)}, bf16[128,1024]{1,0:T(8,128)(2,1)S(1)}, u32[]{:S(2)}, u32[]{:S(2)}) collective-permute-start(bf16[128,1024]{1,0:T(8,128)(2,1)S(1)} %get-tuple-element.30.refs_2_), channel_id=1, source_target_pairs={{0,8},{2,10},{4,12},{6,14},{8,16},{10,18},{12,20},{14,22},{16,24},... | collective-permute-start | bytes 786440 | tf_op jit(solution)/shard_map/ppermute | solution.py:45
  2.5 5.9 %collective-permute-done.refs_2_ = bf16[128,1024]{1,0:T(8,128)(2,1)S(1)} collective-permute-done((bf16[128,1024]{1,0:T(8,128)(2,1)S(1)}, bf16[128,1024]{1,0:T(8,128)(2,1)S(1)}, u32[]{:S(2)}, u32[]{:S(2)}) %collective-permute-start) | collective-permute-done | bytes 262176 | tf_op jit(solution)/shard_map/ppermute | solution.py:45
  8.4 3.2 %collective-permute-start.1 = (bf16[128,1024]{1,0:T(8,128)(2,1)S(1)}, bf16[128,1024]{1,0:T(8,128)(2,1)S(1)}, u32[]{:S(2)}, u32[]{:S(2)}) collective-permute-start(bf16[128,1024]{1,0:T(8,128)(2,1)S(1)} %collective-permute-done.refs_2_), channel_id=1, source_target_pairs={{0,0},{2,2},{4,4},{6,6},{8,16},{10,18},{12,20},{14,22},{16,24},{18... | collective-permute-start | bytes 786440 | tf_op jit(solution)/shard_map/ppermute | solution.py:45
  11.6 1.3 %collective-permute-start.4 = (bf16[128,1024]{1,0:T(8,128)(2,1)S(1)}, bf16[128,1024]{1,0:T(8,128)(2,1)S(1)}, u32[]{:S(2)}, u32[]{:S(2)}) collective-permute-start(bf16[128,1024]{1,0:T(8,128)(2,1)S(1)} %collective-permute-done.refs_2_), channel_id=1, source_target_pairs={{0,4},{2,6},{4,0},{6,2},{8,12},{10,14},{12,8},{14,10},{16,20},{18,... | collective-permute-start | bytes 786440 | tf_op jit(solution)/shard_map/ppermute | solution.py:45
  12.9 0.2 collective-permute-start.10
  13.1 2.4 %collective-permute-start.12 = (bf16[128,1024]{1,0:T(8,128)(2,1)S(1)}, bf16[128,1024]{1,0:T(8,128)(2,1)S(1)}, u32[]{:S(2)}, u32[]{:S(2)}) collective-permute-start(bf16[128,1024]{1,0:T(8,128)(2,1)S(1)} %get-tuple-element.30.refs_2_), channel_id=1, source_target_pairs={{0,2},{2,0},{4,6},{6,4},{8,10},{10,8},{12,14},{14,12},{16,18},{18,... | collective-permute-start | bytes 786440 | tf_op jit(solution)/shard_map/ppermute | solution.py:45
  15.5 0.0 collective-permute-start.9
  15.5 1.1 %collective-permute-done.1.refs_4_ = bf16[128,1024]{1,0:T(8,128)(2,1)S(1)} collective-permute-done((bf16[128,1024]{1,0:T(8,128)(2,1)S(1)}, bf16[128,1024]{1,0:T(8,128)(2,1)S(1)}, u32[]{:S(2)}, u32[]{:S(2)}) %collective-permute-start.1) | collective-permute-done | bytes 262176 | tf_op jit(solution)/shard_map/ppermute | solution.py:45
  16.6 3.1 %collective-permute-start.2 = (bf16[128,1024]{1,0:T(8,128)(2,1)S(1)}, bf16[128,1024]{1,0:T(8,128)(2,1)S(1)}, u32[]{:S(2)}, u32[]{:S(2)}) collective-permute-start(bf16[128,1024]{1,0:T(8,128)(2,1)S(1)} %collective-permute-done.1.refs_4_), channel_id=1, source_target_pairs={{0,0},{2,2},{4,4},{6,6},{8,8},{10,10},{12,12},{14,14},{16,20},{18,... | collective-permute-start | bytes 786440 | tf_op jit(solution)/shard_map/ppermute | solution.py:45
  19.8 0.0 collective-permute-done.4.refs_5_
  19.8 3.2 %collective-permute-start.5 = (bf16[128,1024]{1,0:T(8,128)(2,1)S(1)}, bf16[128,1024]{1,0:T(8,128)(2,1)S(1)}, u32[]{:S(2)}, u32[]{:S(2)}) collective-permute-start(bf16[128,1024]{1,0:T(8,128)(2,1)S(1)} %collective-permute-done.4.refs_5_), channel_id=1, source_target_pairs={{0,0},{2,2},{4,4},{6,6},{8,16},{10,18},{12,12},{14,14},{16,24},{18... | collective-permute-start | bytes 786440 | tf_op jit(solution)/shard_map/ppermute | solution.py:45
  23.0 6.0 %collective-permute-done.10.refs_3_ = bf16[128,1024]{1,0:T(8,128)(2,1)S(1)} collective-permute-done((bf16[128,1024]{1,0:T(8,128)(2,1)S(1)}, bf16[128,1024]{1,0:T(8,128)(2,1)S(1)}, u32[]{:S(2)}, u32[]{:S(2)}) %collective-permute-start.10) | collective-permute-done | bytes 262176 | tf_op jit(solution)/shard_map/ppermute | solution.py:45
  28.9 2.7 %collective-permute-start.11 = (bf16[128,1024]{1,0:T(8,128)(2,1)S(1)}, bf16[128,1024]{1,0:T(8,128)(2,1)S(1)}, u32[]{:S(2)}, u32[]{:S(2)}) collective-permute-start(bf16[128,1024]{1,0:T(8,128)(2,1)S(1)} %collective-permute-done.10.refs_3_), channel_id=1, source_target_pairs={{0,2},{2,0},{4,6},{6,4},{8,10},{10,8},{12,14},{14,12},{16,18},{18,... | collective-permute-start | bytes 786440 | tf_op jit(solution)/shard_map/ppermute | solution.py:45
  31.6 0.0 collective-permute-done.12.refs_3_
  31.6 0.0 collective-permute-start.7
  31.6 0.0 collective-permute-done.9.refs_2_
  31.6 0.5 %collective-permute-start.8 = (bf16[128,1024]{1,0:T(8,128)(2,1)S(1)}, bf16[128,1024]{1,0:T(8,128)(2,1)S(1)}, u32[]{:S(2)}, u32[]{:S(2)}) collective-permute-start(bf16[128,1024]{1,0:T(8,128)(2,1)S(1)} %collective-permute-done.4.refs_5_), channel_id=1, source_target_pairs={{0,2},{2,0},{4,6},{6,4},{8,10},{10,8},{12,14},{14,12},{16,18},{18,... | collective-permute-start | bytes 786440 | tf_op jit(solution)/shard_map/ppermute | solution.py:45
  32.1 2.1 %turn_queries.1 = (bf16[4,896,256]{2,1,0:T(8,128)(2,1)S(1)}, bf16[256,128]{1,0:T(8,128)(2,1)S(1)}, bf16[256,128]{1,0:T(8,128)(2,1)S(1)}, bf16[512,128]{1,0:T(8,1...) custom-call(s32[8]{0:T(128)} %lengths_hbm.3, bf16[128,3584]{1,0:T(8,128)(2,1)} %q_hbm.1, ...), custom_call_target="tpu_custom_call" | custom-call | flops 100000000 | bytes 4000000 | tf_op jit(solution)/shard_map/turn_queries/pallas_call | solution.py:179
  34.2 0.0 collective-permute-done.2.refs_4_
  34.2 0.1 collective-permute-start.3
  34.3 0.0 collective-permute-done.5.refs_5_
  34.3 2.2 %collective-permute-start.6 = (bf16[128,1024]{1,0:T(8,128)(2,1)S(1)}, bf16[128,1024]{1,0:T(8,128)(2,1)S(1)}, u32[]{:S(2)}, u32[]{:S(2)}) collective-permute-start(bf16[128,1024]{1,0:T(8,128)(2,1)S(1)} %collective-permute-done.5.refs_5_), channel_id=1, source_target_pairs={{0,2},{2,0},{4,6},{6,4},{8,10},{10,8},{12,14},{14,12},{16,18},{18,... | collective-permute-start | bytes 786440 | tf_op jit(solution)/shard_map/ppermute | solution.py:45
  36.5 1.2 %shard_map.46 = (f32[4,896,128]{2,1,0:T(8,128)S(1)}, f32[4,896,128]{2,1,0:T(8,128)S(1)}, f32[4,896,128]{2,1,0:T(8,128)S(1)}) custom-call(bf16[4,896,256]{2,1,0:T(8,128)(2,1)S(1)} %get-tuple-element.28.refs_0_, bf16[256,128]{1,0:T(8,128)(2,1)S(1)} %get-tuple-element.34.refs_1_, bf16[128,1024]{1,0:T(8,128)(2,1)S(1)} %get-tuple-element.30.refs_2_, ...), custom_call_target="tpu_custom_call" | custom-call | flops 469762048 | bytes 4000000 | tf_op jit(solution)/shard_map/pallas_call | solution.py:292
  37.8 2.4 %shard_map.47 = (f32[4,896,128]{2,1,0:T(8,128)S(1)}, f32[4,896,128]{2,1,0:T(8,128)S(1)}, f32[4,896,128]{2,1,0:T(8,128)S(1)}) custom-call(bf16[4,896,256]{2,1,0:T(8,128)(2,1)S(1)} %get-tuple-element.28.refs_0_, bf16[256,128]{1,0:T(8,128)(2,1)S(1)} %get-tuple-element.33.refs_1_, ...), custom_call_target="tpu_custom_call", output_to_operand_aliasing={{0}: (4, {}), {1}: (5, {}), {2}: (6, {})} | custom-call | flops 469762048 | bytes 4000000 | tf_op jit(solution)/shard_map/pallas_call | solution.py:292
  40.1 0.0 collective-permute-done.11.refs_3_
  40.1 3.4 %shard_map.48 = (f32[4,896,128]{2,1,0:T(8,128)S(1)}, f32[4,896,128]{2,1,0:T(8,128)S(1)}, f32[4,896,128]{2,1,0:T(8,128)S(1)}) custom-call(bf16[4,896,256]{2,1,0:T(8,128)(2,1)S(1)} %get-tuple-element.28.refs_0_, bf16[512,128]{1,0:T(8,128)(2,1)S(1)} %get-tuple-element.32.refs_1_, ...), custom_call_target="tpu_custom_call", output_to_operand_aliasing={{0}: (6, {}), {1}: (7, {}), {2}: (8, {})} | custom-call | flops 939524096 | bytes 4000000 | tf_op jit(solution)/shard_map/pallas_call | solution.py:292
  43.5 0.0 collective-permute-done.7.refs_2_
  43.6 0.0 collective-permute-done.8.refs_3_
  43.6 3.6 %shard_map.49 = (f32[4,896,128]{2,1,0:T(8,128)S(1)}, f32[4,896,128]{2,1,0:T(8,128)S(1)}, f32[4,896,128]{2,1,0:T(8,128)S(1)}) custom-call(bf16[4,896,256]{2,1,0:T(8,128)(2,1)S(1)} %get-tuple-element.28.refs_0_, bf16[512,128]{1,0:T(8,128)(2,1)S(1)} %get-tuple-element.31.refs_1_, ...), custom_call_target="tpu_custom_call", output_to_operand_aliasing={{0}: (6, {}), {1}: (7, {}), {2}: (8, {})} | custom-call | flops 939524096 | bytes 4000000 | tf_op jit(solution)/shard_map/pallas_call | solution.py:292
  47.2 0.0 collective-permute-done.3.refs_2_
  47.2 2.6 %shard_map.50 = bf16[128,3584]{1,0:T(8,128)(2,1)} custom-call(bf16[4,896,256]{2,1,0:T(8,128)(2,1)S(1)} %get-tuple-element.28.refs_0_, bf16[256,128]{1,0:T(8,128)(2,1)S(1)} %get-tuple-element.29.refs_1_, bf16[128,1024]{1,0:T(8,128)(2,1)S(1)} %collective-permute-done.3.refs_2_, bf16[128,1024]{1,0:T(8,128)(2,1)S(1)} %collective-permute-done.6.refs_3_, ...), custom_call_target="tpu_custom_call" | custom-call | flops 469762048 | bytes 4000000 | tf_op jit(solution)/shard_map/pallas_call | solution.py:292
  (2 shorter events, 0.0 us)
Async XLA Ops:
  1.1 7.2 %collective-permute-start = (bf16[128,1024]{1,0:T(8,128)(2,1)S(1)}, bf16[128,1024]{1,0:T(8,128)(2,1)S(1)}, u32[]{:S(2)}, u32[]{:S(2)}) collective-permute-start(bf16[128,1024]{1,0:T(8,128)(2,1)S(1)} %get-tuple-element.30.refs_2_), channel_id=1, source_target_pairs={{0,8},{2,10},{4,12},{6,14},{8,16},{10,18},{12,20},{14,22},{16,24},... | collective-permute-start | bytes 786440 | tf_op jit(solution)/shard_map/ppermute | solution.py:45
  8.4 8.2 %collective-permute-start.1 = (bf16[128,1024]{1,0:T(8,128)(2,1)S(1)}, bf16[128,1024]{1,0:T(8,128)(2,1)S(1)}, u32[]{:S(2)}, u32[]{:S(2)}) collective-permute-start(bf16[128,1024]{1,0:T(8,128)(2,1)S(1)} %collective-permute-done.refs_2_), channel_id=1, source_target_pairs={{0,0},{2,2},{4,4},{6,6},{8,16},{10,18},{12,20},{14,22},{16,24},{18... | collective-permute-start | bytes 786440 | tf_op jit(solution)/shard_map/ppermute | solution.py:45
  11.6 8.2 %collective-permute-start.4 = (bf16[128,1024]{1,0:T(8,128)(2,1)S(1)}, bf16[128,1024]{1,0:T(8,128)(2,1)S(1)}, u32[]{:S(2)}, u32[]{:S(2)}) collective-permute-start(bf16[128,1024]{1,0:T(8,128)(2,1)S(1)} %collective-permute-done.refs_2_), channel_id=1, source_target_pairs={{0,4},{2,6},{4,0},{6,2},{8,12},{10,14},{12,8},{14,10},{16,20},{18,... | collective-permute-start | bytes 786440 | tf_op jit(solution)/shard_map/ppermute | solution.py:45
  12.9 16.1 %collective-permute-start.10 = (bf16[128,1024]{1,0:T(8,128)(2,1)S(1)}, bf16[128,1024]{1,0:T(8,128)(2,1)S(1)}, u32[]{:S(2)}, u32[]{:S(2)}) collective-permute-start(bf16[128,1024]{1,0:T(8,128)(2,1)S(1)} %get-tuple-element.30.refs_2_), channel_id=1, source_target_pairs={{0,4},{2,6},{4,0},{6,2},{8,12},{10,14},{12,8},{14,10},{16,20},{18,... | collective-permute-start | bytes 786440 | tf_op jit(solution)/shard_map/ppermute | solution.py:45
  13.1 18.5 %collective-permute-start.12 = (bf16[128,1024]{1,0:T(8,128)(2,1)S(1)}, bf16[128,1024]{1,0:T(8,128)(2,1)S(1)}, u32[]{:S(2)}, u32[]{:S(2)}) collective-permute-start(bf16[128,1024]{1,0:T(8,128)(2,1)S(1)} %get-tuple-element.30.refs_2_), channel_id=1, source_target_pairs={{0,2},{2,0},{4,6},{6,4},{8,10},{10,8},{12,14},{14,12},{16,18},{18,... | collective-permute-start | bytes 786440 | tf_op jit(solution)/shard_map/ppermute | solution.py:45
  15.5 16.1 %collective-permute-start.9 = (bf16[128,1024]{1,0:T(8,128)(2,1)S(1)}, bf16[128,1024]{1,0:T(8,128)(2,1)S(1)}, u32[]{:S(2)}, u32[]{:S(2)}) collective-permute-start(bf16[128,1024]{1,0:T(8,128)(2,1)S(1)} %collective-permute-done.refs_2_), channel_id=1, source_target_pairs={{0,2},{2,0},{4,6},{6,4},{8,10},{10,8},{12,14},{14,12},{16,18},{18,... | collective-permute-start | bytes 786440 | tf_op jit(solution)/shard_map/ppermute | solution.py:45
  16.6 17.6 %collective-permute-start.2 = (bf16[128,1024]{1,0:T(8,128)(2,1)S(1)}, bf16[128,1024]{1,0:T(8,128)(2,1)S(1)}, u32[]{:S(2)}, u32[]{:S(2)}) collective-permute-start(bf16[128,1024]{1,0:T(8,128)(2,1)S(1)} %collective-permute-done.1.refs_4_), channel_id=1, source_target_pairs={{0,0},{2,2},{4,4},{6,6},{8,8},{10,10},{12,12},{14,14},{16,20},{18,... | collective-permute-start | bytes 786440 | tf_op jit(solution)/shard_map/ppermute | solution.py:45
  19.8 14.6 %collective-permute-start.5 = (bf16[128,1024]{1,0:T(8,128)(2,1)S(1)}, bf16[128,1024]{1,0:T(8,128)(2,1)S(1)}, u32[]{:S(2)}, u32[]{:S(2)}) collective-permute-start(bf16[128,1024]{1,0:T(8,128)(2,1)S(1)} %collective-permute-done.4.refs_5_), channel_id=1, source_target_pairs={{0,0},{2,2},{4,4},{6,6},{8,16},{10,18},{12,12},{14,14},{16,24},{18... | collective-permute-start | bytes 786440 | tf_op jit(solution)/shard_map/ppermute | solution.py:45
  28.9 11.2 %collective-permute-start.11 = (bf16[128,1024]{1,0:T(8,128)(2,1)S(1)}, bf16[128,1024]{1,0:T(8,128)(2,1)S(1)}, u32[]{:S(2)}, u32[]{:S(2)}) collective-permute-start(bf16[128,1024]{1,0:T(8,128)(2,1)S(1)} %collective-permute-done.10.refs_3_), channel_id=1, source_target_pairs={{0,2},{2,0},{4,6},{6,4},{8,10},{10,8},{12,14},{14,12},{16,18},{18,... | collective-permute-start | bytes 786440 | tf_op jit(solution)/shard_map/ppermute | solution.py:45
  31.6 11.9 %collective-permute-start.7 = (bf16[128,1024]{1,0:T(8,128)(2,1)S(1)}, bf16[128,1024]{1,0:T(8,128)(2,1)S(1)}, u32[]{:S(2)}, u32[]{:S(2)}) collective-permute-start(bf16[128,1024]{1,0:T(8,128)(2,1)S(1)} %collective-permute-done.1.refs_4_), channel_id=1, source_target_pairs={{0,2},{2,0},{4,6},{6,4},{8,10},{10,8},{12,14},{14,12},{16,18},{18,... | collective-permute-start | bytes 786440 | tf_op jit(solution)/shard_map/ppermute | solution.py:45
  31.6 11.9 %collective-permute-start.8 = (bf16[128,1024]{1,0:T(8,128)(2,1)S(1)}, bf16[128,1024]{1,0:T(8,128)(2,1)S(1)}, u32[]{:S(2)}, u32[]{:S(2)}) collective-permute-start(bf16[128,1024]{1,0:T(8,128)(2,1)S(1)} %collective-permute-done.4.refs_5_), channel_id=1, source_target_pairs={{0,2},{2,0},{4,6},{6,4},{8,10},{10,8},{12,14},{14,12},{16,18},{18,... | collective-permute-start | bytes 786440 | tf_op jit(solution)/shard_map/ppermute | solution.py:45
  34.2 12.9 %collective-permute-start.3 = (bf16[128,1024]{1,0:T(8,128)(2,1)S(1)}, bf16[128,1024]{1,0:T(8,128)(2,1)S(1)}, u32[]{:S(2)}, u32[]{:S(2)}) collective-permute-start(bf16[128,1024]{1,0:T(8,128)(2,1)S(1)} %collective-permute-done.2.refs_4_), channel_id=1, source_target_pairs={{0,2},{2,0},{4,6},{6,4},{8,10},{10,8},{12,14},{14,12},{16,18},{18,... | collective-permute-start | bytes 786440 | tf_op jit(solution)/shard_map/ppermute | solution.py:45
  34.3 12.8 %collective-permute-start.6 = (bf16[128,1024]{1,0:T(8,128)(2,1)S(1)}, bf16[128,1024]{1,0:T(8,128)(2,1)S(1)}, u32[]{:S(2)}, u32[]{:S(2)}) collective-permute-start(bf16[128,1024]{1,0:T(8,128)(2,1)S(1)} %collective-permute-done.5.refs_5_), channel_id=1, source_target_pairs={{0,2},{2,0},{4,6},{6,4},{8,10},{10,8},{12,14},{14,12},{16,18},{18,... | collective-permute-start | bytes 786440 | tf_op jit(solution)/shard_map/ppermute | solution.py:45

commit v5 on v4

--- a/solution.py
+++ b/solution.py
@@ -20,21 +20,7 @@
 SLAB = 32
 
 
-def cycles(wanted, count):
-    pairs = dict(wanted)
-    starts = [s for s in pairs if s not in set(pairs.values())]
-    for start in starts:
-        at = start
-        while at in pairs:
-            at = pairs[at]
-        pairs[at] = start
-    for i in range(count):
-        pairs.setdefault(i, i)
-    assert sorted(pairs.values()) == list(range(count))
-    return sorted(pairs.items())
-
-
-class Piece:
+class Held:
     def __init__(self, data, source):
         self.data, self.source = data, source
 
@@ -42,7 +28,56 @@
         source = list(self.source)
         for s, t in pairs:
             source[t] = self.source[s]
-        return Piece(lax.ppermute(self.data, "seq", pairs), source)
+        return Held(self.data if self.data is None else lax.ppermute(self.data, "seq", pairs), source)
+
+
+def joined(a, b):
+    return Held(join(a.data, b.data), [x + y for x, y in zip(a.source, b.source)])
+
+
+def relay(own, chip_reach, kernel):
+    count = len(own.source)
+
+    def around(shift, first, side=None):
+        span = count - first
+        pairs = {}
+        for i in range(count):
+            if i < first or (side is not None and i & 2):
+                pairs[i] = i ^ 1
+            else:
+                pairs[i] = first + (i - first + shift) % span
+        if side is not None:
+            for core in range(2):
+                head, last = first + core, count - shift + core
+                pairs[last], pairs[head + 2] = head + 2, head
+        assert sorted(pairs.values()) == list(range(count))
+        return sorted(pairs.items())
+
+    sibling = [(i, i ^ 1) for i in range(count)]
+    across = [(i, i ^ 2) for i in range(count)]
+
+    def swapped(pieces):
+        both = pieces[0] if len(pieces) == 1 else joined(*pieces)
+        return both.move(sibling)
+
+    full, odd = chip_reach // 2, chip_reach % 2
+    a = own
+    for s in range(1, full + 1):
+        b = a.move(across)
+        here = a.move(around(4, 4 * (s - 1)))
+        if s == 1:
+            kernel("k0", [own, own.move(sibling)])
+        kernel("k%d" % s, [here, b])
+        kernel("kd%d" % s, [swapped([here, b])])
+        a = here
+    stage = full + 1
+    if odd:
+        c = b.move(around(4, 4 * (full - 1), 0))
+        pieces = [a.move(around(2, 4 * full)), c]
+    else:
+        pieces = [a.move(across)]
+    kernel("k%d" % stage, pieces)
+    kernel("last", [swapped(pieces)], True)
 
 
 def rotated(x, cosine, sine):
@@ -192,11 +227,11 @@
     )(in_hbm(lengths), in_hbm(queries), cosine, sine)
 
 
-def attend_kernel(count, docs, first, last, users, *refs):
+def attend_kernel(count, operands, docs, first, last, users, *refs):
     refs = list(refs)
     take = lambda n: [refs.pop(0) for _ in range(n)]
     q_ref, mask_ref = take(2)
-    kv_refs = take(count)
+    kv_refs = take(operands)
     if not first:
         max_in, sum_in, acc_in = take(3)
     if last:
@@ -204,8 +239,11 @@
     else:
         max_out, sum_out, acc_out = take(3)
     score_ref, shrink_ref = take(2)
-
-    rows = kv_refs[0].shape[0]
+    if last:
+        out_hbm, (out_ref, sems) = out_ref, take(2)
+
+    rows = score_ref.shape[2] // count
+    kv_refs = [r.at[n:n + rows] for r in kv_refs for n in range(0, r.shape[0], rows)]
     width = KV_HEADS * HEAD_DIM
     tall = GROUP * rows
     key_lane = lanes_iota((count * rows, HEAD_DIM), 1)
@@ -217,6 +255,7 @@
             k = jnp.concatenate([k, jnp.where(key_lane < docs, mask_ref[...], k)], axis=1)
             return lax.dot_general(q_ref[g], k, (((1,), (1,)), ((), ())), preferred_element_type=jnp.float32)
 
+        copies = []
         score_ref[0] = score(0)
         for g in range(KV_HEADS):
             slot = g % 2
@@ -266,6 +305,12 @@
                 else:
                     acc_out[g, here] = acc
                     sum_out[g, here] = total
+            if last:
+                cols = pl.ds(g * GROUP * HEAD_DIM, GROUP * HEAD_DIM)
+                copies.append(pltpu.make_async_copy(out_ref.at[:, cols], out_hbm.at[:, cols], sems.at[g]))
+                copies[-1].start()
+        for copy in copies:
+            copy.wait()
 
     if first or last:
         body()
@@ -279,26 +324,29 @@
 
 def attend(pieces, docs, places, q, mask, state=None, last=False):
     first = state is None
-    count = len(pieces)
-    rows = pieces[0].data.shape[0]
+    count = len(places)
+    rows = q.shape[1] // GROUP
     stacked = (KV_HEADS, GROUP * rows, HEAD_DIM)
     vmem = pl.BlockSpec(memory_space=pltpu.VMEM)
-    args = [q, mask] + [p.data for p in pieces] + ([] if first else list(state))
+    args = [q, mask] + pieces + ([] if first else list(state))
     if last:
         out_shape = [jax.ShapeDtypeStruct((rows, HEADS * HEAD_DIM), jnp.bfloat16)]
     else:
         out_shape = [jax.ShapeDtypeStruct(stacked, jnp.float32)] * 3
+    scratch = [
+        pltpu.VMEM((2, GROUP * rows, count * rows), jnp.float32),
+        pltpu.VMEM((2, GROUP * rows, HEAD_DIM), jnp.float32),
+    ]
+    if last:
+        scratch += [pltpu.VMEM((rows, HEADS * HEAD_DIM), jnp.bfloat16), pltpu.SemaphoreType.DMA((KV_HEADS,))]
     users = [i for i in range(len(places[0])) if any(bases[i] != NOWHERE for bases in places)]
     return pl.pallas_call(
-        functools.partial(attend_kernel, count, docs, first, last, users),
+        functools.partial(attend_kernel, count, len(pieces), docs, first, last, users),
         out_shape=out_shape,
         in_specs=[vmem] * len(args),
-        out_specs=[vmem] * len(out_shape),
-        scratch_shapes=[
-            pltpu.VMEM((2, GROUP * rows, count * rows), jnp.float32),
-            pltpu.VMEM((2, GROUP * rows, HEAD_DIM), jnp.float32),
-        ],
-        input_output_aliases={} if first or last else {2 + count + n: n for n in range(3)},
+        out_specs=[pl.BlockSpec(memory_space=pltpu.HBM)] if last else [vmem] * len(out_shape),
+        scratch_shapes=scratch,
+        input_output_aliases={} if first or last else {2 + len(pieces) + n: n for n in range(3)},
         cost_estimate=pl.CostEstimate(
             flops=4 * rows * HEADS * count * rows * HEAD_DIM,
             bytes_accessed=4 * 10**6,
@@ -308,6 +356,27 @@
     )(*args)
 
 
+def join_kernel(a_ref, b_ref, out_ref):
+    rows = a_ref.shape[0]
+    out_ref[:rows, :] = a_ref[...]
+    out_ref[rows:, :] = b_ref[...]
+
+
+def join(a, b):
+    if a is None:
+        return None
+    vmem = pl.BlockSpec(memory_space=pltpu.VMEM)
+    return pl.pallas_call(
+        join_kernel,
+        out_shape=jax.ShapeDtypeStruct((2 * a.shape[0], a.shape[1]), a.dtype),
+        in_specs=[vmem] * 2,
+        out_specs=vmem,
+        cost_estimate=pl.CostEstimate(flops=10**5, bytes_accessed=10**6, transcendentals=0),
+        compiler_params=pltpu.CompilerParams(vmem_limit_bytes=VMEM_LIMIT),
+        name="join",
+    )(a, b)
+
+
 def block_reach(count):
     return -(-5 * count // 8)
 
@@ -320,50 +389,39 @@
     rows = queries.shape[0]
     reach, chip_reach = block_reach(count), chip_reach_of(count)
 
-    def closed(shift, keep):
-        return cycles({i: i + shift for i in range(count) if i + shift < count and keep(i)}, count)
-
-    sibling = [(i, i ^ 1) for i in range(count)]
-    across = [(i, i ^ 2) for i in range(count)]
-    own, cosine, sine = prepare(doc_lengths, keys, values)
-    own = Piece(own, list(range(count)))
-    stages = [[own, own.move(sibling)]]
-    a, before, late = own, None, []
-    half_reach = chip_reach // 2
-    for s in range(1, half_reach + 1):
-        b = a.move(across)
-        a = a.move(closed(4, lambda i: i >= 4 * (s - 1)))
-        stages.append(late + [a, b])
-        late = [a.move(sibling), b.move(sibling)]
-        before = b
-    if chip_reach % 2:
-        near = 4 * half_reach
-        c = before.move(closed(4, lambda i: not i & 2 and i >= near - 4))
-        a = a.move(closed(2, lambda i: i >= near))
-        stages += [late + [a, c], [a.move(sibling), c.move(sibling)]]
-    else:
-        b = a.move(across)
-        stages += [late + [b], [b.move(sibling)]]
-
     seen = [set() for _ in range(count)]
-    places = []
-    for pieces in stages:
-        table = [[NOWHERE] * count for _ in pieces]
-        for b, piece in enumerate(pieces):
-            for i in range(count):
-                j = piece.source[i]
-                if i - reach <= j <= i and j not in seen[i]:
-                    seen[i].add(j)
-                    table[b][i] = j * rows
-        places.append(table)
+    places = {}
+
+    def place(name, pieces, last=False):
+        table = []
+        for piece in pieces:
+            for b in range(len(piece.source[0])):
+                bases = [NOWHERE] * count
+                for i in range(count):
+                    j = piece.source[i][b]
+                    if i - reach <= j <= i and j not in seen[i]:
+                        seen[i].add(j)
+                        bases[i] = j * rows
+                table.append(bases)
+        places[name] = table
+
+    source = [(i,) for i in range(count)]
+    relay(Held(None, source), chip_reach, place)
     for i in range(count):
         assert seen[i] == set(range(max(0, i - reach), i + 1))
 
-    q, *masks = turn_queries(doc_lengths, queries, cosine, sine, places)
-    state, docs = None, doc_lengths.shape[0]
-    for n, pieces in enumerate(stages):
-        state = attend(pieces, docs, places[n], q, masks[n], state, last=n == len(stages) - 1)
-    return state[0]
+    own, cosine, sine = prepare(doc_lengths, keys, values)
+    q, *masks = turn_queries(doc_lengths, queries, cosine, sine, list(places.values()))
+    masks = dict(zip(places, masks))
+    docs = doc_lengths.shape[0]
+    held = {"state": None}
+
+    def kernel(name, pieces, last=False):
+        data = [p.data for p in pieces]
+        held["state"] = attend(data, docs, places[name], q, masks[name], held["state"], last)
+
+    relay(Held(own, source), chip_reach, kernel)
+    return held["state"][0]
 
 
 def solution(mesh):

time: 50 us -> 50.9 us (1.018)
  starting transfers between devices: 20.3 us -> 12.3 us
  waiting for transfers between devices: 13 us -> 19.2 us
  Pallas kernels: 16.4 us -> 19 us
    ppermute x13 -> x10, starting transfers between devices: 20.3 us -> 12.3 us  [move(): lax.ppermute(self.data, 'seq', pairs)]
    ppermute x13 -> x10, waiting for transfers between devices: 13 us -> 19.2 us  [move(): lax.ppermute(self.data, 'seq', pairs)]
    pallas_call x5 -> x10, Pallas kernels: 13.2 us -> 15.8 us  [the longest x7 15.7 us: attend(): pl.pallas_call(functools.partial(attend_kernel, count, len(pieces), docs,...]
  transfers between devices with their start and end apart: 13 -> 10, of which waited for: 3 -> 3; matrix products, arithmetic and copies ran while one was open for 0% -> 0% of each run, Pallas kernels for 25% -> 30%
where the time goes in v5:
time: 50.9 us; the launch traced here: 50.8 us
  waiting for transfers between devices  19.2 us (38%)
  Pallas kernels  19 us (37%)
  starting transfers between devices  12.3 us (24%)
    ppermute x10, waiting for transfers between devices, move(): lax.ppermute(self.data, 'seq', pairs)  19.2 us
    pallas_call x7, Pallas kernels, attend(): pl.pallas_call(functools.partial(attend_kernel, count, len(pieces), docs,...  15.7 us
    ppermute x10, starting transfers between devices, move(): lax.ppermute(self.data, 'seq', pairs)  12.3 us
    pallas_call x1, Pallas kernels, turn_queries(): pl.pallas_call(functools.partial(turn_kernel, places, lengths.shape[0]),...  2.07 us
    pallas_call x1, Pallas kernels, prepare(): pl.pallas_call(prepare_kernel, out_shape=[jax.ShapeDtypeStruct((rows, 2 *...  1.13 us
  transfers between devices with their start and end apart: 10, of which 3 were waited for; matrix products, arithmetic and copies ran while one was open for 0% of the time, Pallas kernels for 30%

profile of v5, /device:TPU:17, one launch (start us, length us, event | category | flops | bytes accessed | tf_op | source)
XLA Modules:
  0.0 50.8 jit_solution(6569956831350395823)
XLA Ops:
  0.0 1.1 %prepare.1 = (bf16[128,1024]{1,0:T(8,128)(2,1)S(1)}, f32[128,128]{1,0:T(8,128)S(1)}, f32[128,128]{1,0:T(8,128)S(1)}) custom-call(f32[1,128]{1,0:T(1,128)S(1)} %fusion.2.freq_ref, s32[8]{0:T(128)} %lengths_hbm.3, bf16[128,512]{1,0:T(8,128)(2,1)} %k_hbm.1, bf16[128,512]{1,0:T(8,128)(2,1)} %v_hbm.1), custom_call_target="tpu_custom_call" | custom-call | flops 1000000 | bytes 600000 | tf_op jit(solution)/shard_map/prepare/pallas_call | solution.py:140
  1.1 1.3 %collective-permute-start = (bf16[128,1024]{1,0:T(8,128)(2,1)S(1)}, bf16[128,1024]{1,0:T(8,128)(2,1)S(1)}, u32[]{:S(2)}, u32[]{:S(2)}) collective-permute-start(bf16[128,1024]{1,0:T(8,128)(2,1)S(1)} %get-tuple-element.38.refs_2_), channel_id=1, source_target_pairs={{0,8},{2,10},{4,12},{6,14},{8,16},{10,18},{12,20},{14,22},{16,24},... | collective-permute-start | bytes 786440 | tf_op jit(solution)/shard_map/ppermute | solution.py:31
  2.5 5.9 %collective-permute-done.a_ref.refs_2_ = bf16[128,1024]{1,0:T(8,128)(2,1)S(1)} collective-permute-done((bf16[128,1024]{1,0:T(8,128)(2,1)S(1)}, bf16[128,1024]{1,0:T(8,128)(2,1)S(1)}, u32[]{:S(2)}, u32[]{:S(2)}) %collective-permute-start) | collective-permute-done | bytes 262176 | tf_op jit(solution)/shard_map/ppermute | solution.py:31
  8.4 1.3 %collective-permute-start.1 = (bf16[128,1024]{1,0:T(8,128)(2,1)S(1)}, bf16[128,1024]{1,0:T(8,128)(2,1)S(1)}, u32[]{:S(2)}, u32[]{:S(2)}) collective-permute-start(bf16[128,1024]{1,0:T(8,128)(2,1)S(1)} %collective-permute-done.a_ref.refs_2_), channel_id=1, source_target_pairs={{0,2},{2,0},{4,6},{6,4},{8,16},{10,18},{12,20},{14,22},{16,24},{18... | collective-permute-start | bytes 786440 | tf_op jit(solution)/shard_map/ppermute | solution.py:31
  9.7 1.2 %collective-permute-start.3 = (bf16[128,1024]{1,0:T(8,128)(2,1)S(1)}, bf16[128,1024]{1,0:T(8,128)(2,1)S(1)}, u32[]{:S(2)}, u32[]{:S(2)}) collective-permute-start(bf16[128,1024]{1,0:T(8,128)(2,1)S(1)} %collective-permute-done.a_ref.refs_2_), channel_id=1, source_target_pairs={{0,4},{2,6},{4,0},{6,2},{8,12},{10,14},{12,8},{14,10},{16,20},{18,... | collective-permute-start | bytes 786440 | tf_op jit(solution)/shard_map/ppermute | solution.py:31
  10.9 0.2 collective-permute-start.7
  11.2 3.6 %collective-permute-done.1.a_ref.refs_2_ = bf16[128,1024]{1,0:T(8,128)(2,1)S(1)} collective-permute-done((bf16[128,1024]{1,0:T(8,128)(2,1)S(1)}, bf16[128,1024]{1,0:T(8,128)(2,1)S(1)}, u32[]{:S(2)}, u32[]{:S(2)}) %collective-permute-start.1) | collective-permute-done | bytes 262176 | tf_op jit(solution)/shard_map/ppermute | solution.py:31
  14.7 1.2 %collective-permute-start.2 = (bf16[128,1024]{1,0:T(8,128)(2,1)S(1)}, bf16[128,1024]{1,0:T(8,128)(2,1)S(1)}, u32[]{:S(2)}, u32[]{:S(2)}) collective-permute-start(bf16[128,1024]{1,0:T(8,128)(2,1)S(1)} %collective-permute-done.1.a_ref.refs_2_), channel_id=1, source_target_pairs={{0,2},{2,0},{4,6},{6,4},{8,10},{10,8},{12,14},{14,12},{16,20},{18,... | collective-permute-start | bytes 786440 | tf_op jit(solution)/shard_map/ppermute | solution.py:31
  16.0 0.0 collective-permute-done.3.b_ref.refs_3_
  16.0 1.3 %collective-permute-start.4 = (bf16[128,1024]{1,0:T(8,128)(2,1)S(1)}, bf16[128,1024]{1,0:T(8,128)(2,1)S(1)}, u32[]{:S(2)}, u32[]{:S(2)}) collective-permute-start(bf16[128,1024]{1,0:T(8,128)(2,1)S(1)} %collective-permute-done.3.b_ref.refs_3_), channel_id=1, source_target_pairs={{0,2},{2,0},{4,6},{6,4},{8,16},{10,18},{12,8},{14,10},{16,24},{18,... | collective-permute-start | bytes 786440 | tf_op jit(solution)/shard_map/ppermute | solution.py:31
  17.3 9.7 %collective-permute-done.7.b_ref.refs_3_ = bf16[128,1024]{1,0:T(8,128)(2,1)S(1)} collective-permute-done((bf16[128,1024]{1,0:T(8,128)(2,1)S(1)}, bf16[128,1024]{1,0:T(8,128)(2,1)S(1)}, u32[]{:S(2)}, u32[]{:S(2)}) %collective-permute-start.7) | collective-permute-done | bytes 262176 | tf_op jit(solution)/shard_map/ppermute | solution.py:31
  27.0 2.7 %collective-permute-start.8 = (bf16[256,1024]{1,0:T(8,128)(2,1)S(1)}, bf16[256,1024]{1,0:T(8,128)(2,1)S(1)}, u32[]{:S(2)}, u32[]{:S(2)}) collective-permute-start(bf16[256,1024]{1,0:T(8,128)(2,1)S(1)} %join.5), channel_id=1, source_target_pairs={{0,2},{2,0},{4,6},{6,4},{8,10},{10,8},{12,14},{14,12},{16,18},{18,... | collective-permute-start | bytes 1572872 | tf_op jit(solution)/shard_map/ppermute | solution.py:31
  29.8 0.1 collective-permute-start.6
  29.9 0.5 collective-permute-start.9
  30.4 0.0 collective-permute-done.2.a_ref.refs_2_
  30.4 0.0 collective-permute-done.4.b_ref.refs_3_
  30.4 2.4 %collective-permute-start.5 = (bf16[256,1024]{1,0:T(8,128)(2,1)S(1)}, bf16[256,1024]{1,0:T(8,128)(2,1)S(1)}, u32[]{:S(2)}, u32[]{:S(2)}) collective-permute-start(bf16[256,1024]{1,0:T(8,128)(2,1)S(1)} %join.3), channel_id=1, source_target_pairs={{0,2},{2,0},{4,6},{6,4},{8,10},{10,8},{12,14},{14,12},{16,18},{18,... | collective-permute-start | bytes 1572872 | tf_op jit(solution)/shard_map/ppermute | solution.py:31
  32.8 2.1 %turn_queries.1 = (bf16[4,896,256]{2,1,0:T(8,128)(2,1)S(1)}, bf16[256,128]{1,0:T(8,128)(2,1)S(1)}, bf16[256,128]{1,0:T(8,128)(2,1)S(1)}, bf16[256,128]{1,0:T(8,1...) custom-call(s32[8]{0:T(128)} %lengths_hbm.3, ...), custom_call_target="tpu_custom_call" | custom-call | flops 100000000 | bytes 4000000 | tf_op jit(solution)/shard_map/turn_queries/pallas_call | solution.py:214
  34.9 0.0 collective-permute-done.9.refs_3_
  34.9 1.2 %shard_map.46 = (f32[4,896,128]{2,1,0:T(8,128)S(1)}, f32[4,896,128]{2,1,0:T(8,128)S(1)}, f32[4,896,128]{2,1,0:T(8,128)S(1)}) custom-call(bf16[4,896,256]{2,1,0:T(8,128)(2,1)S(1)} %get-tuple-element.36.refs_0_, bf16[256,128]{1,0:T(8,128)(2,1)S(1)} %get-tuple-element.44.refs_1_, bf16[128,1024]{1,0:T(8,128)(2,1)S(1)} %get-tuple-element.38.refs_2_, ...), custom_call_target="tpu_custom_call" | custom-call | flops 469762048 | bytes 4000000 | tf_op jit(solution)/shard_map/pallas_call | solution.py:343
  36.1 2.4 %shard_map.47 = (f32[4,896,128]{2,1,0:T(8,128)S(1)}, f32[4,896,128]{2,1,0:T(8,128)S(1)}, f32[4,896,128]{2,1,0:T(8,128)S(1)}) custom-call(bf16[4,896,256]{2,1,0:T(8,128)(2,1)S(1)} %get-tuple-element.36.refs_0_, bf16[256,128]{1,0:T(8,128)(2,1)S(1)} %get-tuple-element.43.refs_1_, ...), custom_call_target="tpu_custom_call", output_to_operand_aliasing={{0}: (4, {}), {1}: (5, {}), {2}: (6, {})} | custom-call | flops 469762048 | bytes 4000000 | tf_op jit(solution)/shard_map/pallas_call | solution.py:343
  38.5 0.0 collective-permute-done.8.refs_2_
  38.5 2.4 %shard_map.48 = (f32[4,896,128]{2,1,0:T(8,128)S(1)}, f32[4,896,128]{2,1,0:T(8,128)S(1)}, f32[4,896,128]{2,1,0:T(8,128)S(1)}) custom-call(bf16[4,896,256]{2,1,0:T(8,128)(2,1)S(1)} %get-tuple-element.36.refs_0_, bf16[256,128]{1,0:T(8,128)(2,1)S(1)} %get-tuple-element.42.refs_1_, ...), custom_call_target="tpu_custom_call", output_to_operand_aliasing={{0}: (3, {}), {1}: (4, {}), {2}: (5, {})} | custom-call | flops 469762048 | bytes 4000000 | tf_op jit(solution)/shard_map/pallas_call | solution.py:343
  40.8 2.4 %shard_map.49 = (f32[4,896,128]{2,1,0:T(8,128)S(1)}, f32[4,896,128]{2,1,0:T(8,128)S(1)}, f32[4,896,128]{2,1,0:T(8,128)S(1)}) custom-call(bf16[4,896,256]{2,1,0:T(8,128)(2,1)S(1)} %get-tuple-element.36.refs_0_, bf16[256,128]{1,0:T(8,128)(2,1)S(1)} %get-tuple-element.41.refs_1_, ...), custom_call_target="tpu_custom_call", output_to_operand_aliasing={{0}: (4, {}), {1}: (5, {}), {2}: (6, {})} | custom-call | flops 469762048 | bytes 4000000 | tf_op jit(solution)/shard_map/pallas_call | solution.py:343
  43.2 0.0 collective-permute-done.6.refs_2_
  43.2 2.5 %shard_map.50 = (f32[4,896,128]{2,1,0:T(8,128)S(1)}, f32[4,896,128]{2,1,0:T(8,128)S(1)}, f32[4,896,128]{2,1,0:T(8,128)S(1)}) custom-call(bf16[4,896,256]{2,1,0:T(8,128)(2,1)S(1)} %get-tuple-element.36.refs_0_, bf16[256,128]{1,0:T(8,128)(2,1)S(1)} %get-tuple-element.40.refs_1_, ...), custom_call_target="tpu_custom_call", output_to_operand_aliasing={{0}: (3, {}), {1}: (4, {}), {2}: (5, {})} | custom-call | flops 469762048 | bytes 4000000 | tf_op jit(solution)/shard_map/pallas_call | solution.py:343
  45.8 2.4 %shard_map.51 = (f32[4,896,128]{2,1,0:T(8,128)S(1)}, f32[4,896,128]{2,1,0:T(8,128)S(1)}, f32[4,896,128]{2,1,0:T(8,128)S(1)}) custom-call(bf16[4,896,256]{2,1,0:T(8,128)(2,1)S(1)} %get-tuple-element.36.refs_0_, bf16[256,128]{1,0:T(8,128)(2,1)S(1)} %get-tuple-element.39.refs_1_, ...), custom_call_target="tpu_custom_call", output_to_operand_aliasing={{0}: (4, {}), {1}: (5, {}), {2}: (6, {})} | custom-call | flops 469762048 | bytes 4000000 | tf_op jit(solution)/shard_map/pallas_call | solution.py:343
  48.1 0.0 collective-permute-done.5.refs_2_
  48.1 2.5 %shard_map.52 = bf16[128,3584]{1,0:T(8,128)(2,1)} custom-call(bf16[4,896,256]{2,1,0:T(8,128)(2,1)S(1)} %get-tuple-element.36.refs_0_, bf16[256,128]{1,0:T(8,128)(2,1)S(1)} %get-tuple-element.37.refs_1_, bf16[256,1024]{1,0:T(8,128)(2,1)S(1)} %collective-permute-done.5.refs_2_, f32[4,896,128]{2,1,0:T(8,128)S(1)} %get-tuple-element.60.refs_3_, ...), custom_call_target="tpu_custom_call" | custom-call | flops 469762048 | bytes 4000000 | tf_op jit(solution)/shard_map/pallas_call | solution.py:343
  (4 shorter events, 0.1 us)
Async XLA Ops:
  1.1 7.2 %collective-permute-start = (bf16[128,1024]{1,0:T(8,128)(2,1)S(1)}, bf16[128,1024]{1,0:T(8,128)(2,1)S(1)}, u32[]{:S(2)}, u32[]{:S(2)}) collective-permute-start(bf16[128,1024]{1,0:T(8,128)(2,1)S(1)} %get-tuple-element.38.refs_2_), channel_id=1, source_target_pairs={{0,8},{2,10},{4,12},{6,14},{8,16},{10,18},{12,20},{14,22},{16,24},... | collective-permute-start | bytes 786440 | tf_op jit(solution)/shard_map/ppermute | solution.py:31
  8.4 6.3 %collective-permute-start.1 = (bf16[128,1024]{1,0:T(8,128)(2,1)S(1)}, bf16[128,1024]{1,0:T(8,128)(2,1)S(1)}, u32[]{:S(2)}, u32[]{:S(2)}) collective-permute-start(bf16[128,1024]{1,0:T(8,128)(2,1)S(1)} %collective-permute-done.a_ref.refs_2_), channel_id=1, source_target_pairs={{0,2},{2,0},{4,6},{6,4},{8,16},{10,18},{12,20},{14,22},{16,24},{18... | collective-permute-start | bytes 786440 | tf_op jit(solution)/shard_map/ppermute | solution.py:31
  9.7 6.3 %collective-permute-start.3 = (bf16[128,1024]{1,0:T(8,128)(2,1)S(1)}, bf16[128,1024]{1,0:T(8,128)(2,1)S(1)}, u32[]{:S(2)}, u32[]{:S(2)}) collective-permute-start(bf16[128,1024]{1,0:T(8,128)(2,1)S(1)} %collective-permute-done.a_ref.refs_2_), channel_id=1, source_target_pairs={{0,4},{2,6},{4,0},{6,2},{8,12},{10,14},{12,8},{14,10},{16,20},{18,... | collective-permute-start | bytes 786440 | tf_op jit(solution)/shard_map/ppermute | solution.py:31
  10.9 16.1 %collective-permute-start.7 = (bf16[128,1024]{1,0:T(8,128)(2,1)S(1)}, bf16[128,1024]{1,0:T(8,128)(2,1)S(1)}, u32[]{:S(2)}, u32[]{:S(2)}) collective-permute-start(bf16[128,1024]{1,0:T(8,128)(2,1)S(1)} %get-tuple-element.38.refs_2_), channel_id=1, source_target_pairs={{0,4},{2,6},{4,0},{6,2},{8,12},{10,14},{12,8},{14,10},{16,20},{18,... | collective-permute-start | bytes 786440 | tf_op jit(solution)/shard_map/ppermute | solution.py:31
  14.7 15.6 %collective-permute-start.2 = (bf16[128,1024]{1,0:T(8,128)(2,1)S(1)}, bf16[128,1024]{1,0:T(8,128)(2,1)S(1)}, u32[]{:S(2)}, u32[]{:S(2)}) collective-permute-start(bf16[128,1024]{1,0:T(8,128)(2,1)S(1)} %collective-permute-done.1.a_ref.refs_2_), channel_id=1, source_target_pairs={{0,2},{2,0},{4,6},{6,4},{8,10},{10,8},{12,14},{14,12},{16,20},{18,... | collective-permute-start | bytes 786440 | tf_op jit(solution)/shard_map/ppermute | solution.py:31
  16.0 14.4 %collective-permute-start.4 = (bf16[128,1024]{1,0:T(8,128)(2,1)S(1)}, bf16[128,1024]{1,0:T(8,128)(2,1)S(1)}, u32[]{:S(2)}, u32[]{:S(2)}) collective-permute-start(bf16[128,1024]{1,0:T(8,128)(2,1)S(1)} %collective-permute-done.3.b_ref.refs_3_), channel_id=1, source_target_pairs={{0,2},{2,0},{4,6},{6,4},{8,16},{10,18},{12,8},{14,10},{16,24},{18,... | collective-permute-start | bytes 786440 | tf_op jit(solution)/shard_map/ppermute | solution.py:31
  27.0 11.5 %collective-permute-start.8 = (bf16[256,1024]{1,0:T(8,128)(2,1)S(1)}, bf16[256,1024]{1,0:T(8,128)(2,1)S(1)}, u32[]{:S(2)}, u32[]{:S(2)}) collective-permute-start(bf16[256,1024]{1,0:T(8,128)(2,1)S(1)} %join.5), channel_id=1, source_target_pairs={{0,2},{2,0},{4,6},{6,4},{8,10},{10,8},{12,14},{14,12},{16,18},{18,... | collective-permute-start | bytes 1572872 | tf_op jit(solution)/shard_map/ppermute | solution.py:31
  29.8 13.4 %collective-permute-start.6 = (bf16[256,1024]{1,0:T(8,128)(2,1)S(1)}, bf16[256,1024]{1,0:T(8,128)(2,1)S(1)}, u32[]{:S(2)}, u32[]{:S(2)}) collective-permute-start(bf16[256,1024]{1,0:T(8,128)(2,1)S(1)} %join.4), channel_id=1, source_target_pairs={{0,2},{2,0},{4,6},{6,4},{8,10},{10,8},{12,14},{14,12},{16,18},{18,... | collective-permute-start | bytes 1572872 | tf_op jit(solution)/shard_map/ppermute | solution.py:31
  29.9 5.0 %collective-permute-start.9 = (bf16[128,1024]{1,0:T(8,128)(2,1)S(1)}, bf16[128,1024]{1,0:T(8,128)(2,1)S(1)}, u32[]{:S(2)}, u32[]{:S(2)}) collective-permute-start(bf16[128,1024]{1,0:T(8,128)(2,1)S(1)} %get-tuple-element.38.refs_2_), channel_id=1, source_target_pairs={{0,2},{2,0},{4,6},{6,4},{8,10},{10,8},{12,14},{14,12},{16,18},{18,... | collective-permute-start | bytes 786440 | tf_op jit(solution)/shard_map/ppermute | solution.py:31
  30.4 17.7 %collective-permute-start.5 = (bf16[256,1024]{1,0:T(8,128)(2,1)S(1)}, bf16[256,1024]{1,0:T(8,128)(2,1)S(1)}, u32[]{:S(2)}, u32[]{:S(2)}) collective-permute-start(bf16[256,1024]{1,0:T(8,128)(2,1)S(1)} %join.3), channel_id=1, source_target_pairs={{0,2},{2,0},{4,6},{6,4},{8,10},{10,8},{12,14},{14,12},{16,18},{18,... | collective-permute-start | bytes 1572872 | tf_op jit(solution)/shard_map/ppermute | solution.py:31

commit v6 on v5

--- a/solution.py
+++ b/solution.py
@@ -38,18 +38,14 @@
 def relay(own, chip_reach, kernel):
     count = len(own.source)
 
-    def around(shift, first, side=None):
+    def around(shift, first, narrow=False):
         span = count - first
         pairs = {}
         for i in range(count):
-            if i < first or (side is not None and i & 2):
+            if i < first or (narrow and i & 2):
                 pairs[i] = i ^ 1
             else:
                 pairs[i] = first + (i - first + shift) % span
-        if side is not None:
-            for core in range(2):
-                head, last = first + core, count - shift + core
-                pairs[last], pairs[head + 2] = head + 2, head
         assert sorted(pairs.values()) == list(range(count))
         return sorted(pairs.items())
 
@@ -72,7 +68,7 @@
         a = here
     stage = full + 1
     if odd:
-        c = b.move(around(4, 4 * (full - 1), 0))
+        c = b.move(around(4, 4 * (full - 1), True))
         pieces = [a.move(around(2, 4 * full)), c]
     else:
         pieces = [a.move(across)]
@@ -248,6 +244,26 @@
     tall = GROUP * rows
     key_lane = lanes_iota((count * rows, HEAD_DIM), 1)
     ones = jnp.ones((count * rows, HEAD_DIM), jnp.bfloat16)
+
+    def write(g, at, acc, total):
+        head, row = g * GROUP + at // rows, at % rows
+        cols = slice(head * HEAD_DIM, (head + 1) * HEAD_DIM)
+        out_ref[row:row + SLAB, cols] = (acc / total).astype(jnp.bfloat16)
+
+    def send(g):
+        cols = pl.ds(g * GROUP * HEAD_DIM, GROUP * HEAD_DIM)
+        copy = pltpu.make_async_copy(out_ref.at[:, cols], out_hbm.at[:, cols], sems.at[g])
+        copy.start()
+        return copy
+
+    def finish(result):
+        copies = []
+        for g in range(KV_HEADS):
+            for at in range(0, tall, SLAB):
+                write(g, at, *result(g, slice(at, at + SLAB)))
+            copies.append(send(g))
+        for copy in copies:
+            copy.wait()
 
     def body():
         def score(g):
@@ -299,27 +315,32 @@
                     acc = acc_in[g, here] * shrink + acc
                     total = sum_in[g, here] * shrink + total
                 if last:
-                    head, row = g * GROUP + at // rows, at % rows
-                    cols = slice(head * HEAD_DIM, (head + 1) * HEAD_DIM)
-                    out_ref[row:row + SLAB, cols] = (acc / total).astype(jnp.bfloat16)
+                    write(g, at, acc, total)
                 else:
                     acc_out[g, here] = acc
                     sum_out[g, here] = total
             if last:
-                cols = pl.ds(g * GROUP * HEAD_DIM, GROUP * HEAD_DIM)
-                copies.append(pltpu.make_async_copy(out_ref.at[:, cols], out_hbm.at[:, cols], sems.at[g]))
-                copies[-1].start()
+                copies.append(send(g))
         for copy in copies:
             copy.wait()
 
-    if first or last:
+    if first:
         body()
-    else:
-        me = lax.axis_index("seq")
-        wanted = jnp.bool_(False)
-        for i in users:
-            wanted |= me == i
-        pl.when(wanted)(body)
+        return
+    me = lax.axis_index("seq")
+    wanted = jnp.bool_(False)
+    for i in users:
+        wanted |= me == i
+    pl.when(wanted)(body)
+
+    @pl.when(jnp.logical_not(wanted))
+    def _():
+        if last:
+            finish(lambda g, here: (acc_in[g, here], sum_in[g, here]))
+        else:
+            max_out[...] = max_in[...]
+            sum_out[...] = sum_in[...]
+            acc_out[...] = acc_in[...]
 
 
 def attend(pieces, docs, places, q, mask, state=None, last=False):
@@ -346,7 +367,6 @@
         in_specs=[vmem] * len(args),
         out_specs=[pl.BlockSpec(memory_space=pltpu.HBM)] if last else [vmem] * len(out_shape),
         scratch_shapes=scratch,
-        input_output_aliases={} if first or last else {2 + len(pieces) + n: n for n in range(3)},
         cost_estimate=pl.CostEstimate(
             flops=4 * rows * HEADS * count * rows * HEAD_DIM,
             bytes_accessed=4 * 10**6,

time: 50.9 us -> 47.4 us (0.931)
  Pallas kernels: 19 us -> 15.5 us
    pallas_call x7, Pallas kernels: 15.7 us -> 12.2 us  [attend(): pl.pallas_call(functools.partial(attend_kernel, count, len(pieces), docs,...]
  transfers between devices with their start and end apart: 10 -> 10, of which waited for: 3 -> 3; matrix products, arithmetic and copies ran while one was open for 0% -> 0% of each run, Pallas kernels for 30% -> 25%
where the time goes in v6:
time: 47.4 us; the launch traced here: 47.3 us
  waiting for transfers between devices  19.2 us (41%)
  Pallas kernels  15.5 us (33%)
  starting transfers between devices  12.3 us (26%)
    ppermute x10, waiting for transfers between devices, move(): lax.ppermute(self.data, 'seq', pairs)  19.2 us
    ppermute x10, starting transfers between devices, move(): lax.ppermute(self.data, 'seq', pairs)  12.3 us
    pallas_call x7, Pallas kernels, attend(): pl.pallas_call(functools.partial(attend_kernel, count, len(pieces), docs,...  12.2 us
    pallas_call x1, Pallas kernels, turn_queries(): pl.pallas_call(functools.partial(turn_kernel, places, lengths.shape[0]),...  2.06 us
    pallas_call x1, Pallas kernels, prepare(): pl.pallas_call(prepare_kernel, out_shape=[jax.ShapeDtypeStruct((rows, 2 *...  1.13 us
  transfers between devices with their start and end apart: 10, of which 3 were waited for; matrix products, arithmetic and copies ran while one was open for 0% of the time, Pallas kernels for 25%

profile of v6, /device:TPU:17, one launch (start us, length us, event | category | flops | bytes accessed | tf_op | source)
XLA Modules:
  0.0 47.3 jit_solution(6219784177299651019)
XLA Ops:
  0.0 1.1 %prepare.1 = (bf16[128,1024]{1,0:T(8,128)(2,1)S(1)}, f32[128,128]{1,0:T(8,128)S(1)}, f32[128,128]{1,0:T(8,128)S(1)}) custom-call(f32[1,128]{1,0:T(1,128)S(1)} %fusion.2.freq_ref, s32[8]{0:T(128)} %lengths_hbm.3, bf16[128,512]{1,0:T(8,128)(2,1)} %k_hbm.1, bf16[128,512]{1,0:T(8,128)(2,1)} %v_hbm.1), custom_call_target="tpu_custom_call" | custom-call | flops 1000000 | bytes 600000 | tf_op jit(solution)/shard_map/prepare/pallas_call | solution.py:136
  1.1 1.3 %collective-permute-start = (bf16[128,1024]{1,0:T(8,128)(2,1)S(1)}, bf16[128,1024]{1,0:T(8,128)(2,1)S(1)}, u32[]{:S(2)}, u32[]{:S(2)}) collective-permute-start(bf16[128,1024]{1,0:T(8,128)(2,1)S(1)} %get-tuple-element.38.refs_2_), channel_id=1, source_target_pairs={{0,8},{2,10},{4,12},{6,14},{8,16},{10,18},{12,20},{14,22},{16,24},... | collective-permute-start | bytes 786440 | tf_op jit(solution)/shard_map/ppermute | solution.py:31
  2.5 5.9 %collective-permute-done.a_ref.refs_2_ = bf16[128,1024]{1,0:T(8,128)(2,1)S(1)} collective-permute-done((bf16[128,1024]{1,0:T(8,128)(2,1)S(1)}, bf16[128,1024]{1,0:T(8,128)(2,1)S(1)}, u32[]{:S(2)}, u32[]{:S(2)}) %collective-permute-start) | collective-permute-done | bytes 262176 | tf_op jit(solution)/shard_map/ppermute | solution.py:31
  8.4 1.3 %collective-permute-start.1 = (bf16[128,1024]{1,0:T(8,128)(2,1)S(1)}, bf16[128,1024]{1,0:T(8,128)(2,1)S(1)}, u32[]{:S(2)}, u32[]{:S(2)}) collective-permute-start(bf16[128,1024]{1,0:T(8,128)(2,1)S(1)} %collective-permute-done.a_ref.refs_2_), channel_id=1, source_target_pairs={{0,2},{2,0},{4,6},{6,4},{8,16},{10,18},{12,20},{14,22},{16,24},{18... | collective-permute-start | bytes 786440 | tf_op jit(solution)/shard_map/ppermute | solution.py:31
  9.7 1.2 %collective-permute-start.3 = (bf16[128,1024]{1,0:T(8,128)(2,1)S(1)}, bf16[128,1024]{1,0:T(8,128)(2,1)S(1)}, u32[]{:S(2)}, u32[]{:S(2)}) collective-permute-start(bf16[128,1024]{1,0:T(8,128)(2,1)S(1)} %collective-permute-done.a_ref.refs_2_), channel_id=1, source_target_pairs={{0,4},{2,6},{4,0},{6,2},{8,12},{10,14},{12,8},{14,10},{16,20},{18,... | collective-permute-start | bytes 786440 | tf_op jit(solution)/shard_map/ppermute | solution.py:31
  10.9 0.2 collective-permute-start.7
  11.2 3.6 %collective-permute-done.1.a_ref.refs_2_ = bf16[128,1024]{1,0:T(8,128)(2,1)S(1)} collective-permute-done((bf16[128,1024]{1,0:T(8,128)(2,1)S(1)}, bf16[128,1024]{1,0:T(8,128)(2,1)S(1)}, u32[]{:S(2)}, u32[]{:S(2)}) %collective-permute-start.1) | collective-permute-done | bytes 262176 | tf_op jit(solution)/shard_map/ppermute | solution.py:31
  14.7 1.2 %collective-permute-start.2 = (bf16[128,1024]{1,0:T(8,128)(2,1)S(1)}, bf16[128,1024]{1,0:T(8,128)(2,1)S(1)}, u32[]{:S(2)}, u32[]{:S(2)}) collective-permute-start(bf16[128,1024]{1,0:T(8,128)(2,1)S(1)} %collective-permute-done.1.a_ref.refs_2_), channel_id=1, source_target_pairs={{0,2},{2,0},{4,6},{6,4},{8,10},{10,8},{12,14},{14,12},{16,20},{18,... | collective-permute-start | bytes 786440 | tf_op jit(solution)/shard_map/ppermute | solution.py:31
  16.0 0.0 collective-permute-done.3.b_ref.refs_3_
  16.0 1.3 %collective-permute-start.4 = (bf16[128,1024]{1,0:T(8,128)(2,1)S(1)}, bf16[128,1024]{1,0:T(8,128)(2,1)S(1)}, u32[]{:S(2)}, u32[]{:S(2)}) collective-permute-start(bf16[128,1024]{1,0:T(8,128)(2,1)S(1)} %collective-permute-done.3.b_ref.refs_3_), channel_id=1, source_target_pairs={{0,2},{2,0},{4,6},{6,4},{8,16},{10,18},{12,14},{14,12},{16,24},{18... | collective-permute-start | bytes 786440 | tf_op jit(solution)/shard_map/ppermute | solution.py:31
  17.3 9.7 %collective-permute-done.7.b_ref.refs_3_ = bf16[128,1024]{1,0:T(8,128)(2,1)S(1)} collective-permute-done((bf16[128,1024]{1,0:T(8,128)(2,1)S(1)}, bf16[128,1024]{1,0:T(8,128)(2,1)S(1)}, u32[]{:S(2)}, u32[]{:S(2)}) %collective-permute-start.7) | collective-permute-done | bytes 262176 | tf_op jit(solution)/shard_map/ppermute | solution.py:31
  27.0 2.7 %collective-permute-start.8 = (bf16[256,1024]{1,0:T(8,128)(2,1)S(1)}, bf16[256,1024]{1,0:T(8,128)(2,1)S(1)}, u32[]{:S(2)}, u32[]{:S(2)}) collective-permute-start(bf16[256,1024]{1,0:T(8,128)(2,1)S(1)} %join.5), channel_id=1, source_target_pairs={{0,2},{2,0},{4,6},{6,4},{8,10},{10,8},{12,14},{14,12},{16,18},{18,... | collective-permute-start | bytes 1572872 | tf_op jit(solution)/shard_map/ppermute | solution.py:31
  29.8 0.1 collective-permute-start.6
  29.9 0.5 %collective-permute-start.9 = (bf16[128,1024]{1,0:T(8,128)(2,1)S(1)}, bf16[128,1024]{1,0:T(8,128)(2,1)S(1)}, u32[]{:S(2)}, u32[]{:S(2)}) collective-permute-start(bf16[128,1024]{1,0:T(8,128)(2,1)S(1)} %get-tuple-element.38.refs_2_), channel_id=1, source_target_pairs={{0,2},{2,0},{4,6},{6,4},{8,10},{10,8},{12,14},{14,12},{16,18},{18,... | collective-permute-start | bytes 786440 | tf_op jit(solution)/shard_map/ppermute | solution.py:31
  30.4 0.0 collective-permute-done.2.a_ref.refs_2_
  30.4 0.0 collective-permute-done.4.b_ref.refs_3_
  30.4 2.4 %collective-permute-start.5 = (bf16[256,1024]{1,0:T(8,128)(2,1)S(1)}, bf16[256,1024]{1,0:T(8,128)(2,1)S(1)}, u32[]{:S(2)}, u32[]{:S(2)}) collective-permute-start(bf16[256,1024]{1,0:T(8,128)(2,1)S(1)} %join.3), channel_id=1, source_target_pairs={{0,2},{2,0},{4,6},{6,4},{8,10},{10,8},{12,14},{14,12},{16,18},{18,... | collective-permute-start | bytes 1572872 | tf_op jit(solution)/shard_map/ppermute | solution.py:31
  32.8 2.1 %turn_queries.1 = (bf16[4,896,256]{2,1,0:T(8,128)(2,1)S(1)}, bf16[256,128]{1,0:T(8,128)(2,1)S(1)}, bf16[256,128]{1,0:T(8,128)(2,1)S(1)}, bf16[256,128]{1,0:T(8,1...) custom-call(s32[8]{0:T(128)} %lengths_hbm.3, ...), custom_call_target="tpu_custom_call" | custom-call | flops 100000000 | bytes 4000000 | tf_op jit(solution)/shard_map/turn_queries/pallas_call | solution.py:210
  34.8 0.0 collective-permute-done.9.refs_3_
  34.8 1.2 %shard_map.46 = (f32[4,896,128]{2,1,0:T(8,128)S(1)}, f32[4,896,128]{2,1,0:T(8,128)S(1)}, f32[4,896,128]{2,1,0:T(8,128)S(1)}) custom-call(bf16[4,896,256]{2,1,0:T(8,128)(2,1)S(1)} %get-tuple-element.36.refs_0_, bf16[256,128]{1,0:T(8,128)(2,1)S(1)} %get-tuple-element.44.refs_1_, bf16[128,1024]{1,0:T(8,128)(2,1)S(1)} %get-tuple-element.38.refs_2_, ...), custom_call_target="tpu_custom_call" | custom-call | flops 469762048 | bytes 4000000 | tf_op jit(solution)/shard_map/pallas_call | solution.py:364
  36.1 1.6 %shard_map.47 = (f32[4,896,128]{2,1,0:T(8,128)S(1)}, f32[4,896,128]{2,1,0:T(8,128)S(1)}, f32[4,896,128]{2,1,0:T(8,128)S(1)}) custom-call(bf16[4,896,256]{2,1,0:T(8,128)(2,1)S(1)} %get-tuple-element.36.refs_0_, bf16[256,128]{1,0:T(8,128)(2,1)S(1)} %get-tuple-element.43.refs_1_, bf16[128,1024]{1,0:T(8,128)(2,1)S(1)} %collective-permute-done.a_ref.refs_2_, ...), custom_call_target="tpu_custom_call" | custom-call | flops 469762048 | bytes 4000000 | tf_op jit(solution)/shard_map/pallas_call | solution.py:364
  37.7 0.0 collective-permute-done.8.refs_2_
  37.8 1.6 %shard_map.48 = (f32[4,896,128]{2,1,0:T(8,128)S(1)}, f32[4,896,128]{2,1,0:T(8,128)S(1)}, f32[4,896,128]{2,1,0:T(8,128)S(1)}) custom-call(bf16[4,896,256]{2,1,0:T(8,128)(2,1)S(1)} %get-tuple-element.36.refs_0_, bf16[256,128]{1,0:T(8,128)(2,1)S(1)} %get-tuple-element.42.refs_1_, bf16[256,1024]{1,0:T(8,128)(2,1)S(1)} %collective-permute-done.8.refs_2_, ...), custom_call_target="tpu_custom_call" | custom-call | flops 469762048 | bytes 4000000 | tf_op jit(solution)/shard_map/pallas_call | solution.py:364
  39.4 1.6 %shard_map.49 = (f32[4,896,128]{2,1,0:T(8,128)S(1)}, f32[4,896,128]{2,1,0:T(8,128)S(1)}, f32[4,896,128]{2,1,0:T(8,128)S(1)}) custom-call(bf16[4,896,256]{2,1,0:T(8,128)(2,1)S(1)} %get-tuple-element.36.refs_0_, bf16[256,128]{1,0:T(8,128)(2,1)S(1)} %get-tuple-element.41.refs_1_, bf16[128,1024]{1,0:T(8,128)(2,1)S(1)} %collective-permute-done.1.a_ref.refs_2_, ...), custom_call_target="tpu_custom_call" | custom-call | flops 469762048 | bytes 4000000 | tf_op jit(solution)/shard_map/pallas_call | solution.py:364
  41.1 0.0 collective-permute-done.6.refs_2_
  41.1 1.6 %shard_map.50 = (f32[4,896,128]{2,1,0:T(8,128)S(1)}, f32[4,896,128]{2,1,0:T(8,128)S(1)}, f32[4,896,128]{2,1,0:T(8,128)S(1)}) custom-call(bf16[4,896,256]{2,1,0:T(8,128)(2,1)S(1)} %get-tuple-element.36.refs_0_, bf16[256,128]{1,0:T(8,128)(2,1)S(1)} %get-tuple-element.40.refs_1_, bf16[256,1024]{1,0:T(8,128)(2,1)S(1)} %collective-permute-done.6.refs_2_, ...), custom_call_target="tpu_custom_call" | custom-call | flops 469762048 | bytes 4000000 | tf_op jit(solution)/shard_map/pallas_call | solution.py:364
  42.7 1.8 %shard_map.51 = (f32[4,896,128]{2,1,0:T(8,128)S(1)}, f32[4,896,128]{2,1,0:T(8,128)S(1)}, f32[4,896,128]{2,1,0:T(8,128)S(1)}) custom-call(bf16[4,896,256]{2,1,0:T(8,128)(2,1)S(1)} %get-tuple-element.36.refs_0_, bf16[256,128]{1,0:T(8,128)(2,1)S(1)} %get-tuple-element.39.refs_1_, bf16[128,1024]{1,0:T(8,128)(2,1)S(1)} %collective-permute-done.2.a_ref.refs_2_, ...), custom_call_target="tpu_custom_call" | custom-call | flops 469762048 | bytes 4000000 | tf_op jit(solution)/shard_map/pallas_call | solution.py:364
  44.6 0.0 collective-permute-done.5.refs_2_
  44.6 2.5 %shard_map.52 = bf16[128,3584]{1,0:T(8,128)(2,1)} custom-call(bf16[4,896,256]{2,1,0:T(8,128)(2,1)S(1)} %get-tuple-element.36.refs_0_, bf16[256,128]{1,0:T(8,128)(2,1)S(1)} %get-tuple-element.37.refs_1_, bf16[256,1024]{1,0:T(8,128)(2,1)S(1)} %collective-permute-done.5.refs_2_, f32[4,896,128]{2,1,0:T(8,128)S(1)} %get-tuple-element.60.refs_3_, ...), custom_call_target="tpu_custom_call" | custom-call | flops 469762048 | bytes 4000000 | tf_op jit(solution)/shard_map/pallas_call | solution.py:364
  (4 shorter events, 0.1 us)
Async XLA Ops:
  1.1 7.2 %collective-permute-start = (bf16[128,1024]{1,0:T(8,128)(2,1)S(1)}, bf16[128,1024]{1,0:T(8,128)(2,1)S(1)}, u32[]{:S(2)}, u32[]{:S(2)}) collective-permute-start(bf16[128,1024]{1,0:T(8,128)(2,1)S(1)} %get-tuple-element.38.refs_2_), channel_id=1, source_target_pairs={{0,8},{2,10},{4,12},{6,14},{8,16},{10,18},{12,20},{14,22},{16,24},... | collective-permute-start | bytes 786440 | tf_op jit(solution)/shard_map/ppermute | solution.py:31
  8.4 6.3 %collective-permute-start.1 = (bf16[128,1024]{1,0:T(8,128)(2,1)S(1)}, bf16[128,1024]{1,0:T(8,128)(2,1)S(1)}, u32[]{:S(2)}, u32[]{:S(2)}) collective-permute-start(bf16[128,1024]{1,0:T(8,128)(2,1)S(1)} %collective-permute-done.a_ref.refs_2_), channel_id=1, source_target_pairs={{0,2},{2,0},{4,6},{6,4},{8,16},{10,18},{12,20},{14,22},{16,24},{18... | collective-permute-start | bytes 786440 | tf_op jit(solution)/shard_map/ppermute | solution.py:31
  9.7 6.3 %collective-permute-start.3 = (bf16[128,1024]{1,0:T(8,128)(2,1)S(1)}, bf16[128,1024]{1,0:T(8,128)(2,1)S(1)}, u32[]{:S(2)}, u32[]{:S(2)}) collective-permute-start(bf16[128,1024]{1,0:T(8,128)(2,1)S(1)} %collective-permute-done.a_ref.refs_2_), channel_id=1, source_target_pairs={{0,4},{2,6},{4,0},{6,2},{8,12},{10,14},{12,8},{14,10},{16,20},{18,... | collective-permute-start | bytes 786440 | tf_op jit(solution)/shard_map/ppermute | solution.py:31
  10.9 16.1 %collective-permute-start.7 = (bf16[128,1024]{1,0:T(8,128)(2,1)S(1)}, bf16[128,1024]{1,0:T(8,128)(2,1)S(1)}, u32[]{:S(2)}, u32[]{:S(2)}) collective-permute-start(bf16[128,1024]{1,0:T(8,128)(2,1)S(1)} %get-tuple-element.38.refs_2_), channel_id=1, source_target_pairs={{0,4},{2,6},{4,0},{6,2},{8,12},{10,14},{12,8},{14,10},{16,20},{18,... | collective-permute-start | bytes 786440 | tf_op jit(solution)/shard_map/ppermute | solution.py:31
  14.7 15.6 %collective-permute-start.2 = (bf16[128,1024]{1,0:T(8,128)(2,1)S(1)}, bf16[128,1024]{1,0:T(8,128)(2,1)S(1)}, u32[]{:S(2)}, u32[]{:S(2)}) collective-permute-start(bf16[128,1024]{1,0:T(8,128)(2,1)S(1)} %collective-permute-done.1.a_ref.refs_2_), channel_id=1, source_target_pairs={{0,2},{2,0},{4,6},{6,4},{8,10},{10,8},{12,14},{14,12},{16,20},{18,... | collective-permute-start | bytes 786440 | tf_op jit(solution)/shard_map/ppermute | solution.py:31
  16.0 14.4 %collective-permute-start.4 = (bf16[128,1024]{1,0:T(8,128)(2,1)S(1)}, bf16[128,1024]{1,0:T(8,128)(2,1)S(1)}, u32[]{:S(2)}, u32[]{:S(2)}) collective-permute-start(bf16[128,1024]{1,0:T(8,128)(2,1)S(1)} %collective-permute-done.3.b_ref.refs_3_), channel_id=1, source_target_pairs={{0,2},{2,0},{4,6},{6,4},{8,16},{10,18},{12,14},{14,12},{16,24},{18... | collective-permute-start | bytes 786440 | tf_op jit(solution)/shard_map/ppermute | solution.py:31
  27.0 10.7 %collective-permute-start.8 = (bf16[256,1024]{1,0:T(8,128)(2,1)S(1)}, bf16[256,1024]{1,0:T(8,128)(2,1)S(1)}, u32[]{:S(2)}, u32[]{:S(2)}) collective-permute-start(bf16[256,1024]{1,0:T(8,128)(2,1)S(1)} %join.5), channel_id=1, source_target_pairs={{0,2},{2,0},{4,6},{6,4},{8,10},{10,8},{12,14},{14,12},{16,18},{18,... | collective-permute-start | bytes 1572872 | tf_op jit(solution)/shard_map/ppermute | solution.py:31
  29.8 11.3 %collective-permute-start.6 = (bf16[256,1024]{1,0:T(8,128)(2,1)S(1)}, bf16[256,1024]{1,0:T(8,128)(2,1)S(1)}, u32[]{:S(2)}, u32[]{:S(2)}) collective-permute-start(bf16[256,1024]{1,0:T(8,128)(2,1)S(1)} %join.4), channel_id=1, source_target_pairs={{0,2},{2,0},{4,6},{6,4},{8,10},{10,8},{12,14},{14,12},{16,18},{18,... | collective-permute-start | bytes 1572872 | tf_op jit(solution)/shard_map/ppermute | solution.py:31
  29.9 5.0 %collective-permute-start.9 = (bf16[128,1024]{1,0:T(8,128)(2,1)S(1)}, bf16[128,1024]{1,0:T(8,128)(2,1)S(1)}, u32[]{:S(2)}, u32[]{:S(2)}) collective-permute-start(bf16[128,1024]{1,0:T(8,128)(2,1)S(1)} %get-tuple-element.38.refs_2_), channel_id=1, source_target_pairs={{0,2},{2,0},{4,6},{6,4},{8,10},{10,8},{12,14},{14,12},{16,18},{18,... | collective-permute-start | bytes 786440 | tf_op jit(solution)/shard_map/ppermute | solution.py:31
  30.4 14.2 %collective-permute-start.5 = (bf16[256,1024]{1,0:T(8,128)(2,1)S(1)}, bf16[256,1024]{1,0:T(8,128)(2,1)S(1)}, u32[]{:S(2)}, u32[]{:S(2)}) collective-permute-start(bf16[256,1024]{1,0:T(8,128)(2,1)S(1)} %join.3), channel_id=1, source_target_pairs={{0,2},{2,0},{4,6},{6,4},{8,10},{10,8},{12,14},{14,12},{16,18},{18,... | collective-permute-start | bytes 1572872 | tf_op jit(solution)/shard_map/ppermute | solution.py:31

commit v7 on v6

--- a/solution.py
+++ b/solution.py
@@ -38,7 +38,7 @@
 def relay(own, chip_reach, kernel):
     count = len(own.source)
 
-    def around(shift, first, narrow=False):
+    def around(shift, first, narrow=False, via=False):
         span = count - first
         pairs = {}
         for i in range(count):
@@ -46,6 +46,10 @@
                 pairs[i] = i ^ 1
             else:
                 pairs[i] = first + (i - first + shift) % span
+        if via:
+            for core in range(2):
+                last, middle = count - shift + core, first - 2 + core
+                pairs[last], pairs[middle] = middle, first + core
         assert sorted(pairs.values()) == list(range(count))
         return sorted(pairs.items())
 
@@ -223,7 +227,7 @@
     )(in_hbm(lengths), in_hbm(queries), cosine, sine)
 
 
-def attend_kernel(count, operands, docs, first, last, users, *refs):
+def attend_kernel(count, operands, docs, first, last, users, early, devices, *refs):
     refs = list(refs)
     take = lambda n: [refs.pop(0) for _ in range(n)]
     q_ref, mask_ref = take(2)
@@ -231,12 +235,15 @@
     if not first:
         max_in, sum_in, acc_in = take(3)
     if last:
-        (out_ref,) = take(1)
+        take(1)
+        (out_hbm,) = take(1)
     else:
         max_out, sum_out, acc_out = take(3)
+        if early:
+            (out_hbm,) = take(1)
     score_ref, shrink_ref = take(2)
-    if last:
-        out_hbm, (out_ref, sems) = out_ref, take(2)
+    if last or early:
+        out_ref, sems = take(2)
 
     rows = score_ref.shape[2] // count
     kv_refs = [r.at[n:n + rows] for r in kv_refs for n in range(0, r.shape[0], rows)]
@@ -328,44 +335,60 @@
         body()
         return
     me = lax.axis_index("seq")
-    wanted = jnp.bool_(False)
-    for i in users:
-        wanted |= me == i
-    pl.when(wanted)(body)
-
-    @pl.when(jnp.logical_not(wanted))
-    def _():
-        if last:
-            finish(lambda g, here: (acc_in[g, here], sum_in[g, here]))
-        else:
+
+    def among(devices):
+        found = jnp.bool_(False)
+        for i in devices:
+            found |= me == i
+        return found
+
+    pl.when(among(users))(body)
+    if not last:
+
+        @pl.when(among([i for i in range(devices) if i not in users and i not in early]))
+        def _():
             max_out[...] = max_in[...]
             sum_out[...] = sum_in[...]
             acc_out[...] = acc_in[...]
 
-
-def attend(pieces, docs, places, q, mask, state=None, last=False):
+    if last or early:
+        ending = [i for i in range(devices) if i not in users and i not in early] if last else early
+
+        @pl.when(among(ending))
+        def _():
+            finish(lambda g, here: (acc_in[g, here], sum_in[g, here]))
+
+
+def users_of(places):
+    return [i for i in range(len(places[0])) if any(bases[i] != NOWHERE for bases in places)]
+
+
+def attend(pieces, docs, places, q, mask, state=None, last=False, early=()):
     first = state is None
     count = len(places)
     rows = q.shape[1] // GROUP
     stacked = (KV_HEADS, GROUP * rows, HEAD_DIM)
     vmem = pl.BlockSpec(memory_space=pltpu.VMEM)
     args = [q, mask] + pieces + ([] if first else list(state))
+    result = jax.ShapeDtypeStruct((rows, HEADS * HEAD_DIM), jnp.bfloat16)
     if last:
-        out_shape = [jax.ShapeDtypeStruct((rows, HEADS * HEAD_DIM), jnp.bfloat16)]
+        out_shape = [result]
     else:
-        out_shape = [jax.ShapeDtypeStruct(stacked, jnp.float32)] * 3
+        out_shape = [jax.ShapeDtypeStruct(stacked, jnp.float32)] * 3 + ([result] if early else [])
     scratch = [
         pltpu.VMEM((2, GROUP * rows, count * rows), jnp.float32),
         pltpu.VMEM((2, GROUP * rows, HEAD_DIM), jnp.float32),
     ]
-    if last:
+    if last or early:
         scratch += [pltpu.VMEM((rows, HEADS * HEAD_DIM), jnp.bfloat16), pltpu.SemaphoreType.DMA((KV_HEADS,))]
-    users = [i for i in range(len(places[0])) if any(bases[i] != NOWHERE for bases in places)]
+    hbm = pl.BlockSpec(memory_space=pltpu.HBM)
+    users = users_of(places)
     return pl.pallas_call(
-        functools.partial(attend_kernel, count, len(pieces), docs, first, last, users),
+        functools.partial(attend_kernel, count, len(pieces), docs, first, last, users, early, len(places[0])),
         out_shape=out_shape,
-        in_specs=[vmem] * len(args),
-        out_specs=[pl.BlockSpec(memory_space=pltpu.HBM)] if last else [vmem] * len(out_shape),
+        in_specs=[hbm if last and n == len(args) - 1 else vmem for n in range(len(args))],
+        out_specs=[hbm if x is result else vmem for x in out_shape],
+        input_output_aliases={len(args) - 1: 0} if last else {},
         scratch_shapes=scratch,
         cost_estimate=pl.CostEstimate(
             flops=4 * rows * HEADS * count * rows * HEAD_DIM,
@@ -435,10 +458,14 @@
     masks = dict(zip(places, masks))
     docs = doc_lengths.shape[0]
     held = {"state": None}
+    before_last = list(places)[-2]
+    busy = users_of(places[before_last]) + users_of(places["last"])
+    early = [i for i in range(count) if i not in busy]
 
     def kernel(name, pieces, last=False):
         data = [p.data for p in pieces]
-        held["state"] = attend(data, docs, places[name], q, masks[name], held["state"], last)
+        ends = early if last or name == before_last else ()
+        held["state"] = attend(data, docs, places[name], q, masks[name], held["state"], last, ends)
 
     relay(Held(own, source), chip_reach, kernel)
     return held["state"][0]

time: 47.4 us -> 47.5 us (level)
  the two profiles are of different devices: /device:TPU:17 before, /device:TPU:19 now
where the time goes in v7:
time: 47.5 us; the launch traced here: 47.3 us
  waiting for transfers between devices  19.2 us (40%)
  Pallas kernels  15.5 us (33%)
  starting transfers between devices  12.3 us (26%)
    ppermute x10, waiting for transfers between devices, move(): lax.ppermute(self.data, 'seq', pairs)  19.2 us
    ppermute x10, starting transfers between devices, move(): lax.ppermute(self.data, 'seq', pairs)  12.3 us
    pallas_call x7, Pallas kernels, attend(): pl.pallas_call(functools.partial(attend_kernel, count, len(pieces), docs,...  12.2 us
    pallas_call x1, Pallas kernels, turn_queries(): pl.pallas_call(functools.partial(turn_kernel, places, lengths.shape[0]),...  2.06 us
    pallas_call x1, Pallas kernels, prepare(): pl.pallas_call(prepare_kernel, out_shape=[jax.ShapeDtypeStruct((rows, 2 *...  1.13 us
  transfers between devices with their start and end apart: 10, of which 3 were waited for; matrix products, arithmetic and copies ran while one was open for 0% of the time, Pallas kernels for 25%

profile of v7, /device:TPU:19, one launch (start us, length us, event | category | flops | bytes accessed | tf_op | source)
XLA Modules:
  0.0 47.3 jit_solution(14317030070534019201)
XLA Ops:
  0.0 1.1 %prepare.1 = (bf16[128,1024]{1,0:T(8,128)(2,1)S(1)}, f32[128,128]{1,0:T(8,128)S(1)}, f32[128,128]{1,0:T(8,128)S(1)}) custom-call(f32[1,128]{1,0:T(1,128)S(1)} %fusion.2.freq_ref, s32[8]{0:T(128)} %lengths_hbm.3, bf16[128,512]{1,0:T(8,128)(2,1)} %k_hbm.1, bf16[128,512]{1,0:T(8,128)(2,1)} %v_hbm.1), custom_call_target="tpu_custom_call" | custom-call | flops 1000000 | bytes 600000 | tf_op jit(solution)/shard_map/prepare/pallas_call | solution.py:140
  1.1 1.3 %collective-permute-start = (bf16[128,1024]{1,0:T(8,128)(2,1)S(1)}, bf16[128,1024]{1,0:T(8,128)(2,1)S(1)}, u32[]{:S(2)}, u32[]{:S(2)}) collective-permute-start(bf16[128,1024]{1,0:T(8,128)(2,1)S(1)} %get-tuple-element.39.refs_2_), channel_id=1, source_target_pairs={{0,8},{2,10},{4,12},{6,14},{8,16},{10,18},{12,20},{14,22},{16,24},... | collective-permute-start | bytes 786440 | tf_op jit(solution)/shard_map/ppermute | solution.py:31
  2.5 5.9 %collective-permute-done.a_ref.refs_2_ = bf16[128,1024]{1,0:T(8,128)(2,1)S(1)} collective-permute-done((bf16[128,1024]{1,0:T(8,128)(2,1)S(1)}, bf16[128,1024]{1,0:T(8,128)(2,1)S(1)}, u32[]{:S(2)}, u32[]{:S(2)}) %collective-permute-start) | collective-permute-done | bytes 262176 | tf_op jit(solution)/shard_map/ppermute | solution.py:31
  8.4 1.3 %collective-permute-start.1 = (bf16[128,1024]{1,0:T(8,128)(2,1)S(1)}, bf16[128,1024]{1,0:T(8,128)(2,1)S(1)}, u32[]{:S(2)}, u32[]{:S(2)}) collective-permute-start(bf16[128,1024]{1,0:T(8,128)(2,1)S(1)} %collective-permute-done.a_ref.refs_2_), channel_id=1, source_target_pairs={{0,2},{2,0},{4,6},{6,4},{8,16},{10,18},{12,20},{14,22},{16,24},{18... | collective-permute-start | bytes 786440 | tf_op jit(solution)/shard_map/ppermute | solution.py:31
  9.7 1.2 %collective-permute-start.3 = (bf16[128,1024]{1,0:T(8,128)(2,1)S(1)}, bf16[128,1024]{1,0:T(8,128)(2,1)S(1)}, u32[]{:S(2)}, u32[]{:S(2)}) collective-permute-start(bf16[128,1024]{1,0:T(8,128)(2,1)S(1)} %collective-permute-done.a_ref.refs_2_), channel_id=1, source_target_pairs={{0,4},{2,6},{4,0},{6,2},{8,12},{10,14},{12,8},{14,10},{16,20},{18,... | collective-permute-start | bytes 786440 | tf_op jit(solution)/shard_map/ppermute | solution.py:31
  10.9 0.2 collective-permute-start.7
  11.2 3.6 %collective-permute-done.1.a_ref.refs_2_ = bf16[128,1024]{1,0:T(8,128)(2,1)S(1)} collective-permute-done((bf16[128,1024]{1,0:T(8,128)(2,1)S(1)}, bf16[128,1024]{1,0:T(8,128)(2,1)S(1)}, u32[]{:S(2)}, u32[]{:S(2)}) %collective-permute-start.1) | collective-permute-done | bytes 262176 | tf_op jit(solution)/shard_map/ppermute | solution.py:31
  14.7 1.2 %collective-permute-start.2 = (bf16[128,1024]{1,0:T(8,128)(2,1)S(1)}, bf16[128,1024]{1,0:T(8,128)(2,1)S(1)}, u32[]{:S(2)}, u32[]{:S(2)}) collective-permute-start(bf16[128,1024]{1,0:T(8,128)(2,1)S(1)} %collective-permute-done.1.a_ref.refs_2_), channel_id=1, source_target_pairs={{0,2},{2,0},{4,6},{6,4},{8,10},{10,8},{12,14},{14,12},{16,20},{18,... | collective-permute-start | bytes 786440 | tf_op jit(solution)/shard_map/ppermute | solution.py:31
  16.0 0.0 collective-permute-done.3.b_ref.refs_3_
  16.0 1.3 %collective-permute-start.4 = (bf16[128,1024]{1,0:T(8,128)(2,1)S(1)}, bf16[128,1024]{1,0:T(8,128)(2,1)S(1)}, u32[]{:S(2)}, u32[]{:S(2)}) collective-permute-start(bf16[128,1024]{1,0:T(8,128)(2,1)S(1)} %collective-permute-done.3.b_ref.refs_3_), channel_id=1, source_target_pairs={{0,2},{2,0},{4,6},{6,4},{8,16},{10,18},{12,14},{14,12},{16,24},{18... | collective-permute-start | bytes 786440 | tf_op jit(solution)/shard_map/ppermute | solution.py:31
  17.3 9.7 %collective-permute-done.7.b_ref.refs_3_ = bf16[128,1024]{1,0:T(8,128)(2,1)S(1)} collective-permute-done((bf16[128,1024]{1,0:T(8,128)(2,1)S(1)}, bf16[128,1024]{1,0:T(8,128)(2,1)S(1)}, u32[]{:S(2)}, u32[]{:S(2)}) %collective-permute-start.7) | collective-permute-done | bytes 262176 | tf_op jit(solution)/shard_map/ppermute | solution.py:31
  27.0 2.7 %collective-permute-start.8 = (bf16[256,1024]{1,0:T(8,128)(2,1)S(1)}, bf16[256,1024]{1,0:T(8,128)(2,1)S(1)}, u32[]{:S(2)}, u32[]{:S(2)}) collective-permute-start(bf16[256,1024]{1,0:T(8,128)(2,1)S(1)} %join.5), channel_id=1, source_target_pairs={{0,2},{2,0},{4,6},{6,4},{8,10},{10,8},{12,14},{14,12},{16,18},{18,... | collective-permute-start | bytes 1572872 | tf_op jit(solution)/shard_map/ppermute | solution.py:31
  29.8 0.1 collective-permute-start.6
  29.9 0.5 %collective-permute-start.9 = (bf16[128,1024]{1,0:T(8,128)(2,1)S(1)}, bf16[128,1024]{1,0:T(8,128)(2,1)S(1)}, u32[]{:S(2)}, u32[]{:S(2)}) collective-permute-start(bf16[128,1024]{1,0:T(8,128)(2,1)S(1)} %get-tuple-element.39.refs_2_), channel_id=1, source_target_pairs={{0,2},{2,0},{4,6},{6,4},{8,10},{10,8},{12,14},{14,12},{16,18},{18,... | collective-permute-start | bytes 786440 | tf_op jit(solution)/shard_map/ppermute | solution.py:31
  30.4 0.0 collective-permute-done.2.a_ref.refs_2_
  30.4 0.0 collective-permute-done.4.b_ref.refs_3_
  30.4 2.4 %collective-permute-start.5 = (bf16[256,1024]{1,0:T(8,128)(2,1)S(1)}, bf16[256,1024]{1,0:T(8,128)(2,1)S(1)}, u32[]{:S(2)}, u32[]{:S(2)}) collective-permute-start(bf16[256,1024]{1,0:T(8,128)(2,1)S(1)} %join.3), channel_id=1, source_target_pairs={{0,2},{2,0},{4,6},{6,4},{8,10},{10,8},{12,14},{14,12},{16,18},{18,... | collective-permute-start | bytes 1572872 | tf_op jit(solution)/shard_map/ppermute | solution.py:31
  32.8 2.1 %turn_queries.1 = (bf16[4,896,256]{2,1,0:T(8,128)(2,1)S(1)}, bf16[256,128]{1,0:T(8,128)(2,1)S(1)}, bf16[256,128]{1,0:T(8,128)(2,1)S(1)}, bf16[256,128]{1,0:T(8,1...) custom-call(s32[8]{0:T(128)} %lengths_hbm.3, ...), custom_call_target="tpu_custom_call" | custom-call | flops 100000000 | bytes 4000000 | tf_op jit(solution)/shard_map/turn_queries/pallas_call | solution.py:214
  34.8 0.0 collective-permute-done.9.refs_3_
  34.8 1.2 %shard_map.46 = (f32[4,896,128]{2,1,0:T(8,128)S(1)}, f32[4,896,128]{2,1,0:T(8,128)S(1)}, f32[4,896,128]{2,1,0:T(8,128)S(1)}) custom-call(bf16[4,896,256]{2,1,0:T(8,128)(2,1)S(1)} %get-tuple-element.37.refs_0_, bf16[256,128]{1,0:T(8,128)(2,1)S(1)} %get-tuple-element.45.refs_1_, bf16[128,1024]{1,0:T(8,128)(2,1)S(1)} %get-tuple-element.39.refs_2_, ...), custom_call_target="tpu_custom_call" | custom-call | flops 469762048 | bytes 4000000 | tf_op jit(solution)/shard_map/pallas_call | solution.py:386
  36.1 1.7 %shard_map.47 = (f32[4,896,128]{2,1,0:T(8,128)S(1)}, f32[4,896,128]{2,1,0:T(8,128)S(1)}, f32[4,896,128]{2,1,0:T(8,128)S(1)}) custom-call(bf16[4,896,256]{2,1,0:T(8,128)(2,1)S(1)} %get-tuple-element.37.refs_0_, bf16[256,128]{1,0:T(8,128)(2,1)S(1)} %get-tuple-element.44.refs_1_, bf16[128,1024]{1,0:T(8,128)(2,1)S(1)} %collective-permute-done.a_ref.refs_2_, ...), custom_call_target="tpu_custom_call" | custom-call | flops 469762048 | bytes 4000000 | tf_op jit(solution)/shard_map/pallas_call | solution.py:386
  37.7 0.0 collective-permute-done.8.refs_2_
  37.8 1.7 %shard_map.48 = (f32[4,896,128]{2,1,0:T(8,128)S(1)}, f32[4,896,128]{2,1,0:T(8,128)S(1)}, f32[4,896,128]{2,1,0:T(8,128)S(1)}) custom-call(bf16[4,896,256]{2,1,0:T(8,128)(2,1)S(1)} %get-tuple-element.37.refs_0_, bf16[256,128]{1,0:T(8,128)(2,1)S(1)} %get-tuple-element.43.refs_1_, bf16[256,1024]{1,0:T(8,128)(2,1)S(1)} %collective-permute-done.8.refs_2_, ...), custom_call_target="tpu_custom_call" | custom-call | flops 469762048 | bytes 4000000 | tf_op jit(solution)/shard_map/pallas_call | solution.py:386
  39.4 1.7 %shard_map.49 = (f32[4,896,128]{2,1,0:T(8,128)S(1)}, f32[4,896,128]{2,1,0:T(8,128)S(1)}, f32[4,896,128]{2,1,0:T(8,128)S(1)}) custom-call(bf16[4,896,256]{2,1,0:T(8,128)(2,1)S(1)} %get-tuple-element.37.refs_0_, bf16[256,128]{1,0:T(8,128)(2,1)S(1)} %get-tuple-element.42.refs_1_, bf16[128,1024]{1,0:T(8,128)(2,1)S(1)} %collective-permute-done.1.a_ref.refs_2_, ...), custom_call_target="tpu_custom_call" | custom-call | flops 469762048 | bytes 4000000 | tf_op jit(solution)/shard_map/pallas_call | solution.py:386
  41.1 0.0 collective-permute-done.6.refs_2_
  41.1 1.7 %shard_map.50 = (f32[4,896,128]{2,1,0:T(8,128)S(1)}, f32[4,896,128]{2,1,0:T(8,128)S(1)}, f32[4,896,128]{2,1,0:T(8,128)S(1)}) custom-call(bf16[4,896,256]{2,1,0:T(8,128)(2,1)S(1)} %get-tuple-element.37.refs_0_, bf16[256,128]{1,0:T(8,128)(2,1)S(1)} %get-tuple-element.41.refs_1_, bf16[256,1024]{1,0:T(8,128)(2,1)S(1)} %collective-permute-done.6.refs_2_, ...), custom_call_target="tpu_custom_call" | custom-call | flops 469762048 | bytes 4000000 | tf_op jit(solution)/shard_map/pallas_call | solution.py:386
  42.8 1.9 %shard_map.51 = (f32[4,896,128]{2,1,0:T(8,128)S(1)}, f32[4,896,128]{2,1,0:T(8,128)S(1)}, f32[4,896,128]{2,1,0:T(8,128)S(1)}, bf16[128,3584]{1,0:T(8,128)(2,1)}) custom-call(bf16[4,896,256]{2,1,0:T(8,128)(2,1)S(1)} %get-tuple-element.37.refs_0_, bf16[256,128]{1,0:T(8,128)(2,1)S(1)} %get-tuple-element.40.refs_1_, ...), custom_call_target="tpu_custom_call" | custom-call | flops 469762048 | bytes 4000000 | tf_op jit(solution)/shard_map/pallas_call | solution.py:386
  44.6 0.0 collective-permute-done.5.refs_2_
  44.6 2.5 %shard_map.52 = bf16[128,3584]{1,0:T(8,128)(2,1)} custom-call(bf16[4,896,256]{2,1,0:T(8,128)(2,1)S(1)} %get-tuple-element.37.refs_0_, bf16[256,128]{1,0:T(8,128)(2,1)S(1)} %get-tuple-element.38.refs_1_, bf16[256,1024]{1,0:T(8,128)(2,1)S(1)} %collective-permute-done.5.refs_2_, ...), custom_call_target="tpu_custom_call", output_to_operand_aliasing={{}: (6, {})} | custom-call | flops 469762048 | bytes 4000000 | tf_op jit(solution)/shard_map/pallas_call | solution.py:386
  (4 shorter events, 0.1 us)
Async XLA Ops:
  1.1 7.2 %collective-permute-start = (bf16[128,1024]{1,0:T(8,128)(2,1)S(1)}, bf16[128,1024]{1,0:T(8,128)(2,1)S(1)}, u32[]{:S(2)}, u32[]{:S(2)}) collective-permute-start(bf16[128,1024]{1,0:T(8,128)(2,1)S(1)} %get-tuple-element.39.refs_2_), channel_id=1, source_target_pairs={{0,8},{2,10},{4,12},{6,14},{8,16},{10,18},{12,20},{14,22},{16,24},... | collective-permute-start | bytes 786440 | tf_op jit(solution)/shard_map/ppermute | solution.py:31
  8.4 6.3 %collective-permute-start.1 = (bf16[128,1024]{1,0:T(8,128)(2,1)S(1)}, bf16[128,1024]{1,0:T(8,128)(2,1)S(1)}, u32[]{:S(2)}, u32[]{:S(2)}) collective-permute-start(bf16[128,1024]{1,0:T(8,128)(2,1)S(1)} %collective-permute-done.a_ref.refs_2_), channel_id=1, source_target_pairs={{0,2},{2,0},{4,6},{6,4},{8,16},{10,18},{12,20},{14,22},{16,24},{18... | collective-permute-start | bytes 786440 | tf_op jit(solution)/shard_map/ppermute | solution.py:31
  9.7 6.3 %collective-permute-start.3 = (bf16[128,1024]{1,0:T(8,128)(2,1)S(1)}, bf16[128,1024]{1,0:T(8,128)(2,1)S(1)}, u32[]{:S(2)}, u32[]{:S(2)}) collective-permute-start(bf16[128,1024]{1,0:T(8,128)(2,1)S(1)} %collective-permute-done.a_ref.refs_2_), channel_id=1, source_target_pairs={{0,4},{2,6},{4,0},{6,2},{8,12},{10,14},{12,8},{14,10},{16,20},{18,... | collective-permute-start | bytes 786440 | tf_op jit(solution)/shard_map/ppermute | solution.py:31
  10.9 16.1 %collective-permute-start.7 = (bf16[128,1024]{1,0:T(8,128)(2,1)S(1)}, bf16[128,1024]{1,0:T(8,128)(2,1)S(1)}, u32[]{:S(2)}, u32[]{:S(2)}) collective-permute-start(bf16[128,1024]{1,0:T(8,128)(2,1)S(1)} %get-tuple-element.39.refs_2_), channel_id=1, source_target_pairs={{0,4},{2,6},{4,0},{6,2},{8,12},{10,14},{12,8},{14,10},{16,20},{18,... | collective-permute-start | bytes 786440 | tf_op jit(solution)/shard_map/ppermute | solution.py:31
  14.7 15.6 %collective-permute-start.2 = (bf16[128,1024]{1,0:T(8,128)(2,1)S(1)}, bf16[128,1024]{1,0:T(8,128)(2,1)S(1)}, u32[]{:S(2)}, u32[]{:S(2)}) collective-permute-start(bf16[128,1024]{1,0:T(8,128)(2,1)S(1)} %collective-permute-done.1.a_ref.refs_2_), channel_id=1, source_target_pairs={{0,2},{2,0},{4,6},{6,4},{8,10},{10,8},{12,14},{14,12},{16,20},{18,... | collective-permute-start | bytes 786440 | tf_op jit(solution)/shard_map/ppermute | solution.py:31
  16.0 14.4 %collective-permute-start.4 = (bf16[128,1024]{1,0:T(8,128)(2,1)S(1)}, bf16[128,1024]{1,0:T(8,128)(2,1)S(1)}, u32[]{:S(2)}, u32[]{:S(2)}) collective-permute-start(bf16[128,1024]{1,0:T(8,128)(2,1)S(1)} %collective-permute-done.3.b_ref.refs_3_), channel_id=1, source_target_pairs={{0,2},{2,0},{4,6},{6,4},{8,16},{10,18},{12,14},{14,12},{16,24},{18... | collective-permute-start | bytes 786440 | tf_op jit(solution)/shard_map/ppermute | solution.py:31
  27.0 10.7 %collective-permute-start.8 = (bf16[256,1024]{1,0:T(8,128)(2,1)S(1)}, bf16[256,1024]{1,0:T(8,128)(2,1)S(1)}, u32[]{:S(2)}, u32[]{:S(2)}) collective-permute-start(bf16[256,1024]{1,0:T(8,128)(2,1)S(1)} %join.5), channel_id=1, source_target_pairs={{0,2},{2,0},{4,6},{6,4},{8,10},{10,8},{12,14},{14,12},{16,18},{18,... | collective-permute-start | bytes 1572872 | tf_op jit(solution)/shard_map/ppermute | solution.py:31
  29.8 11.3 %collective-permute-start.6 = (bf16[256,1024]{1,0:T(8,128)(2,1)S(1)}, bf16[256,1024]{1,0:T(8,128)(2,1)S(1)}, u32[]{:S(2)}, u32[]{:S(2)}) collective-permute-start(bf16[256,1024]{1,0:T(8,128)(2,1)S(1)} %join.4), channel_id=1, source_target_pairs={{0,2},{2,0},{4,6},{6,4},{8,10},{10,8},{12,14},{14,12},{16,18},{18,... | collective-permute-start | bytes 1572872 | tf_op jit(solution)/shard_map/ppermute | solution.py:31
  29.9 5.0 %collective-permute-start.9 = (bf16[128,1024]{1,0:T(8,128)(2,1)S(1)}, bf16[128,1024]{1,0:T(8,128)(2,1)S(1)}, u32[]{:S(2)}, u32[]{:S(2)}) collective-permute-start(bf16[128,1024]{1,0:T(8,128)(2,1)S(1)} %get-tuple-element.39.refs_2_), channel_id=1, source_target_pairs={{0,2},{2,0},{4,6},{6,4},{8,10},{10,8},{12,14},{14,12},{16,18},{18,... | collective-permute-start | bytes 786440 | tf_op jit(solution)/shard_map/ppermute | solution.py:31
  30.4 14.2 %collective-permute-start.5 = (bf16[256,1024]{1,0:T(8,128)(2,1)S(1)}, bf16[256,1024]{1,0:T(8,128)(2,1)S(1)}, u32[]{:S(2)}, u32[]{:S(2)}) collective-permute-start(bf16[256,1024]{1,0:T(8,128)(2,1)S(1)} %join.3), channel_id=1, source_target_pairs={{0,2},{2,0},{4,6},{6,4},{8,10},{10,8},{12,14},{14,12},{16,18},{18,... | collective-permute-start | bytes 1572872 | tf_op jit(solution)/shard_map/ppermute | solution.py:31
